TPU v7x, 32 devices: a whole 2x2x4 slice. The times are simulated.
32 devices in a mesh: node: 8 (over z, y), local: 4 (over x, core).
Axes of the slice: x: 2, y: 2, z: 4, core: 2. Of those that a mesh axis runs over, the one named last changes fastest.
Arguments:
- tokens: bfloat16 [4096, 2048], P(('node', 'local')), may hold values from -6 to 6
- norm_gain: float32 [2048], replicated, may hold values from 0.1 to 1.9
- router_weight: bfloat16 [2048, 16], replicated, may hold values from -0.125 to 0.125
- placement: int32 [16], replicated, may hold values from 0 to 15, each once
- expert_ids: int32 [4096, 6], P(('node', 'local')), may hold values from 0 to 15, all different within a row; in each aligned block of 128 rows (0 to 127, 128 to 255, ...) at most 72 rows name the same one
- w_gate: bfloat16 [2048, 22528], P(None, ('node', 'local')), may hold values from -0.125 to 0.125
- w_up: bfloat16 [2048, 22528], P(None, ('node', 'local')), may hold values from -0.125 to 0.125
- w_down: bfloat16 [22528, 2048], P(('node', 'local')), may hold values from -0.15625 to 0.15625
- shared_gate: bfloat16 [2048, 2816], P(None, 'local'), may hold values from -0.125 to 0.125
- shared_up: bfloat16 [2048, 2816], P(None, 'local'), may hold values from -0.125 to 0.125
- shared_down: bfloat16 [2816, 2048], P('local'), may hold values from -0.109375 to 0.109375
Outputs:
- moe_out: bfloat16 [4096, 2048], P(('node', 'local'))
Inputs may be any that keep to these rules, and one draw needn't show every extreme that they name: Expert e's weights stand in slot placement[e]; every slot holds one expert. `expert_ids`: each row names 6 different experts. Among the rows of one device (aligned blocks of 128 rows) no expert is named more than 72 times, a bound that some block reaches.
All inputs are finite; a program needn't handle non-finite values.
Results may differ from a plain program's by a relative error of at most 0.011.
Values may be sent and summed in bfloat16 or wider, within the bound.
No kernel may reach another device: no remote copies, remote signals or barrier semaphores. Data moves between devices by JAX's collectives and lax.ppermute only.
A program may use at most 128 MiB of HBM per device.

v0:
```python
import math

import jax
import jax.numpy as jnp
import numpy as np
from jax import lax
from jax.experimental import pallas as pl
from jax.experimental.pallas import tpu as pltpu
from jax.sharding import PartitionSpec as P


AXES = ("node", "local")
F32 = jnp.float32
BF16 = jnp.bfloat16
STRIP = 8
UNUSED = -4096.0
PIECE = 256
LIMIT = 16 << 20


def places(dims):
    return [dict(zip(dims, p)) for p in np.ndindex(*dims.values())]


def index_of(dims, place):
    index = 0
    for name, size in dims.items():
        index = index * size + place[name] % size
    return index


def moved(dims, place, axes, step):
    axis = axes[place["c"] % len(axes)]
    return index_of(dims, {**place, axis: place[axis] + step})


def shift(block, dims, axes, step):
    route = [(i, moved(dims, p, axes, step)) for i, p in enumerate(places(dims))]
    return lax.ppermute(block, AXES, route)


def targets(dims, axes):
    size = dims[axes[0]]
    table = [[moved(dims, p, axes, d) // dims["c"] for d in range(size)] for p in places(dims)]
    return lax.dynamic_index_in_dim(
        jnp.asarray(np.array(table, np.int32)), lax.axis_index(AXES), 0, keepdims=False
    )


def routing_rows(normed, router_weight, placement, expert_ids):
    slots = placement.shape[0]
    tok_rows = normed.shape[0]
    slot_iota = jnp.arange(slots, dtype=jnp.int32)
    to_slot = (placement[:, None] == slot_iota).astype(BF16)
    slot_router = jnp.dot(router_weight, to_slot, preferred_element_type=F32).astype(BF16)
    logits = lax.dot_general(slot_router, normed, (((0,), (1,)), ((), ())), preferred_element_type=F32)
    named = expert_ids[:, :, None] == slot_iota
    token_slots = jnp.sum(jnp.where(named, placement, 0), -1)
    hot = jnp.any(token_slots.T[:, None, :] == slot_iota[:, None], 0)
    picked = jnp.where(hot, jax.nn.sigmoid(logits), 0.0)
    gates = picked / jnp.sum(picked, 0, keepdims=True)
    upper = jnp.arange(tok_rows)[:, None] <= jnp.arange(tok_rows)
    running = jnp.dot(hot.astype(BF16), upper.astype(BF16), preferred_element_type=F32)
    return jnp.concatenate([gates, jnp.where(hot, running, UNUSED)], 0).astype(BF16)


def pack(rows, width):
    count, lanes = rows.shape
    strips = -(-count // STRIP)
    rows = jnp.pad(rows, ((0, strips * STRIP - count), (0, 0)))
    parts = [rows[i * STRIP : (i + 1) * STRIP] for i in range(strips)]
    packed = jnp.concatenate(parts, 1)
    return jnp.pad(packed, ((0, 0), (0, width - strips * lanes)))


def table_row(block, tok_rows, row):
    start = pl.multiple_of(row // STRIP * tok_rows, tok_rows)
    group = block[tok_rows : tok_rows + STRIP, pl.ds(start, tok_rows)].astype(F32)
    lines = lax.broadcasted_iota(jnp.int32, group.shape, 0)
    return jnp.sum(jnp.where(lines == row % STRIP, group, 0.0), 0, keepdims=True)


def choice(blocks, tok_rows, slots, slot, list_rows, capacity, gated):
    lines = lax.broadcasted_iota(jnp.int32, (list_rows, tok_rows), 0).astype(F32)
    columns = []
    for i, block in enumerate(blocks):
        place = table_row(block, tok_rows, slots + slot)
        value = table_row(block, tok_rows, slot) if gated else 1.0
        columns.append(jnp.where(lines + float(1 - i * capacity) == place, value, 0.0))
    return jnp.concatenate(columns, 1).astype(BF16)


def stacked(blocks, tok_rows):
    return jnp.concatenate([b[:tok_rows] for b in blocks], 0)


def vmem():
    return pl.BlockSpec(memory_space=pltpu.VMEM)


def kept(arrays, space=pltpu.VMEM):
    return [pltpu.with_memory_space_constraint(a, space) for a in arrays]


def load(arrays, after):
    def kernel(*refs):
        sources, outs, sems = refs[: len(arrays)], refs[-len(arrays) - 1 : -1], refs[-1]
        copies = [pltpu.make_async_copy(s, o, sems.at[i]) for i, (s, o) in enumerate(zip(sources, outs))]
        for copy in copies:
            copy.start()
        for copy in copies:
            copy.wait()

    call = pl.pallas_call(
        kernel,
        out_shape=[pltpu.VMEM(a.shape, a.dtype) for a in arrays],
        in_specs=[anywhere()] * (len(arrays) + len(after)),
        out_specs=[vmem()] * len(arrays),
        scratch_shapes=[pltpu.SemaphoreType.DMA((len(arrays),))],
        compiler_params=pltpu.CompilerParams(vmem_limit_bytes=LIMIT),
        cost_estimate=pl.CostEstimate(flops=1 << 32, bytes_accessed=0, transcendentals=0),
        name="load",
    )
    return list(call(*kept(arrays, pltpu.HBM), *after))


def anywhere():
    return pl.BlockSpec(memory_space=pl.ANY)


def send_rows(blocks, chosen, shape, after):
    slots, tok_rows, capacity, list_rows = shape
    width = blocks[0].shape[1]
    outs = chosen.shape[0] - 1

    def kernel(slot_ref, *refs):
        block_refs = refs[: len(blocks)]
        out_refs = refs[len(refs) - outs :]
        tokens = stacked(block_refs, tok_rows)
        for d, out in enumerate(out_refs):
            hot = choice(block_refs, tok_rows, slots, slot_ref[d + 1], list_rows, capacity, False)
            out[...] = jnp.dot(hot, tokens, preferred_element_type=F32).astype(BF16)

    flops = 2 * outs * list_rows * len(blocks) * tok_rows * width
    call = pl.pallas_call(
        kernel,
        out_shape=[pltpu.VMEM((list_rows, width), BF16)] * outs,
        in_specs=[pl.BlockSpec(memory_space=pltpu.SMEM)]
        + [vmem()] * len(blocks)
        + [anywhere()] * len(after),
        out_specs=[vmem()] * outs,
        cost_estimate=pl.CostEstimate(flops=4 * flops, bytes_accessed=0, transcendentals=0),
        compiler_params=pltpu.CompilerParams(vmem_limit_bytes=LIMIT),
        name="send_rows",
    )
    return list(call(chosen, *kept(blocks), *after))


def feed_forward(blocks, came, slices, chosen, shape, after):
    slots, tok_rows, capacity, list_rows = shape
    width = blocks[0].shape[1]
    routed = chosen is not None
    group = list_rows if routed else len(blocks) * tok_rows
    groups = 1 + (len(came) if routed else len(came) // len(blocks))
    count = group * groups
    hidden = slices[0][0].shape[0]
    pieces = [(lo, min(PIECE, hidden - lo)) for lo in range(0, hidden, PIECE)]

    def kernel(*refs):
        refs = list(refs)
        slot_ref = refs.pop(0) if routed else None
        block_refs = [refs.pop(0) for _ in blocks]
        came_refs = [refs.pop(0) for _ in came]
        weights = [[refs.pop(0) for _ in range(3)] for _ in slices]
        for _ in after:
            refs.pop(0)
        out_refs = [refs.pop(0) for _ in range(groups)]
        rows, active, total, *streamed = refs
        if not routed:
            *stores, sems = streamed

            def copy(i, n, j, part):
                source, store = weights[i][n].at[part], stores[n].at[i, part]
                return pltpu.make_async_copy(source, store, sems.at[i, n, j])

            parts = [pl.ds(lo, size) for lo, size in pieces]
            for i in range(len(slices)):
                for j, part in enumerate(parts):
                    copy(i, 0, j, part).start()
                    copy(i, 1, j, part).start()
                copy(i, 2, 0, pl.ds(0, hidden)).start()

        tokens = stacked(block_refs, tok_rows)
        if routed:
            hot = choice(block_refs, tok_rows, slots, slot_ref[0], list_rows, capacity, False)
            rows[:group] = jnp.dot(hot, tokens, preferred_element_type=F32).astype(BF16)
        else:
            rows[:group] = tokens
        if routed:
            for d, ref in enumerate(came_refs):
                rows[(d + 1) * group : (d + 2) * group] = ref[...]
        else:
            for d, ref in enumerate(came_refs):
                start = group + d * tok_rows
                rows[start : start + tok_rows] = ref[:tok_rows]
        across = (((1,), (1,)), ((), ()))
        for i, (gate_ref, up_ref, down_ref) in enumerate(weights):
            values = rows[...]
            if not routed:
                gate_ref, up_ref, down_ref = [store.at[i] for store in stores]
            for j, (lo, size) in enumerate(pieces):
                span = slice(lo, lo + size)
                if not routed:
                    copy(i, 0, j, parts[j]).wait()
                    copy(i, 1, j, parts[j]).wait()
                gate = lax.dot_general(values, gate_ref[span], across, preferred_element_type=F32)
                up = lax.dot_general(values, up_ref[span], across, preferred_element_type=F32)
                active[:, span] = (gate / (1.0 + jnp.exp(-gate)) * up).astype(BF16)
            if not routed:
                copy(i, 2, 0, pl.ds(0, hidden)).wait()
            part = jnp.dot(active[...], down_ref[...], preferred_element_type=F32)
            if i:
                part = total[...] + part
            if i + 1 < len(weights):
                total[...] = part
                continue
            for d, out in enumerate(out_refs):
                out[...] = part[d * group : (d + 1) * group].astype(out.dtype)

    flops = 6 * count * width * hidden * len(slices)
    operands = [chosen] if routed else []
    stream = []
    if not routed:
        stream = [pltpu.VMEM((len(slices), hidden, width), BF16)] * 3
        stream += [pltpu.SemaphoreType.DMA((len(slices), 3, len(pieces)))]
    call = pl.pallas_call(
        kernel,
        out_shape=[
            pltpu.VMEM((group, width), BF16 if routed or d else F32) for d in range(groups)
        ],
        in_specs=[pl.BlockSpec(memory_space=pltpu.SMEM)] * len(operands)
        + [vmem()] * (len(blocks) + len(came))
        + [vmem() if routed else anywhere()] * (3 * len(slices))
        + [anywhere()] * len(after),
        out_specs=[vmem()] * groups,
        scratch_shapes=[
            pltpu.VMEM((count, width), BF16),
            pltpu.VMEM((count, hidden), BF16),
            pltpu.VMEM((count, width), F32),
        ]
        + stream,
        compiler_params=pltpu.CompilerParams(vmem_limit_bytes=LIMIT if routed else 2 * LIMIT),
        cost_estimate=pl.CostEstimate(flops=flops, bytes_accessed=0, transcendentals=0),
        name="experts" if routed else "shared",
    )
    weights = [w for s in slices for w in s]
    weights = kept(weights, pltpu.VMEM if routed else pltpu.HBM)
    return list(call(*operands, *kept(blocks), *kept(came), *weights, *after))


def combine(blocks, back, chosen, extra, shape, after):
    slots, tok_rows, capacity, list_rows = shape
    width = blocks[0].shape[1]

    def kernel(slot_ref, *refs):
        refs = list(refs)
        block_refs = [refs.pop(0) for _ in blocks]
        back_refs = [refs.pop(0) for _ in back]
        extra_refs = [refs.pop(0) for _ in extra]
        for _ in after:
            refs.pop(0)
        out_refs = refs
        weights = [
            choice(block_refs, tok_rows, slots, slot_ref[d], list_rows, capacity, True)
            for d in range(len(back))
        ]
        for i, out in enumerate(out_refs):
            span = slice(i * tok_rows, (i + 1) * tok_rows)
            sums = None
            for w, ref in zip(weights, back_refs):
                part = lax.dot_general(
                    w[:, span], ref[...], (((0,), (0,)), ((), ())), preferred_element_type=F32
                )
                sums = part if sums is None else sums + part
            for ref in extra_refs:
                sums = sums + ref[span]
            out[...] = sums.astype(out.dtype)

    flops = 2 * len(back) * list_rows * len(blocks) * tok_rows * width
    call = pl.pallas_call(
        kernel,
        out_shape=[
            pltpu.VMEM((tok_rows, width), BF16 if i else F32) for i in range(len(blocks))
        ],
        in_specs=[pl.BlockSpec(memory_space=pltpu.SMEM)]
        + [vmem()] * (len(blocks) + len(back) + len(extra))
        + [anywhere()] * len(after),
        out_specs=[vmem()] * len(blocks),
        cost_estimate=pl.CostEstimate(flops=4 * flops, bytes_accessed=0, transcendentals=0),
        compiler_params=pltpu.CompilerParams(vmem_limit_bytes=LIMIT),
        name="combine",
    )
    return list(call(chosen, *kept(blocks), *kept(back), *kept(extra), *after))


def body(
    tokens,
    norm_gain,
    router_weight,
    placement,
    expert_ids,
    w_gate,
    w_up,
    w_down,
    shared_gate,
    shared_up,
    shared_down,
):
    slots = placement.shape[0]
    tok_rows, width = tokens.shape
    capacity = 3 * tok_rows * expert_ids.shape[1] // (2 * slots)
    node_count = lax.axis_size("node")
    local_count = lax.axis_size("local")
    cores = node_count * local_count // slots
    x_count = local_count // cores
    y_count = math.gcd(node_count, x_count)
    dims = {"z": node_count // y_count, "y": y_count, "x": x_count, "c": cores}
    list_rows = -(-x_count * capacity // 16) * 16
    shape = (slots, tok_rows, capacity, list_rows)
    steps = dims["z"]
    mixed = ("xy", "yx") if x_count == y_count else ("xy", "xy")
    orders = [("xy", "xy")] + [mixed] * (steps - 1)

    def slices_of(*weights):
        return [list(weights)] + [
            [shift(w, dims, "c", step) for w in weights] for step in range(1, cores)
        ]

    expert_slices = slices_of(w_gate.T, w_up.T, w_down)

    floats = tokens.astype(F32)
    normed = (
        floats * lax.rsqrt(jnp.mean(floats * floats, -1, keepdims=True) + 1e-06) * norm_gain
    ).astype(BF16)
    routing = routing_rows(normed, router_weight, placement, expert_ids)
    own = [jnp.concatenate([normed, pack(routing, width)], 0)]
    for _ in range(1, steps):
        own.append(shift(own[-1], dims, "z", 1))

    last = own[:1]
    loaded = load([w for weights in expert_slices for w in weights], last)
    expert_slices = [loaded[i : i + 3] for i in range(0, len(loaded), 3)]
    last = loaded[-1:]
    blocks, chosen, came, results, parts = {}, {}, {}, {}, {}
    firsts = [[o[0] for o in order] for order in orders]
    seconds = [[o[1] for o in order] for order in orders]
    for step in range(steps):
        chosen[step] = targets(dims, seconds[step])
        blocks[step] = [own[step]] + [
            shift(own[step], dims, firsts[step], d) for d in range(1, dims[firsts[step][0]])
        ]

    def send(step):
        nonlocal last
        sent = send_rows(blocks[step], chosen[step], shape, last)
        last = sent[:1]
        came[step] = [shift(r, dims, seconds[step], d + 1) for d, r in enumerate(sent)]

    def run(step):
        nonlocal last
        results[step] = feed_forward(
            blocks[step], came[step], expert_slices, chosen[step], shape, last
        )
        last = results[step][:1]

    def give(step, held=None):
        own_rows, *rest = results[step]
        if held is not None:
            rest = lax.optimization_barrier((*rest, results[held][0]))[:-1]
        results[step] = [own_rows] + [
            shift(r, dims, seconds[step], -d - 1) for d, r in enumerate(rest)
        ]

    def join(step, extra=()):
        nonlocal last
        out = combine(blocks[step], results[step], chosen[step], extra, shape, last)
        last = out[:1]
        parts[step] = out[:1] + [
            shift(r, dims, firsts[step], -d - 1) for d, r in enumerate(out[1:])
        ]

    later = list(range(1, steps))
    send(0)
    peers = [shift(b, dims, "c", d) for d in range(1, cores) for b in blocks[0]]
    shared = feed_forward(
        blocks[0], peers, [[shared_gate.T, shared_up.T, shared_down]], None, shape, last
    )
    last = shared[:1]
    shared = shared[:1] + [shift(r, dims, "c", -d - 1) for d, r in enumerate(shared[1:])]
    for step in later[:1]:
        send(step)
    run(0)
    for n, step in enumerate(later):
        if n + 1 < len(later):
            send(later[n + 1])
        if n > 1:
            join(later[n - 2])
        run(step)
        give(step)
        if n == 0:
            give(0, step)
    for step in later[-2:-1]:
        join(step)
    if not later:
        give(0)
    join(0, shared)
    for step in later[-1:]:
        join(step)

    passed = []
    for step in later + [0]:
        total = parts[step][0]
        for part in parts[step][1:] + passed:
            total = total + part.astype(F32)
        total = total.astype(BF16)
        if step:
            passed = [shift(total, dims, "z", 1)]
    return total


def solution(mesh):
    in_specs = (
        P(AXES, None),
        P(),
        P(),
        P(),
        P(AXES, None),
        P(None, AXES),
        P(None, AXES),
        P(AXES, None),
        P(None, "local"),
        P(None, "local"),
        P("local", None),
    )
    out_specs = P(AXES, None)

    return jax.shard_map(body, mesh=mesh, in_specs=in_specs, out_specs=out_specs, check_vma=False)
```

profile of v0, /device:TPU:0, one launch (start us, length us, event | category | flops | bytes accessed | tf_op | source)
XLA Modules:
  0.0 170.6 jit_solution(12819930329562850521)
XLA Ops:
  3.2 1.2 fusion.9
  5.7 2.7 %collective-permute-start.5 = (bf16[136,2048]{1,0:T(8,128)(2,1)S(1)}, bf16[136,2048]{1,0:T(8,128)(2,1)S(1)}, u32[]{:S(2)}, u32[]{:S(2)}) collective-permute-start(bf16[136,2048]{1,0:T(8,128)(2,1)S(1)} %pad_maximum_fusion.refs_6_.refs_0_.refs_1_), channel_id=1, source_target_pairs={{0,8},{1,9},{2,10},{3,11},{4,12},{5,13},{6,14},{7,15},{8,16},{9,17... | collective-permute-start | bytes 1671176 | tf_op jit(solution)/shard_map/ppermute | solution.py:39
  8.4 1.5 collective-permute-start
  9.9 13.8 %collective-permute-done.5.refs_0_.refs_1_ = bf16[136,2048]{1,0:T(8,128)(2,1)S(1)} collective-permute-done((bf16[136,2048]{1,0:T(8,128)(2,1)S(1)}, bf16[136,2048]{1,0:T(8,128)(2,1)S(1)}, u32[]{:S(2)}, u32[]{:S(2)}) %collective-permute-start.5) | collective-permute-done | bytes 557088 | tf_op jit(solution)/shard_map/ppermute | solution.py:39
  24.3 15.5 %collective-permute-done.10.refs_0_.refs_1_ = bf16[136,2048]{1,0:T(8,128)(2,1)S(1)} collective-permute-done((bf16[136,2048]{1,0:T(8,128)(2,1)S(1)}, bf16[136,2048]{1,0:T(8,128)(2,1)S(1)}, u32[]{:S(2)}, u32[]{:S(2)}) %collective-permute-start.10) | collective-permute-done | bytes 557088 | tf_op jit(solution)/shard_map/ppermute | solution.py:39
  39.8 1.3 collective-permute-start.6
  41.2 6.1 %load.1 = (bf16[704,2048]{1,0:T(8,128)(2,1)S(1)}, bf16[704,2048]{1,0:T(8,128)(2,1)S(1)}, bf16[704,2048]{1,0:T(8,128)(2,1)S(1)}, bf16[704,2048]{1,0:T(8,128)(2,1)...) custom-call(bf16[704,2048]{1,0:T(8,128)(2,1)} %bitcast.13, bf16[704,2048]{1,0:T(8,128)(2,1)} %bitcast.15, ...), custom_call_target="tpu_custom_call" | custom-call | flops 4294967296 | tf_op jit(solution)/shard_map/load/pallas_call | solution.py:124
  48.1 1.6 collective-permute-start.4
  51.0 7.3 %shared.1 = (f32[256,2048]{1,0:T(8,128)S(1)}, bf16[256,2048]{1,0:T(8,128)(2,1)S(1)}) custom-call(bf16[136,2048]{1,0:T(8,128)(2,1)S(1)} %pad_maximum_fusion.refs_6_.refs_0_.refs_1_, bf16[136,2048]{1,0:T(8,128)(2,1)S(1)} %collective-permute-done.refs_1_.refs_2_, bf16[136,2048]{1,0:T(8,128)(2,1)S(1)} %collective-permute-done.7.refs_2_, ...), custom_call_target="tpu_custom_call" | custom-call | flops 4429185024 | tf_op jit(solution)/shard_map/shared/pallas_call | solution.py:258
  60.0 1.3 collective-permute-start.16
  61.2 3.2 %collective-permute-done.4.refs_3_ = bf16[144,2048]{1,0:T(8,128)(2,1)S(1)} collective-permute-done((bf16[144,2048]{1,0:T(8,128)(2,1)S(1)}, bf16[144,2048]{1,0:T(8,128)(2,1)S(1)}, u32[]{:S(2)}, u32[]{:S(2)}) %collective-permute-start.4) | collective-permute-done | bytes 589856 | tf_op jit(solution)/shard_map/ppermute | solution.py:39
  64.4 6.4 %experts.4 = (bf16[144,2048]{1,0:T(8,128)(2,1)S(1)}, bf16[144,2048]{1,0:T(8,128)(2,1)S(1)}) custom-call(s32[2]{0:T(128)S(1)} %dynamic-slice_bitcast_fusion.1.slot_ref.refs_0_, bf16[136,2048]{1,0:T(8,128)(2,1)S(1)} %pad_maximum_fusion.refs_6_.refs_0_.refs_1_, bf16[136,2048]{1,0:T(8,128)(2,1)S(1)} %collective-permute-done.refs_1_.refs_2_, ...), custom_call_target="tpu_custom_call" | custom-call | flops 4982833152 | tf_op jit(solution)/shard_map/experts/pallas_call | solution.py:258
  71.7 1.6 collective-permute-start.14
  73.3 3.7 %collective-permute-done.9.refs_3_ = bf16[144,2048]{1,0:T(8,128)(2,1)S(1)} collective-permute-done((bf16[144,2048]{1,0:T(8,128)(2,1)S(1)}, bf16[144,2048]{1,0:T(8,128)(2,1)S(1)}, u32[]{:S(2)}, u32[]{:S(2)}) %collective-permute-start.9) | collective-permute-done | bytes 589856 | tf_op jit(solution)/shard_map/ppermute | solution.py:39
  77.0 6.6 %experts.5 = (bf16[144,2048]{1,0:T(8,128)(2,1)S(1)}, bf16[144,2048]{1,0:T(8,128)(2,1)S(1)}) custom-call(s32[2]{0:T(128)S(1)} %dynamic-slice_bitcast_fusion.slot_ref.refs_0_, bf16[136,2048]{1,0:T(8,128)(2,1)S(1)} %collective-permute-done.5.refs_0_.refs_1_, bf16[136,2048]{1,0:T(8,128)(2,1)S(1)} %collective-permute-done.6.refs_1_.refs_2_, ...), custom_call_target="tpu_custom_call" | custom-call | flops 4982833152 | tf_op jit(solution)/shard_map/experts/pallas_call | solution.py:258
  83.7 1.6 collective-permute-start.19
  86.7 1.7 %collective-permute-done.14.refs_3_ = bf16[144,2048]{1,0:T(8,128)(2,1)S(1)} collective-permute-done((bf16[144,2048]{1,0:T(8,128)(2,1)S(1)}, bf16[144,2048]{1,0:T(8,128)(2,1)S(1)}, u32[]{:S(2)}, u32[]{:S(2)}) %collective-permute-start.14) | collective-permute-done | bytes 589856 | tf_op jit(solution)/shard_map/ppermute | solution.py:39
  88.5 6.4 %experts.6 = (bf16[144,2048]{1,0:T(8,128)(2,1)S(1)}, bf16[144,2048]{1,0:T(8,128)(2,1)S(1)}) custom-call(s32[2]{0:T(128)S(1)} %dynamic-slice_bitcast_fusion.slot_ref.refs_0_, bf16[136,2048]{1,0:T(8,128)(2,1)S(1)} %collective-permute-done.10.refs_0_.refs_1_, bf16[136,2048]{1,0:T(8,128)(2,1)S(1)} %collective-permute-done.11.refs_1_.refs_2_, ...), custom_call_target="tpu_custom_call" | custom-call | flops 4982833152 | tf_op jit(solution)/shard_map/experts/pallas_call | solution.py:258
  94.9 1.3 combine.4
  98.3 1.3 collective-permute-start.17
  99.6 3.4 %collective-permute-done.18.refs_3_ = bf16[144,2048]{1,0:T(8,128)(2,1)S(1)} collective-permute-done((bf16[144,2048]{1,0:T(8,128)(2,1)S(1)}, bf16[144,2048]{1,0:T(8,128)(2,1)S(1)}, u32[]{:S(2)}, u32[]{:S(2)}) %collective-permute-start.18) | collective-permute-done | bytes 589856 | tf_op jit(solution)/shard_map/ppermute | solution.py:39
  103.0 6.6 %experts.7 = (bf16[144,2048]{1,0:T(8,128)(2,1)S(1)}, bf16[144,2048]{1,0:T(8,128)(2,1)S(1)}) custom-call(s32[2]{0:T(128)S(1)} %dynamic-slice_bitcast_fusion.slot_ref.refs_0_, bf16[136,2048]{1,0:T(8,128)(2,1)S(1)} %collective-permute-done.15.refs_0_.refs_1_, bf16[136,2048]{1,0:T(8,128)(2,1)S(1)} %collective-permute-done.16.refs_1_.refs_2_, ...), custom_call_target="tpu_custom_call" | custom-call | flops 4982833152 | tf_op jit(solution)/shard_map/experts/pallas_call | solution.py:258
  109.6 1.8 %collective-permute-start.21 = (bf16[144,2048]{1,0:T(8,128)(2,1)S(1)}, bf16[144,2048]{1,0:T(8,128)(2,1)S(1)}, u32[]{:S(2)}, u32[]{:S(2)}) collective-permute-start(bf16[144,2048]{1,0:T(8,128)(2,1)S(1)} %get-tuple-element.50), channel_id=1, source_target_pairs={{0,4},{1,3},{2,6},{3,1},{4,0},{5,7},{6,2},{7,5},{8,12},{9,11},{10,... | collective-permute-start | bytes 1769480 | tf_op jit(solution)/shard_map/ppermute | solution.py:39
  111.7 16.6 %collective-permute-done.17.refs_3_ = bf16[144,2048]{1,0:T(8,128)(2,1)S(1)} collective-permute-done((bf16[144,2048]{1,0:T(8,128)(2,1)S(1)}, bf16[144,2048]{1,0:T(8,128)(2,1)S(1)}, u32[]{:S(2)}, u32[]{:S(2)}) %collective-permute-start.17) | collective-permute-done | bytes 589856 | tf_op jit(solution)/shard_map/ppermute | solution.py:39
  128.3 1.3 combine.5
  129.9 1.4 combine.6
  131.3 9.7 %collective-permute-done.21.refs_3_ = bf16[144,2048]{1,0:T(8,128)(2,1)S(1)} collective-permute-done((bf16[144,2048]{1,0:T(8,128)(2,1)S(1)}, bf16[144,2048]{1,0:T(8,128)(2,1)S(1)}, u32[]{:S(2)}, u32[]{:S(2)}) %collective-permute-start.21) | collective-permute-done | bytes 589856 | tf_op jit(solution)/shard_map/ppermute | solution.py:39
  140.9 1.3 combine.7
  142.8 1.9 %collective-permute-start.20 = (bf16[128,2048]{1,0:T(8,128)(2,1)S(1)}, bf16[128,2048]{1,0:T(8,128)(2,1)S(1)}, u32[]{:S(2)}, u32[]{:S(2)}) collective-permute-start(bf16[128,2048]{1,0:T(8,128)(2,1)S(1)} %get-tuple-element.49), channel_id=1, source_target_pairs={{0,2},{1,3},{2,0},{3,1},{4,6},{5,7},{6,4},{7,5},{8,10},{9,11},{10,... | collective-permute-start | bytes 1572872 | tf_op jit(solution)/shard_map/ppermute | solution.py:39
  144.7 6.8 %collective-permute-done.22 = bf16[128,2048]{1,0:T(8,128)(2,1)S(1)} collective-permute-done((bf16[128,2048]{1,0:T(8,128)(2,1)S(1)}, bf16[128,2048]{1,0:T(8,128)(2,1)S(1)}, u32[]{:S(2)}, u32[]{:S(2)}) %collective-permute-start.22) | collective-permute-done | bytes 524320 | tf_op jit(solution)/shard_map/ppermute | solution.py:39
  151.5 6.9 %collective-permute-done.26 = bf16[128,2048]{1,0:T(8,128)(2,1)S(1)} collective-permute-done((bf16[128,2048]{1,0:T(8,128)(2,1)S(1)}, bf16[128,2048]{1,0:T(8,128)(2,1)S(1)}, u32[]{:S(2)}, u32[]{:S(2)}) %collective-permute-start.26) | collective-permute-done | bytes 524320 | tf_op jit(solution)/shard_map/ppermute | solution.py:39
  158.7 11.0 %collective-permute-done.27 = bf16[128,2048]{1,0:T(8,128)(2,1)S(1)} collective-permute-done((bf16[128,2048]{1,0:T(8,128)(2,1)S(1)}, bf16[128,2048]{1,0:T(8,128)(2,1)S(1)}, u32[]{:S(2)}, u32[]{:S(2)}) %collective-permute-start.27) | collective-permute-done | bytes 524320 | tf_op jit(solution)/shard_map/ppermute | solution.py:39
  (59 shorter events, 15.7 us)
Async XLA Ops:
  0.0 4.4 %copy-start = (bf16[2048,16]{0,1:T(8,128)(2,1)S(1)}, bf16[2048,16]{0,1:T(8,128)(2,1)}, u32[]{:S(2)}) copy-start(bf16[2048,16]{0,1:T(8,128)(2,1)} %param.17) | copy-start | bytes 196612
  0.0 41.1 %collective-permute-start.1 = (bf16[704,2048]{1,0:T(8,128)(2,1)}, bf16[704,2048]{1,0:T(8,128)(2,1)}, u32[]{:S(2)}, u32[]{:S(2)}) collective-permute-start(bf16[704,2048]{1,0:T(8,128)(2,1)} %bitcast.12), channel_id=1, source_target_pairs={{0,1},{1,0},{2,3},{3,2},{4,5},{5,4},{6,7},{7,6},{8,9},{9,8},{10,11... | collective-permute-start | bytes 8650760 | tf_op jit(solution)/shard_map/ppermute | solution.py:39
  0.5 40.6 %collective-permute-start.2 = (bf16[704,2048]{1,0:T(8,128)(2,1)}, bf16[704,2048]{1,0:T(8,128)(2,1)}, u32[]{:S(2)}, u32[]{:S(2)}) collective-permute-start(bf16[704,2048]{1,0:T(8,128)(2,1)} %bitcast.14), channel_id=1, source_target_pairs={{0,1},{1,0},{2,3},{3,2},{4,5},{5,4},{6,7},{7,6},{8,9},{9,8},{10,11... | collective-permute-start | bytes 8650760 | tf_op jit(solution)/shard_map/ppermute | solution.py:39
  0.6 40.6 %collective-permute-start.3 = (bf16[704,2048]{1,0:T(8,128)(2,1)}, bf16[704,2048]{1,0:T(8,128)(2,1)}, u32[]{:S(2)}, u32[]{:S(2)}) collective-permute-start(bf16[704,2048]{1,0:T(8,128)(2,1)} %refs_2_.1), channel_id=1, source_target_pairs={{0,1},{1,0},{2,3},{3,2},{4,5},{5,4},{6,7},{7,6},{8,9},{9,8},{10,11... | collective-permute-start | bytes 8650760 | tf_op jit(solution)/shard_map/ppermute | solution.py:39
  5.7 17.9 %collective-permute-start.5 = (bf16[136,2048]{1,0:T(8,128)(2,1)S(1)}, bf16[136,2048]{1,0:T(8,128)(2,1)S(1)}, u32[]{:S(2)}, u32[]{:S(2)}) collective-permute-start(bf16[136,2048]{1,0:T(8,128)(2,1)S(1)} %pad_maximum_fusion.refs_6_.refs_0_.refs_1_), channel_id=1, source_target_pairs={{0,8},{1,9},{2,10},{3,11},{4,12},{5,13},{6,14},{7,15},{8,16},{9,17... | collective-permute-start | bytes 1671176 | tf_op jit(solution)/shard_map/ppermute | solution.py:39
  8.4 16.0 %collective-permute-start = (bf16[136,2048]{1,0:T(8,128)(2,1)S(1)}, bf16[136,2048]{1,0:T(8,128)(2,1)S(1)}, u32[]{:S(2)}, u32[]{:S(2)}) collective-permute-start(bf16[136,2048]{1,0:T(8,128)(2,1)S(1)} %pad_maximum_fusion.refs_6_.refs_0_.refs_1_), channel_id=1, source_target_pairs={{0,2},{1,3},{2,0},{3,1},{4,6},{5,7},{6,4},{7,5},{8,10},{9,11},{10,... | collective-permute-start | bytes 1671176 | tf_op jit(solution)/shard_map/ppermute | solution.py:39
  23.6 16.2 %collective-permute-start.10 = (bf16[136,2048]{1,0:T(8,128)(2,1)S(1)}, bf16[136,2048]{1,0:T(8,128)(2,1)S(1)}, u32[]{:S(2)}, u32[]{:S(2)}) collective-permute-start(bf16[136,2048]{1,0:T(8,128)(2,1)S(1)} %collective-permute-done.5.refs_0_.refs_1_), channel_id=1, source_target_pairs={{0,8},{1,9},{2,10},{3,11},{4,12},{5,13},{6,14},{7,15},{8,16},{9,17... | collective-permute-start | bytes 1671176 | tf_op jit(solution)/shard_map/ppermute | solution.py:39
  24.3 26.1 %collective-permute-start.7 = (bf16[136,2048]{1,0:T(8,128)(2,1)S(1)}, bf16[136,2048]{1,0:T(8,128)(2,1)S(1)}, u32[]{:S(2)}, u32[]{:S(2)}) collective-permute-start(bf16[136,2048]{1,0:T(8,128)(2,1)S(1)} %pad_maximum_fusion.refs_6_.refs_0_.refs_1_), channel_id=1, source_target_pairs={{0,1},{1,0},{2,3},{3,2},{4,5},{5,4},{6,7},{7,6},{8,9},{9,8},{10,11... | collective-permute-start | bytes 1671176 | tf_op jit(solution)/shard_map/ppermute | solution.py:39
  39.8 18.5 %collective-permute-start.6 = (bf16[136,2048]{1,0:T(8,128)(2,1)S(1)}, bf16[136,2048]{1,0:T(8,128)(2,1)S(1)}, u32[]{:S(2)}, u32[]{:S(2)}) collective-permute-start(bf16[136,2048]{1,0:T(8,128)(2,1)S(1)} %collective-permute-done.5.refs_0_.refs_1_), channel_id=1, source_target_pairs={{0,2},{1,5},{2,0},{3,7},{4,6},{5,1},{6,4},{7,3},{8,10},{9,13},{10,... | collective-permute-start | bytes 1671176 | tf_op jit(solution)/shard_map/ppermute | solution.py:39
  41.1 9.9 %collective-permute-start.8 = (bf16[136,2048]{1,0:T(8,128)(2,1)S(1)}, bf16[136,2048]{1,0:T(8,128)(2,1)S(1)}, u32[]{:S(2)}, u32[]{:S(2)}) collective-permute-start(bf16[136,2048]{1,0:T(8,128)(2,1)S(1)} %collective-permute-done.refs_1_.refs_2_), channel_id=1, source_target_pairs={{0,1},{1,0},{2,3},{3,2},{4,5},{5,4},{6,7},{7,6},{8,9},{9,8},{10,11... | collective-permute-start | bytes 1671176 | tf_op jit(solution)/shard_map/ppermute | solution.py:39
  41.1 18.9 %collective-permute-start.15 = (bf16[136,2048]{1,0:T(8,128)(2,1)S(1)}, bf16[136,2048]{1,0:T(8,128)(2,1)S(1)}, u32[]{:S(2)}, u32[]{:S(2)}) collective-permute-start(bf16[136,2048]{1,0:T(8,128)(2,1)S(1)} %collective-permute-done.10.refs_0_.refs_1_), channel_id=1, source_target_pairs={{0,8},{1,9},{2,10},{3,11},{4,12},{5,13},{6,14},{7,15},{8,16},{9,17... | collective-permute-start | bytes 1671176 | tf_op jit(solution)/shard_map/ppermute | solution.py:39
  48.1 16.3 %collective-permute-start.4 = (bf16[144,2048]{1,0:T(8,128)(2,1)S(1)}, bf16[144,2048]{1,0:T(8,128)(2,1)S(1)}, u32[]{:S(2)}, u32[]{:S(2)}) collective-permute-start(bf16[144,2048]{1,0:T(8,128)(2,1)S(1)} %send_rows.4.refs_7_), channel_id=1, source_target_pairs={{0,4},{1,5},{2,6},{3,7},{4,0},{5,1},{6,2},{7,3},{8,12},{9,13},{10,... | collective-permute-start | bytes 1769480 | tf_op jit(solution)/shard_map/ppermute | solution.py:39
  50.4 20.4 %collective-permute-start.11 = (bf16[136,2048]{1,0:T(8,128)(2,1)S(1)}, bf16[136,2048]{1,0:T(8,128)(2,1)S(1)}, u32[]{:S(2)}, u32[]{:S(2)}) collective-permute-start(bf16[136,2048]{1,0:T(8,128)(2,1)S(1)} %collective-permute-done.10.refs_0_.refs_1_), channel_id=1, source_target_pairs={{0,2},{1,5},{2,0},{3,7},{4,6},{5,1},{6,4},{7,3},{8,10},{9,13},{10,... | collective-permute-start | bytes 1671176 | tf_op jit(solution)/shard_map/ppermute | solution.py:39
  59.2 17.9 %collective-permute-start.9 = (bf16[144,2048]{1,0:T(8,128)(2,1)S(1)}, bf16[144,2048]{1,0:T(8,128)(2,1)S(1)}, u32[]{:S(2)}, u32[]{:S(2)}) collective-permute-start(bf16[144,2048]{1,0:T(8,128)(2,1)S(1)} %send_rows.5.refs_10_), channel_id=1, source_target_pairs={{0,4},{1,3},{2,6},{3,1},{4,0},{5,7},{6,2},{7,5},{8,12},{9,11},{10,... | collective-permute-start | bytes 1769480 | tf_op jit(solution)/shard_map/ppermute | solution.py:39
  60.0 25.3 %collective-permute-start.16 = (bf16[136,2048]{1,0:T(8,128)(2,1)S(1)}, bf16[136,2048]{1,0:T(8,128)(2,1)S(1)}, u32[]{:S(2)}, u32[]{:S(2)}) collective-permute-start(bf16[136,2048]{1,0:T(8,128)(2,1)S(1)} %collective-permute-done.15.refs_0_.refs_1_), channel_id=1, source_target_pairs={{0,2},{1,5},{2,0},{3,7},{4,6},{5,1},{6,4},{7,3},{8,10},{9,13},{10,... | collective-permute-start | bytes 1671176 | tf_op jit(solution)/shard_map/ppermute | solution.py:39
  71.7 16.7 %collective-permute-start.14 = (bf16[144,2048]{1,0:T(8,128)(2,1)S(1)}, bf16[144,2048]{1,0:T(8,128)(2,1)S(1)}, u32[]{:S(2)}, u32[]{:S(2)}) collective-permute-start(bf16[144,2048]{1,0:T(8,128)(2,1)S(1)} %send_rows.6.refs_10_), channel_id=1, source_target_pairs={{0,4},{1,3},{2,6},{3,1},{4,0},{5,7},{6,2},{7,5},{8,12},{9,11},{10,... | collective-permute-start | bytes 1769480 | tf_op jit(solution)/shard_map/ppermute | solution.py:39
  83.7 11.2 %collective-permute-start.19 = (bf16[144,2048]{1,0:T(8,128)(2,1)S(1)}, bf16[144,2048]{1,0:T(8,128)(2,1)S(1)}, u32[]{:S(2)}, u32[]{:S(2)}) collective-permute-start(bf16[144,2048]{1,0:T(8,128)(2,1)S(1)} %get-tuple-element.44), channel_id=1, source_target_pairs={{0,4},{1,3},{2,6},{3,1},{4,0},{5,7},{6,2},{7,5},{8,12},{9,11},{10,... | collective-permute-start | bytes 1769480 | tf_op jit(solution)/shard_map/ppermute | solution.py:39
  86.1 16.9 %collective-permute-start.18 = (bf16[144,2048]{1,0:T(8,128)(2,1)S(1)}, bf16[144,2048]{1,0:T(8,128)(2,1)S(1)}, u32[]{:S(2)}, u32[]{:S(2)}) collective-permute-start(bf16[144,2048]{1,0:T(8,128)(2,1)S(1)} %send_rows.7.refs_10_), channel_id=1, source_target_pairs={{0,4},{1,3},{2,6},{3,1},{4,0},{5,7},{6,2},{7,5},{8,12},{9,11},{10,... | collective-permute-start | bytes 1769480 | tf_op jit(solution)/shard_map/ppermute | solution.py:39
  96.2 15.2 %collective-permute-start.24 = (bf16[128,2048]{1,0:T(8,128)(2,1)S(1)}, bf16[128,2048]{1,0:T(8,128)(2,1)S(1)}, u32[]{:S(2)}, u32[]{:S(2)}) collective-permute-start(bf16[128,2048]{1,0:T(8,128)(2,1)S(1)} %get-tuple-element.54), channel_id=1, source_target_pairs={{0,2},{1,5},{2,0},{3,7},{4,6},{5,1},{6,4},{7,3},{8,10},{9,13},{10,... | collective-permute-start | bytes 1572872 | tf_op jit(solution)/shard_map/ppermute | solution.py:39
  97.0 32.9 %collective-permute-start.13 = (bf16[256,2048]{1,0:T(8,128)(2,1)S(1)}, bf16[256,2048]{1,0:T(8,128)(2,1)S(1)}, u32[]{:S(2)}, u32[]{:S(2)}) collective-permute-start(bf16[256,2048]{1,0:T(8,128)(2,1)S(1)} %get-tuple-element.41), channel_id=1, source_target_pairs={{0,1},{1,0},{2,3},{3,2},{4,5},{5,4},{6,7},{7,6},{8,9},{9,8},{10,11... | collective-permute-start | bytes 3145736 | tf_op jit(solution)/shard_map/ppermute | solution.py:39
  97.6 32.3 %collective-permute-start.12 = (bf16[144,2048]{1,0:T(8,128)(2,1)S(1)}, bf16[144,2048]{1,0:T(8,128)(2,1)S(1)}, u32[]{:S(2)}, u32[]{:S(2)}) collective-permute-start(bf16[144,2048]{1,0:T(8,128)(2,1)S(1)} %get-tuple-element.40), channel_id=1, source_target_pairs={{0,4},{1,5},{2,6},{3,7},{4,0},{5,1},{6,2},{7,3},{8,12},{9,13},{10,... | collective-permute-start | bytes 1769480 | tf_op jit(solution)/shard_map/ppermute | solution.py:39
  98.3 29.9 %collective-permute-start.17 = (bf16[144,2048]{1,0:T(8,128)(2,1)S(1)}, bf16[144,2048]{1,0:T(8,128)(2,1)S(1)}, u32[]{:S(2)}, u32[]{:S(2)}) collective-permute-start(bf16[144,2048]{1,0:T(8,128)(2,1)S(1)} %get-tuple-element.43), channel_id=1, source_target_pairs={{0,4},{1,3},{2,6},{3,1},{4,0},{5,7},{6,2},{7,5},{8,12},{9,11},{10,... | collective-permute-start | bytes 1769480 | tf_op jit(solution)/shard_map/ppermute | solution.py:39
  109.6 31.3 %collective-permute-start.21 = (bf16[144,2048]{1,0:T(8,128)(2,1)S(1)}, bf16[144,2048]{1,0:T(8,128)(2,1)S(1)}, u32[]{:S(2)}, u32[]{:S(2)}) collective-permute-start(bf16[144,2048]{1,0:T(8,128)(2,1)S(1)} %get-tuple-element.50), channel_id=1, source_target_pairs={{0,4},{1,3},{2,6},{3,1},{4,0},{5,7},{6,2},{7,5},{8,12},{9,11},{10,... | collective-permute-start | bytes 1769480 | tf_op jit(solution)/shard_map/ppermute | solution.py:39
  111.6 30.9 %collective-permute-start.25 = (bf16[128,2048]{1,0:T(8,128)(2,1)S(1)}, bf16[128,2048]{1,0:T(8,128)(2,1)S(1)}, u32[]{:S(2)}, u32[]{:S(2)}) collective-permute-start(bf16[128,2048]{1,0:T(8,128)(2,1)S(1)} %add_convert_fusion.3), channel_id=1, source_target_pairs={{0,8},{1,9},{2,10},{3,11},{4,12},{5,13},{6,14},{7,15},{8,16},{9,17... | collective-permute-start | bytes 1572872 | tf_op jit(solution)/shard_map/ppermute | solution.py:39
  129.6 12.9 %collective-permute-start.23 = (bf16[128,2048]{1,0:T(8,128)(2,1)S(1)}, bf16[128,2048]{1,0:T(8,128)(2,1)S(1)}, u32[]{:S(2)}, u32[]{:S(2)}) collective-permute-start(bf16[128,2048]{1,0:T(8,128)(2,1)S(1)} %get-tuple-element.53), channel_id=1, source_target_pairs={{0,2},{1,5},{2,0},{3,7},{4,6},{5,1},{6,4},{7,3},{8,10},{9,13},{10,... | collective-permute-start | bytes 1572872 | tf_op jit(solution)/shard_map/ppermute | solution.py:39
  142.2 9.2 %collective-permute-start.22 = (bf16[128,2048]{1,0:T(8,128)(2,1)S(1)}, bf16[128,2048]{1,0:T(8,128)(2,1)S(1)}, u32[]{:S(2)}, u32[]{:S(2)}) collective-permute-start(bf16[128,2048]{1,0:T(8,128)(2,1)S(1)} %get-tuple-element.52), channel_id=1, source_target_pairs={{0,2},{1,5},{2,0},{3,7},{4,6},{5,1},{6,4},{7,3},{8,10},{9,13},{10,... | collective-permute-start | bytes 1572872 | tf_op jit(solution)/shard_map/ppermute | solution.py:39
  142.5 28.1 %copy-start.1 = (bf16[2048,16]{0,1:T(8,128)(2,1)S(1)}, bf16[2048,16]{0,1:T(8,128)(2,1)}, u32[]{:S(2)}) copy-start(bf16[2048,16]{0,1:T(8,128)(2,1)} %param.17) | copy-start | bytes 196612
  142.7 15.7 %collective-permute-start.26 = (bf16[128,2048]{1,0:T(8,128)(2,1)S(1)}, bf16[128,2048]{1,0:T(8,128)(2,1)S(1)}, u32[]{:S(2)}, u32[]{:S(2)}) collective-permute-start(bf16[128,2048]{1,0:T(8,128)(2,1)S(1)} %add_convert_fusion.2), channel_id=1, source_target_pairs={{0,8},{1,9},{2,10},{3,11},{4,12},{5,13},{6,14},{7,15},{8,16},{9,17... | collective-permute-start | bytes 1572872 | tf_op jit(solution)/shard_map/ppermute | solution.py:39
  142.8 15.9 %collective-permute-start.20 = (bf16[128,2048]{1,0:T(8,128)(2,1)S(1)}, bf16[128,2048]{1,0:T(8,128)(2,1)S(1)}, u32[]{:S(2)}, u32[]{:S(2)}) collective-permute-start(bf16[128,2048]{1,0:T(8,128)(2,1)S(1)} %get-tuple-element.49), channel_id=1, source_target_pairs={{0,2},{1,3},{2,0},{3,1},{4,6},{5,7},{6,4},{7,5},{8,10},{9,11},{10,... | collective-permute-start | bytes 1572872 | tf_op jit(solution)/shard_map/ppermute | solution.py:39
  158.6 11.0 %collective-permute-start.27 = (bf16[128,2048]{1,0:T(8,128)(2,1)S(1)}, bf16[128,2048]{1,0:T(8,128)(2,1)S(1)}, u32[]{:S(2)}, u32[]{:S(2)}) collective-permute-start(bf16[128,2048]{1,0:T(8,128)(2,1)S(1)} %add_convert_fusion.1), channel_id=1, source_target_pairs={{0,8},{1,9},{2,10},{3,11},{4,12},{5,13},{6,14},{7,15},{8,16},{9,17... | collective-permute-start | bytes 1572872 | tf_op jit(solution)/shard_map/ppermute | solution.py:39
where the time goes:
time: 171 us
  waiting for transfers between devices  92.3 us (54%)
  Pallas kernels  48.3 us (28%)
  starting transfers between devices  22.3 us (13%)
  other arithmetic  4.84 us (3%)
    ppermute x28, waiting for transfers between devices, shift(): return lax.ppermute(block, AXES, route)  92.3 us
    pallas_call x5, Pallas kernels, feed_forward(): return list(call(*operands, *kept(blocks), *kept(came), *weights, *after))  33.4 us
    ppermute x28, starting transfers between devices, shift(): return lax.ppermute(block, AXES, route)  22.3 us
    pallas_call x1, Pallas kernels, load(): return list(call(*kept(arrays, pltpu.HBM), *after))  6.06 us
    pallas_call x4, Pallas kernels, combine(): return list(call(chosen, *kept(blocks), *kept(back), *kept(extra), *after))  5.29 us
    pallas_call x4, Pallas kernels, send_rows(): return list(call(chosen, *kept(blocks), *after))  3.49 us
  transfers between devices with their start and end apart: 28, of which 11 were waited for; matrix products, arithmetic and copies ran while one was open for 4% of the time, Pallas kernels for 28%

commit v1 on v0

--- a/solution.py
+++ b/solution.py
@@ -15,7 +15,7 @@
 STRIP = 8
 UNUSED = -4096.0
 PIECE = 256
-LIMIT = 16 << 20
+LIMIT = 10 << 20
 
 
 def places(dims):
@@ -34,14 +34,21 @@
     return index_of(dims, {**place, axis: place[axis] + step})
 
 
-def shift(block, dims, axes, step):
-    route = [(i, moved(dims, p, axes, step)) for i, p in enumerate(places(dims))]
+def shift(block, dims, axes, step, only=None):
+    route = [
+        (i, moved(dims, p, axes, step))
+        for i, p in enumerate(places(dims))
+        if only is None or p["c"] in only
+    ]
     return lax.ppermute(block, AXES, route)
 
 
-def targets(dims, axes):
+def targets(dims, axes, direct):
     size = dims[axes[0]]
-    table = [[moved(dims, p, axes, d) // dims["c"] for d in range(size)] for p in places(dims)]
+    table = [
+        [moved(dims, p, axes, d) // dims["c"] for d in range(size)] + [int(p["c"] in direct)]
+        for p in places(dims)
+    ]
     return lax.dynamic_index_in_dim(
         jnp.asarray(np.array(table, np.int32)), lax.axis_index(AXES), 0, keepdims=False
     )
@@ -131,7 +138,7 @@
 def send_rows(blocks, chosen, shape, after):
     slots, tok_rows, capacity, list_rows = shape
     width = blocks[0].shape[1]
-    outs = chosen.shape[0] - 1
+    outs = chosen.shape[0] - 2
 
     def kernel(slot_ref, *refs):
         block_refs = refs[: len(blocks)]
@@ -283,7 +290,8 @@
                 )
                 sums = part if sums is None else sums + part
             for ref in extra_refs:
-                sums = sums + ref[span]
+                more = ref[span].astype(F32)
+                sums = sums + (more * slot_ref[len(back)].astype(F32) if i else more)
             out[...] = sums.astype(out.dtype)
 
     flops = 2 * len(back) * list_rows * len(blocks) * tok_rows * width
@@ -329,7 +337,9 @@
     shape = (slots, tok_rows, capacity, list_rows)
     steps = dims["z"]
     mixed = ("xy", "yx") if x_count == y_count else ("xy", "xy")
-    orders = [("xy", "xy")] + [mixed] * (steps - 1)
+    orders = [mixed] * steps
+    direct = [c for c in range(cores) if mixed[c % 2][0] == "x"]
+    others = [c for c in range(cores) if c not in direct]
 
     def slices_of(*weights):
         return [list(weights)] + [
@@ -348,14 +358,11 @@
         own.append(shift(own[-1], dims, "z", 1))
 
     last = own[:1]
-    loaded = load([w for weights in expert_slices for w in weights], last)
-    expert_slices = [loaded[i : i + 3] for i in range(0, len(loaded), 3)]
-    last = loaded[-1:]
     blocks, chosen, came, results, parts = {}, {}, {}, {}, {}
     firsts = [[o[0] for o in order] for order in orders]
     seconds = [[o[1] for o in order] for order in orders]
     for step in range(steps):
-        chosen[step] = targets(dims, seconds[step])
+        chosen[step] = targets(dims, seconds[step], direct)
         blocks[step] = [own[step]] + [
             shift(own[step], dims, firsts[step], d) for d in range(1, dims[firsts[step][0]])
         ]
@@ -373,10 +380,8 @@
         )
         last = results[step][:1]
 
-    def give(step, held=None):
+    def give(step):
         own_rows, *rest = results[step]
-        if held is not None:
-            rest = lax.optimization_barrier((*rest, results[held][0]))[:-1]
         results[step] = [own_rows] + [
             shift(r, dims, seconds[step], -d - 1) for d, r in enumerate(rest)
         ]
@@ -389,38 +394,58 @@
             shift(r, dims, firsts[step], -d - 1) for d, r in enumerate(out[1:])
         ]
 
+    wide = blocks[0]
+    if others:
+        side = [shift(own[0], dims, "x", d, others) for d in range(1, dims["x"])]
+        wide = own[:1] + [
+            jnp.where(chosen[0][-1] > 0, b, s) for b, s in zip(blocks[0][1:], side)
+        ]
+    peers = [shift(b, dims, "c", d) for d in range(1, cores) for b in wide]
+
+    def spread():
+        nonlocal last, shared
+        shared = feed_forward(
+            wide, peers, [[shared_gate.T, shared_up.T, shared_down]], None, shape, last
+        )
+        last = shared[:1]
+        shared = shared[:1] + [shift(r, dims, "c", -d - 1) for d, r in enumerate(shared[1:])]
+        for d in range(1, dims["x"] if others else 1):
+            span = slice(d * tok_rows, (d + 1) * tok_rows)
+            away = sum(r[span].astype(F32) for r in shared).astype(BF16)
+            aside.append(shift(away, dims, "x", -d, others))
+
+    shared, aside = [], []
     later = list(range(1, steps))
-    send(0)
-    peers = [shift(b, dims, "c", d) for d in range(1, cores) for b in blocks[0]]
-    shared = feed_forward(
-        blocks[0], peers, [[shared_gate.T, shared_up.T, shared_down]], None, shape, last
-    )
-    last = shared[:1]
-    shared = shared[:1] + [shift(r, dims, "c", -d - 1) for d, r in enumerate(shared[1:])]
-    for step in later[:1]:
+    loaded = load([w for weights in expert_slices for w in weights], last)
+    expert_slices = [loaded[i : i + 3] for i in range(0, len(loaded), 3)]
+    last = loaded[-1:]
+    for step in [0] + later[:1]:
         send(step)
-    run(0)
-    for n, step in enumerate(later):
-        if n + 1 < len(later):
-            send(later[n + 1])
-        if n > 1:
-            join(later[n - 2])
+    for step in [0] + later[:1]:
         run(step)
         give(step)
-        if n == 0:
-            give(0, step)
-    for step in later[-2:-1]:
+    for step in later[1:2]:
+        send(step)
+    spread()
+    for step in later[:1]:
         join(step)
-    if not later:
-        give(0)
+    for step in later[1:2]:
+        run(step)
+        give(step)
+    for step in later[2:]:
+        send(step)
     join(0, shared)
-    for step in later[-1:]:
+    for step in later[1:2]:
+        join(step)
+    for step in later[2:]:
+        run(step)
+        give(step)
         join(step)
 
     passed = []
     for step in later + [0]:
         total = parts[step][0]
-        for part in parts[step][1:] + passed:
+        for part in parts[step][1:] + passed + ([] if step else aside):
             total = total + part.astype(F32)
         total = total.astype(BF16)
         if step:

time: 171 us -> 159 us (0.930)
  waiting for transfers between devices: 92.3 us -> 74.6 us
  starting transfers between devices: 22.3 us -> 27.1 us
    ppermute x28 -> x30, waiting for transfers between devices: 92.3 us -> 74.6 us  [shift(): return lax.ppermute(block, AXES, route)]
    ppermute x28 -> x30, starting transfers between devices: 22.3 us -> 27.1 us  [shift(): return lax.ppermute(block, AXES, route)]
  transfers between devices with their start and end apart: 28 -> 30, of which waited for: 11 -> 12; matrix products, arithmetic and copies ran while one was open for 4% -> 4% of each run, Pallas kernels for 28% -> 30%
where the time goes in v1:
time: 159 us
  waiting for transfers between devices  74.6 us (47%)
  Pallas kernels  48.5 us (31%)
  starting transfers between devices  27.1 us (17%)
  other arithmetic  5.17 us (3%)
    ppermute x30, waiting for transfers between devices, shift(): return lax.ppermute(block, AXES, route)  74.6 us
    pallas_call x5, Pallas kernels, feed_forward(): return list(call(*operands, *kept(blocks), *kept(came), *weights, *after))  33.6 us
    ppermute x30, starting transfers between devices, shift(): return lax.ppermute(block, AXES, route)  27.1 us
    pallas_call x1, Pallas kernels, load(): return list(call(*kept(arrays, pltpu.HBM), *after))  6.06 us
    pallas_call x4, Pallas kernels, combine(): return list(call(chosen, *kept(blocks), *kept(back), *kept(extra), *after))  5.33 us
    pallas_call x4, Pallas kernels, send_rows(): return list(call(chosen, *kept(blocks), *after))  3.49 us
  transfers between devices with their start and end apart: 30, of which 12 were waited for; matrix products, arithmetic and copies ran while one was open for 4% of the time, Pallas kernels for 30%

profile of v1, /device:TPU:0, one launch (start us, length us, event | category | flops | bytes accessed | tf_op | source)
XLA Modules:
  0.0 159.0 jit_solution(16267223233368711345)
XLA Ops:
  1.8 1.2 fusion.7
  3.2 1.2 fusion.9
  5.7 2.7 %collective-permute-start.5 = (bf16[136,2048]{1,0:T(8,128)(2,1)S(1)}, bf16[136,2048]{1,0:T(8,128)(2,1)S(1)}, u32[]{:S(2)}, u32[]{:S(2)}) collective-permute-start(bf16[136,2048]{1,0:T(8,128)(2,1)S(1)} %pad_maximum_fusion.refs_6_.refs_0_.refs_1_), channel_id=1, source_target_pairs={{0,8},{1,9},{2,10},{3,11},{4,12},{5,13},{6,14},{7,15},{8,16},{9,17... | collective-permute-start | bytes 1671176 | tf_op jit(solution)/shard_map/ppermute | solution.py:43
  8.4 1.5 collective-permute-start
  9.9 13.8 %collective-permute-done.5.refs_0_.refs_1_ = bf16[136,2048]{1,0:T(8,128)(2,1)S(1)} collective-permute-done((bf16[136,2048]{1,0:T(8,128)(2,1)S(1)}, bf16[136,2048]{1,0:T(8,128)(2,1)S(1)}, u32[]{:S(2)}, u32[]{:S(2)}) %collective-permute-start.5) | collective-permute-done | bytes 557088 | tf_op jit(solution)/shard_map/ppermute | solution.py:43
  23.6 1.5 collective-permute-start.6
  26.5 6.1 %load.1 = (bf16[704,2048]{1,0:T(8,128)(2,1)S(1)}, bf16[704,2048]{1,0:T(8,128)(2,1)S(1)}, bf16[704,2048]{1,0:T(8,128)(2,1)S(1)}, bf16[704,2048]{1,0:T(8,128)(2,1)...) custom-call(bf16[704,2048]{1,0:T(8,128)(2,1)} %bitcast.12, bf16[704,2048]{1,0:T(8,128)(2,1)} %bitcast.14, ...), custom_call_target="tpu_custom_call" | custom-call | flops 4294967296 | tf_op jit(solution)/shard_map/load/pallas_call | solution.py:131
  33.5 1.6 collective-permute-start.4
  37.8 2.1 %collective-permute-start.13 = (bf16[144,2048]{1,0:T(8,128)(2,1)S(1)}, bf16[144,2048]{1,0:T(8,128)(2,1)S(1)}, u32[]{:S(2)}, u32[]{:S(2)}) collective-permute-start(bf16[144,2048]{1,0:T(8,128)(2,1)S(1)} %send_rows.5.refs_10_), channel_id=1, source_target_pairs={{0,4},{1,3},{2,6},{3,1},{4,0},{5,7},{6,2},{7,5},{8,12},{9,11},{10,... | collective-permute-start | bytes 1769480 | tf_op jit(solution)/shard_map/ppermute | solution.py:43
  40.1 11.9 %collective-permute-done.11.refs_0_.refs_1_ = bf16[136,2048]{1,0:T(8,128)(2,1)S(1)} collective-permute-done((bf16[136,2048]{1,0:T(8,128)(2,1)S(1)}, bf16[136,2048]{1,0:T(8,128)(2,1)S(1)}, u32[]{:S(2)}, u32[]{:S(2)}) %collective-permute-start.11) | collective-permute-done | bytes 557088 | tf_op jit(solution)/shard_map/ppermute | solution.py:43
  52.4 6.5 %experts.4 = (bf16[144,2048]{1,0:T(8,128)(2,1)S(1)}, bf16[144,2048]{1,0:T(8,128)(2,1)S(1)}) custom-call(s32[3]{0:T(128)S(1)} %get-tuple-element.53.slot_ref.refs_0_, bf16[136,2048]{1,0:T(8,128)(2,1)S(1)} %pad_maximum_fusion.refs_6_.refs_0_.refs_1_, bf16[136,2048]{1,0:T(8,128)(2,1)S(1)} %collective-permute-done.refs_1_.refs_2_, ...), custom_call_target="tpu_custom_call" | custom-call | flops 4982833152 | tf_op jit(solution)/shard_map/experts/pallas_call | solution.py:265
  58.9 6.5 %experts.5 = (bf16[144,2048]{1,0:T(8,128)(2,1)S(1)}, bf16[144,2048]{1,0:T(8,128)(2,1)S(1)}) custom-call(s32[3]{0:T(128)S(1)} %get-tuple-element.53.slot_ref.refs_0_, bf16[136,2048]{1,0:T(8,128)(2,1)S(1)} %collective-permute-done.5.refs_0_.refs_1_, bf16[136,2048]{1,0:T(8,128)(2,1)S(1)} %collective-permute-done.6.refs_1_.refs_2_, ...), custom_call_target="tpu_custom_call" | custom-call | flops 4982833152 | tf_op jit(solution)/shard_map/experts/pallas_call | solution.py:265
  66.9 1.6 collective-permute-start.17
  68.5 7.5 %shared.1 = (f32[256,2048]{1,0:T(8,128)S(1)}, bf16[256,2048]{1,0:T(8,128)(2,1)S(1)}) custom-call(bf16[136,2048]{1,0:T(8,128)(2,1)S(1)} %pad_maximum_fusion.refs_6_.refs_0_.refs_1_, bf16[136,2048]{1,0:T(8,128)(2,1)S(1)} %broadcast_select_fusion.refs_1_, bf16[136,2048]{1,0:T(8,128)(2,1)S(1)} %collective-permute-done.9.refs_2_, ...), custom_call_target="tpu_custom_call" | custom-call | flops 4429185024 | tf_op jit(solution)/shard_map/shared/pallas_call | solution.py:265
  76.1 1.7 %collective-permute-start.16 = (bf16[136,2048]{1,0:T(8,128)(2,1)S(1)}, bf16[136,2048]{1,0:T(8,128)(2,1)S(1)}, u32[]{:S(2)}, u32[]{:S(2)}) collective-permute-start(bf16[136,2048]{1,0:T(8,128)(2,1)S(1)} %collective-permute-done.15.refs_0_.refs_1_), channel_id=1, source_target_pairs={{0,2},{1,5},{2,0},{3,7},{4,6},{5,1},{6,4},{7,3},{8,10},{9,13},{10,... | collective-permute-start | bytes 1671176 | tf_op jit(solution)/shard_map/ppermute | solution.py:43
  78.5 1.3 combine.4
  80.1 4.1 %collective-permute-done.17.refs_3_ = bf16[144,2048]{1,0:T(8,128)(2,1)S(1)} collective-permute-done((bf16[144,2048]{1,0:T(8,128)(2,1)S(1)}, bf16[144,2048]{1,0:T(8,128)(2,1)S(1)}, u32[]{:S(2)}, u32[]{:S(2)}) %collective-permute-start.17) | collective-permute-done | bytes 589856 | tf_op jit(solution)/shard_map/ppermute | solution.py:43
  84.2 6.5 %experts.6 = (bf16[144,2048]{1,0:T(8,128)(2,1)S(1)}, bf16[144,2048]{1,0:T(8,128)(2,1)S(1)}) custom-call(s32[3]{0:T(128)S(1)} %get-tuple-element.53.slot_ref.refs_0_, bf16[136,2048]{1,0:T(8,128)(2,1)S(1)} %collective-permute-done.11.refs_0_.refs_1_, bf16[136,2048]{1,0:T(8,128)(2,1)S(1)} %collective-permute-done.12.refs_1_.refs_2_, ...), custom_call_target="tpu_custom_call" | custom-call | flops 4982833152 | tf_op jit(solution)/shard_map/experts/pallas_call | solution.py:265
  93.8 3.1 %collective-permute-done.7.refs_3_ = bf16[144,2048]{1,0:T(8,128)(2,1)S(1)} collective-permute-done((bf16[144,2048]{1,0:T(8,128)(2,1)S(1)}, bf16[144,2048]{1,0:T(8,128)(2,1)S(1)}, u32[]{:S(2)}, u32[]{:S(2)}) %collective-permute-start.7) | collective-permute-done | bytes 589856 | tf_op jit(solution)/shard_map/ppermute | solution.py:43
  96.9 1.4 combine.5
  98.3 4.7 %collective-permute-done.25 = bf16[128,2048]{1,0:T(8,128)(2,1)S(1)} collective-permute-done((bf16[128,2048]{1,0:T(8,128)(2,1)S(1)}, bf16[128,2048]{1,0:T(8,128)(2,1)S(1)}, u32[]{:S(2)}, u32[]{:S(2)}) %collective-permute-start.25) | collective-permute-done | bytes 524320 | tf_op jit(solution)/shard_map/ppermute | solution.py:43
  103.4 2.6 %collective-permute-done.21.refs_3_ = bf16[144,2048]{1,0:T(8,128)(2,1)S(1)} collective-permute-done((bf16[144,2048]{1,0:T(8,128)(2,1)S(1)}, bf16[144,2048]{1,0:T(8,128)(2,1)S(1)}, u32[]{:S(2)}, u32[]{:S(2)}) %collective-permute-start.21) | collective-permute-done | bytes 589856 | tf_op jit(solution)/shard_map/ppermute | solution.py:43
  105.9 1.3 combine.6
  107.3 1.7 %collective-permute-start.24 = (bf16[128,2048]{1,0:T(8,128)(2,1)S(1)}, bf16[128,2048]{1,0:T(8,128)(2,1)S(1)}, u32[]{:S(2)}, u32[]{:S(2)}) collective-permute-start(bf16[128,2048]{1,0:T(8,128)(2,1)S(1)} %get-tuple-element.51), channel_id=1, source_target_pairs={{0,2},{1,5},{2,0},{3,7},{4,6},{5,1},{6,4},{7,3},{8,10},{9,13},{10,... | collective-permute-start | bytes 1572872 | tf_op jit(solution)/shard_map/ppermute | solution.py:43
  108.9 6.6 %collective-permute-done.20.refs_3_ = bf16[144,2048]{1,0:T(8,128)(2,1)S(1)} collective-permute-done((bf16[144,2048]{1,0:T(8,128)(2,1)S(1)}, bf16[144,2048]{1,0:T(8,128)(2,1)S(1)}, u32[]{:S(2)}, u32[]{:S(2)}) %collective-permute-start.20) | collective-permute-done | bytes 589856 | tf_op jit(solution)/shard_map/ppermute | solution.py:43
  115.5 6.5 %experts.7 = (bf16[144,2048]{1,0:T(8,128)(2,1)S(1)}, bf16[144,2048]{1,0:T(8,128)(2,1)S(1)}) custom-call(s32[3]{0:T(128)S(1)} %get-tuple-element.53.slot_ref.refs_0_, bf16[136,2048]{1,0:T(8,128)(2,1)S(1)} %collective-permute-done.15.refs_0_.refs_1_, bf16[136,2048]{1,0:T(8,128)(2,1)S(1)} %collective-permute-done.16.refs_1_.refs_2_, ...), custom_call_target="tpu_custom_call" | custom-call | flops 4982833152 | tf_op jit(solution)/shard_map/experts/pallas_call | solution.py:265
  122.7 9.9 %collective-permute-done.22.refs_3_ = bf16[144,2048]{1,0:T(8,128)(2,1)S(1)} collective-permute-done((bf16[144,2048]{1,0:T(8,128)(2,1)S(1)}, bf16[144,2048]{1,0:T(8,128)(2,1)S(1)}, u32[]{:S(2)}, u32[]{:S(2)}) %collective-permute-start.22) | collective-permute-done | bytes 589856 | tf_op jit(solution)/shard_map/ppermute | solution.py:43
  132.7 1.3 combine.7
  134.0 5.0 %collective-permute-start.23 = (bf16[128,2048]{1,0:T(8,128)(2,1)S(1)}, bf16[128,2048]{1,0:T(8,128)(2,1)S(1)}, u32[]{:S(2)}, u32[]{:S(2)}) collective-permute-start(bf16[128,2048]{1,0:T(8,128)(2,1)S(1)} %get-tuple-element.50), channel_id=1, source_target_pairs={{0,2},{1,5},{2,0},{3,7},{4,6},{5,1},{6,4},{7,3},{8,10},{9,13},{10,... | collective-permute-start | bytes 1572872 | tf_op jit(solution)/shard_map/ppermute | solution.py:43
  139.9 6.2 %collective-permute-done.23 = bf16[128,2048]{1,0:T(8,128)(2,1)S(1)} collective-permute-done((bf16[128,2048]{1,0:T(8,128)(2,1)S(1)}, bf16[128,2048]{1,0:T(8,128)(2,1)S(1)}, u32[]{:S(2)}, u32[]{:S(2)}) %collective-permute-start.23) | collective-permute-done | bytes 524320 | tf_op jit(solution)/shard_map/ppermute | solution.py:43
  146.4 5.3 %collective-permute-done.19 = bf16[128,2048]{1,0:T(8,128)(2,1)S(1)} collective-permute-done((bf16[128,2048]{1,0:T(8,128)(2,1)S(1)}, bf16[128,2048]{1,0:T(8,128)(2,1)S(1)}, u32[]{:S(2)}, u32[]{:S(2)}) %collective-permute-start.19) | collective-permute-done | bytes 524320 | tf_op jit(solution)/shard_map/ppermute | solution.py:43
  151.8 6.0 %collective-permute-done.28 = bf16[128,2048]{1,0:T(8,128)(2,1)S(1)} collective-permute-done((bf16[128,2048]{1,0:T(8,128)(2,1)S(1)}, bf16[128,2048]{1,0:T(8,128)(2,1)S(1)}, u32[]{:S(2)}, u32[]{:S(2)}) %collective-permute-start.28) | collective-permute-done | bytes 524320 | tf_op jit(solution)/shard_map/ppermute | solution.py:43
  (65 shorter events, 17.0 us)
Async XLA Ops:
  0.0 4.4 %copy-start = (bf16[2048,16]{0,1:T(8,128)(2,1)S(1)}, bf16[2048,16]{0,1:T(8,128)(2,1)}, u32[]{:S(2)}) copy-start(bf16[2048,16]{0,1:T(8,128)(2,1)} %param.17) | copy-start | bytes 196612
  0.0 25.8 %collective-permute-start.1 = (bf16[704,2048]{1,0:T(8,128)(2,1)}, bf16[704,2048]{1,0:T(8,128)(2,1)}, u32[]{:S(2)}, u32[]{:S(2)}) collective-permute-start(bf16[704,2048]{1,0:T(8,128)(2,1)} %bitcast.11), channel_id=1, source_target_pairs={{0,1},{1,0},{2,3},{3,2},{4,5},{5,4},{6,7},{7,6},{8,9},{9,8},{10,11... | collective-permute-start | bytes 8650760 | tf_op jit(solution)/shard_map/ppermute | solution.py:43
  0.5 26.0 %collective-permute-start.2 = (bf16[704,2048]{1,0:T(8,128)(2,1)}, bf16[704,2048]{1,0:T(8,128)(2,1)}, u32[]{:S(2)}, u32[]{:S(2)}) collective-permute-start(bf16[704,2048]{1,0:T(8,128)(2,1)} %bitcast.13), channel_id=1, source_target_pairs={{0,1},{1,0},{2,3},{3,2},{4,5},{5,4},{6,7},{7,6},{8,9},{9,8},{10,11... | collective-permute-start | bytes 8650760 | tf_op jit(solution)/shard_map/ppermute | solution.py:43
  0.6 26.0 %collective-permute-start.3 = (bf16[704,2048]{1,0:T(8,128)(2,1)}, bf16[704,2048]{1,0:T(8,128)(2,1)}, u32[]{:S(2)}, u32[]{:S(2)}) collective-permute-start(bf16[704,2048]{1,0:T(8,128)(2,1)} %refs_2_.1), channel_id=1, source_target_pairs={{0,1},{1,0},{2,3},{3,2},{4,5},{5,4},{6,7},{7,6},{8,9},{9,8},{10,11... | collective-permute-start | bytes 8650760 | tf_op jit(solution)/shard_map/ppermute | solution.py:43
  5.7 17.9 %collective-permute-start.5 = (bf16[136,2048]{1,0:T(8,128)(2,1)S(1)}, bf16[136,2048]{1,0:T(8,128)(2,1)S(1)}, u32[]{:S(2)}, u32[]{:S(2)}) collective-permute-start(bf16[136,2048]{1,0:T(8,128)(2,1)S(1)} %pad_maximum_fusion.refs_6_.refs_0_.refs_1_), channel_id=1, source_target_pairs={{0,8},{1,9},{2,10},{3,11},{4,12},{5,13},{6,14},{7,15},{8,16},{9,17... | collective-permute-start | bytes 1671176 | tf_op jit(solution)/shard_map/ppermute | solution.py:43
  8.4 24.2 %collective-permute-start = (bf16[136,2048]{1,0:T(8,128)(2,1)S(1)}, bf16[136,2048]{1,0:T(8,128)(2,1)S(1)}, u32[]{:S(2)}, u32[]{:S(2)}) collective-permute-start(bf16[136,2048]{1,0:T(8,128)(2,1)S(1)} %pad_maximum_fusion.refs_6_.refs_0_.refs_1_), channel_id=1, source_target_pairs={{0,2},{1,5},{2,0},{3,7},{4,6},{5,1},{6,4},{7,3},{8,10},{9,13},{10,... | collective-permute-start | bytes 1671176 | tf_op jit(solution)/shard_map/ppermute | solution.py:43
  23.6 13.2 %collective-permute-start.6 = (bf16[136,2048]{1,0:T(8,128)(2,1)S(1)}, bf16[136,2048]{1,0:T(8,128)(2,1)S(1)}, u32[]{:S(2)}, u32[]{:S(2)}) collective-permute-start(bf16[136,2048]{1,0:T(8,128)(2,1)S(1)} %collective-permute-done.5.refs_0_.refs_1_), channel_id=1, source_target_pairs={{0,2},{1,5},{2,0},{3,7},{4,6},{5,1},{6,4},{7,3},{8,10},{9,13},{10,... | collective-permute-start | bytes 1671176 | tf_op jit(solution)/shard_map/ppermute | solution.py:43
  25.8 14.1 %collective-permute-start.8 = (bf16[136,2048]{1,0:T(8,128)(2,1)S(1)}, bf16[136,2048]{1,0:T(8,128)(2,1)S(1)}, u32[]{:S(2)}, u32[]{:S(2)}) collective-permute-start(bf16[136,2048]{1,0:T(8,128)(2,1)S(1)} %pad_maximum_fusion.refs_6_.refs_0_.refs_1_), channel_id=1, source_target_pairs={{1,3},{3,1},{5,7},{7,5},{9,11},{11,9},{13,15},{15,13},{17,19},{19,... | collective-permute-start | bytes 1671176 | tf_op jit(solution)/shard_map/ppermute | solution.py:43
  33.5 18.9 %collective-permute-start.4 = (bf16[144,2048]{1,0:T(8,128)(2,1)S(1)}, bf16[144,2048]{1,0:T(8,128)(2,1)S(1)}, u32[]{:S(2)}, u32[]{:S(2)}) collective-permute-start(bf16[144,2048]{1,0:T(8,128)(2,1)S(1)} %send_rows.4.refs_2_), channel_id=1, source_target_pairs={{0,4},{1,3},{2,6},{3,1},{4,0},{5,7},{6,2},{7,5},{8,12},{9,11},{10,... | collective-permute-start | bytes 1769480 | tf_op jit(solution)/shard_map/ppermute | solution.py:43
  35.1 16.9 %collective-permute-start.11 = (bf16[136,2048]{1,0:T(8,128)(2,1)S(1)}, bf16[136,2048]{1,0:T(8,128)(2,1)S(1)}, u32[]{:S(2)}, u32[]{:S(2)}) collective-permute-start(bf16[136,2048]{1,0:T(8,128)(2,1)S(1)} %collective-permute-done.5.refs_0_.refs_1_), channel_id=1, source_target_pairs={{0,8},{1,9},{2,10},{3,11},{4,12},{5,13},{6,14},{7,15},{8,16},{9,17... | collective-permute-start | bytes 1671176 | tf_op jit(solution)/shard_map/ppermute | solution.py:43
  35.1 33.4 %collective-permute-start.9 = (bf16[136,2048]{1,0:T(8,128)(2,1)S(1)}, bf16[136,2048]{1,0:T(8,128)(2,1)S(1)}, u32[]{:S(2)}, u32[]{:S(2)}) collective-permute-start(bf16[136,2048]{1,0:T(8,128)(2,1)S(1)} %pad_maximum_fusion.refs_6_.refs_0_.refs_1_), channel_id=1, source_target_pairs={{0,1},{1,0},{2,3},{3,2},{4,5},{5,4},{6,7},{7,6},{8,9},{9,8},{10,11... | collective-permute-start | bytes 1671176 | tf_op jit(solution)/shard_map/ppermute | solution.py:43
  37.8 21.1 %collective-permute-start.13 = (bf16[144,2048]{1,0:T(8,128)(2,1)S(1)}, bf16[144,2048]{1,0:T(8,128)(2,1)S(1)}, u32[]{:S(2)}, u32[]{:S(2)}) collective-permute-start(bf16[144,2048]{1,0:T(8,128)(2,1)S(1)} %send_rows.5.refs_10_), channel_id=1, source_target_pairs={{0,4},{1,3},{2,6},{3,1},{4,0},{5,7},{6,2},{7,5},{8,12},{9,11},{10,... | collective-permute-start | bytes 1769480 | tf_op jit(solution)/shard_map/ppermute | solution.py:43
  40.0 28.5 %collective-permute-start.10 = (bf16[136,2048]{1,0:T(8,128)(2,1)S(1)}, bf16[136,2048]{1,0:T(8,128)(2,1)S(1)}, u32[]{:S(2)}, u32[]{:S(2)}) collective-permute-start(bf16[136,2048]{1,0:T(8,128)(2,1)S(1)} %broadcast_select_fusion.refs_1_), channel_id=1, source_target_pairs={{0,1},{1,0},{2,3},{3,2},{4,5},{5,4},{6,7},{7,6},{8,9},{9,8},{10,11... | collective-permute-start | bytes 1671176 | tf_op jit(solution)/shard_map/ppermute | solution.py:43
  52.0 14.1 %collective-permute-start.12 = (bf16[136,2048]{1,0:T(8,128)(2,1)S(1)}, bf16[136,2048]{1,0:T(8,128)(2,1)S(1)}, u32[]{:S(2)}, u32[]{:S(2)}) collective-permute-start(bf16[136,2048]{1,0:T(8,128)(2,1)S(1)} %collective-permute-done.11.refs_0_.refs_1_), channel_id=1, source_target_pairs={{0,2},{1,5},{2,0},{3,7},{4,6},{5,1},{6,4},{7,3},{8,10},{9,13},{10,... | collective-permute-start | bytes 1671176 | tf_op jit(solution)/shard_map/ppermute | solution.py:43
  52.4 23.7 %collective-permute-start.15 = (bf16[136,2048]{1,0:T(8,128)(2,1)S(1)}, bf16[136,2048]{1,0:T(8,128)(2,1)S(1)}, u32[]{:S(2)}, u32[]{:S(2)}) collective-permute-start(bf16[136,2048]{1,0:T(8,128)(2,1)S(1)} %collective-permute-done.11.refs_0_.refs_1_), channel_id=1, source_target_pairs={{0,8},{1,9},{2,10},{3,11},{4,12},{5,13},{6,14},{7,15},{8,16},{9,17... | collective-permute-start | bytes 1671176 | tf_op jit(solution)/shard_map/ppermute | solution.py:43
  65.4 13.1 %collective-permute-start.18 = (bf16[144,2048]{1,0:T(8,128)(2,1)S(1)}, bf16[144,2048]{1,0:T(8,128)(2,1)S(1)}, u32[]{:S(2)}, u32[]{:S(2)}) collective-permute-start(bf16[144,2048]{1,0:T(8,128)(2,1)S(1)} %get-tuple-element.40), channel_id=1, source_target_pairs={{0,4},{1,3},{2,6},{3,1},{4,0},{5,7},{6,2},{7,5},{8,12},{9,11},{10,... | collective-permute-start | bytes 1769480 | tf_op jit(solution)/shard_map/ppermute | solution.py:43
  66.9 17.3 %collective-permute-start.17 = (bf16[144,2048]{1,0:T(8,128)(2,1)S(1)}, bf16[144,2048]{1,0:T(8,128)(2,1)S(1)}, u32[]{:S(2)}, u32[]{:S(2)}) collective-permute-start(bf16[144,2048]{1,0:T(8,128)(2,1)S(1)} %send_rows.6.refs_7_), channel_id=1, source_target_pairs={{0,4},{1,3},{2,6},{3,1},{4,0},{5,7},{6,2},{7,5},{8,12},{9,11},{10,... | collective-permute-start | bytes 1769480 | tf_op jit(solution)/shard_map/ppermute | solution.py:43
  76.0 20.8 %collective-permute-start.14 = (bf16[256,2048]{1,0:T(8,128)(2,1)S(1)}, bf16[256,2048]{1,0:T(8,128)(2,1)S(1)}, u32[]{:S(2)}, u32[]{:S(2)}) collective-permute-start(bf16[256,2048]{1,0:T(8,128)(2,1)S(1)} %get-tuple-element.39), channel_id=1, source_target_pairs={{0,1},{1,0},{2,3},{3,2},{4,5},{5,4},{6,7},{7,6},{8,9},{9,8},{10,11... | collective-permute-start | bytes 3145736 | tf_op jit(solution)/shard_map/ppermute | solution.py:43
  76.1 15.6 %collective-permute-start.16 = (bf16[136,2048]{1,0:T(8,128)(2,1)S(1)}, bf16[136,2048]{1,0:T(8,128)(2,1)S(1)}, u32[]{:S(2)}, u32[]{:S(2)}) collective-permute-start(bf16[136,2048]{1,0:T(8,128)(2,1)S(1)} %collective-permute-done.15.refs_0_.refs_1_), channel_id=1, source_target_pairs={{0,2},{1,5},{2,0},{3,7},{4,6},{5,1},{6,4},{7,3},{8,10},{9,13},{10,... | collective-permute-start | bytes 1671176 | tf_op jit(solution)/shard_map/ppermute | solution.py:43
  77.8 19.0 %collective-permute-start.7 = (bf16[144,2048]{1,0:T(8,128)(2,1)S(1)}, bf16[144,2048]{1,0:T(8,128)(2,1)S(1)}, u32[]{:S(2)}, u32[]{:S(2)}) collective-permute-start(bf16[144,2048]{1,0:T(8,128)(2,1)S(1)} %get-tuple-element.36), channel_id=1, source_target_pairs={{0,4},{1,3},{2,6},{3,1},{4,0},{5,7},{6,2},{7,5},{8,12},{9,11},{10,... | collective-permute-start | bytes 1769480 | tf_op jit(solution)/shard_map/ppermute | solution.py:43
  79.9 23.1 %collective-permute-start.25 = (bf16[128,2048]{1,0:T(8,128)(2,1)S(1)}, bf16[128,2048]{1,0:T(8,128)(2,1)S(1)}, u32[]{:S(2)}, u32[]{:S(2)}) collective-permute-start(bf16[128,2048]{1,0:T(8,128)(2,1)S(1)} %get-tuple-element.52), channel_id=1, source_target_pairs={{0,2},{1,5},{2,0},{3,7},{4,6},{5,1},{6,4},{7,3},{8,10},{9,13},{10,... | collective-permute-start | bytes 1572872 | tf_op jit(solution)/shard_map/ppermute | solution.py:43
  90.7 15.2 %collective-permute-start.21 = (bf16[144,2048]{1,0:T(8,128)(2,1)S(1)}, bf16[144,2048]{1,0:T(8,128)(2,1)S(1)}, u32[]{:S(2)}, u32[]{:S(2)}) collective-permute-start(bf16[144,2048]{1,0:T(8,128)(2,1)S(1)} %get-tuple-element.45), channel_id=1, source_target_pairs={{0,4},{1,3},{2,6},{3,1},{4,0},{5,7},{6,2},{7,5},{8,12},{9,11},{10,... | collective-permute-start | bytes 1769480 | tf_op jit(solution)/shard_map/ppermute | solution.py:43
  92.6 22.9 %collective-permute-start.20 = (bf16[144,2048]{1,0:T(8,128)(2,1)S(1)}, bf16[144,2048]{1,0:T(8,128)(2,1)S(1)}, u32[]{:S(2)}, u32[]{:S(2)}) collective-permute-start(bf16[144,2048]{1,0:T(8,128)(2,1)S(1)} %send_rows.7.refs_6_), channel_id=1, source_target_pairs={{0,4},{1,3},{2,6},{3,1},{4,0},{5,7},{6,2},{7,5},{8,12},{9,11},{10,... | collective-permute-start | bytes 1769480 | tf_op jit(solution)/shard_map/ppermute | solution.py:43
  103.0 19.1 %collective-permute-start.26 = (bf16[128,2048]{1,0:T(8,128)(2,1)S(1)}, bf16[128,2048]{1,0:T(8,128)(2,1)S(1)}, u32[]{:S(2)}, u32[]{:S(2)}) collective-permute-start(bf16[128,2048]{1,0:T(8,128)(2,1)S(1)} %add_convert_fusion.4), channel_id=1, source_target_pairs={{0,8},{1,9},{2,10},{3,11},{4,12},{5,13},{6,14},{7,15},{8,16},{9,17... | collective-permute-start | bytes 1572872 | tf_op jit(solution)/shard_map/ppermute | solution.py:43
  107.3 14.9 %collective-permute-start.24 = (bf16[128,2048]{1,0:T(8,128)(2,1)S(1)}, bf16[128,2048]{1,0:T(8,128)(2,1)S(1)}, u32[]{:S(2)}, u32[]{:S(2)}) collective-permute-start(bf16[128,2048]{1,0:T(8,128)(2,1)S(1)} %get-tuple-element.51), channel_id=1, source_target_pairs={{0,2},{1,5},{2,0},{3,7},{4,6},{5,1},{6,4},{7,3},{8,10},{9,13},{10,... | collective-permute-start | bytes 1572872 | tf_op jit(solution)/shard_map/ppermute | solution.py:43
  122.0 10.6 %collective-permute-start.22 = (bf16[144,2048]{1,0:T(8,128)(2,1)S(1)}, bf16[144,2048]{1,0:T(8,128)(2,1)S(1)}, u32[]{:S(2)}, u32[]{:S(2)}) collective-permute-start(bf16[144,2048]{1,0:T(8,128)(2,1)S(1)} %get-tuple-element.48), channel_id=1, source_target_pairs={{0,4},{1,3},{2,6},{3,1},{4,0},{5,7},{6,2},{7,5},{8,12},{9,11},{10,... | collective-permute-start | bytes 1769480 | tf_op jit(solution)/shard_map/ppermute | solution.py:43
  122.3 17.6 %collective-permute-start.27 = (bf16[128,2048]{1,0:T(8,128)(2,1)S(1)}, bf16[128,2048]{1,0:T(8,128)(2,1)S(1)}, u32[]{:S(2)}, u32[]{:S(2)}) collective-permute-start(bf16[128,2048]{1,0:T(8,128)(2,1)S(1)} %add_convert_fusion.3), channel_id=1, source_target_pairs={{0,8},{1,9},{2,10},{3,11},{4,12},{5,13},{6,14},{7,15},{8,16},{9,17... | collective-permute-start | bytes 1572872 | tf_op jit(solution)/shard_map/ppermute | solution.py:43
  134.0 12.2 %collective-permute-start.23 = (bf16[128,2048]{1,0:T(8,128)(2,1)S(1)}, bf16[128,2048]{1,0:T(8,128)(2,1)S(1)}, u32[]{:S(2)}, u32[]{:S(2)}) collective-permute-start(bf16[128,2048]{1,0:T(8,128)(2,1)S(1)} %get-tuple-element.50), channel_id=1, source_target_pairs={{0,2},{1,5},{2,0},{3,7},{4,6},{5,1},{6,4},{7,3},{8,10},{9,13},{10,... | collective-permute-start | bytes 1572872 | tf_op jit(solution)/shard_map/ppermute | solution.py:43
  139.0 12.8 %collective-permute-start.19 = (bf16[128,2048]{1,0:T(8,128)(2,1)S(1)}, bf16[128,2048]{1,0:T(8,128)(2,1)S(1)}, u32[]{:S(2)}, u32[]{:S(2)}) collective-permute-start(bf16[128,2048]{1,0:T(8,128)(2,1)S(1)} %get-tuple-element.44), channel_id=1, source_target_pairs={{0,2},{1,5},{2,0},{3,7},{4,6},{5,1},{6,4},{7,3},{8,10},{9,13},{10,... | collective-permute-start | bytes 1572872 | tf_op jit(solution)/shard_map/ppermute | solution.py:43
  139.2 12.6 %collective-permute-start.29 = (bf16[128,2048]{1,0:T(8,128)(2,1)S(1)}, bf16[128,2048]{1,0:T(8,128)(2,1)S(1)}, u32[]{:S(2)}, u32[]{:S(2)}) collective-permute-start(bf16[128,2048]{1,0:T(8,128)(2,1)S(1)} %add_convert_fusion.1), channel_id=1, source_target_pairs={{1,3},{3,1},{5,7},{7,5},{9,11},{11,9},{13,15},{15,13},{17,19},{19,... | collective-permute-start | bytes 1572872 | tf_op jit(solution)/shard_map/ppermute | solution.py:43
  146.2 12.8 %copy-start.1 = (bf16[2048,16]{0,1:T(8,128)(2,1)S(1)}, bf16[2048,16]{0,1:T(8,128)(2,1)}, u32[]{:S(2)}) copy-start(bf16[2048,16]{0,1:T(8,128)(2,1)} %param.17) | copy-start | bytes 196612
  146.4 11.4 %collective-permute-start.28 = (bf16[128,2048]{1,0:T(8,128)(2,1)S(1)}, bf16[128,2048]{1,0:T(8,128)(2,1)S(1)}, u32[]{:S(2)}, u32[]{:S(2)}) collective-permute-start(bf16[128,2048]{1,0:T(8,128)(2,1)S(1)} %add_convert_fusion.2), channel_id=1, source_target_pairs={{0,8},{1,9},{2,10},{3,11},{4,12},{5,13},{6,14},{7,15},{8,16},{9,17... | collective-permute-start | bytes 1572872 | tf_op jit(solution)/shard_map/ppermute | solution.py:43

commit v2 on v1

--- a/solution.py
+++ b/solution.py
@@ -416,17 +416,25 @@
 
     shared, aside = [], []
     later = list(range(1, steps))
-    loaded = load([w for weights in expert_slices for w in weights], last)
-    expert_slices = [loaded[i : i + 3] for i in range(0, len(loaded), 3)]
-    last = loaded[-1:]
-    for step in [0] + later[:1]:
+
+    def fill(number):
+        nonlocal last
+        expert_slices[number] = load(expert_slices[number], last)
+        last = expert_slices[number][-1:]
+
+    fill(0)
+    send(0)
+    for number in range(1, cores):
+        fill(number)
+    run(0)
+    for step in later[:1]:
         send(step)
-    for step in [0] + later[:1]:
+    give(0)
+    for step in later[:1]:
         run(step)
         give(step)
     for step in later[1:2]:
         send(step)
-    spread()
     for step in later[:1]:
         join(step)
     for step in later[1:2]:
@@ -434,12 +442,14 @@
         give(step)
     for step in later[2:]:
         send(step)
-    join(0, shared)
+    spread()
     for step in later[1:2]:
         join(step)
     for step in later[2:]:
         run(step)
         give(step)
+    join(0, shared)
+    for step in later[2:]:
         join(step)
 
     passed = []

time: 159 us -> 153 us (0.962)
  waiting for transfers between devices: 74.6 us -> 61.1 us
  starting transfers between devices: 27.1 us -> 33.3 us
    ppermute x30, waiting for transfers between devices: 74.6 us -> 61.1 us  [shift(): return lax.ppermute(block, AXES, route)]
    ppermute x30, starting transfers between devices: 27.1 us -> 33.3 us  [shift(): return lax.ppermute(block, AXES, route)]
    pallas_call x1 -> x2, Pallas kernels: 6.06 us -> 7.12 us  [load(): return list(call(*kept(arrays, pltpu.HBM), *after))]
  transfers between devices with their start and end apart: 30 -> 30, of which waited for: 12 -> 13; matrix products, arithmetic and copies ran while one was open for 4% -> 4% of each run, Pallas kernels for 30% -> 32%
where the time goes in v2:
time: 153 us; the launch traced here: 152 us
  waiting for transfers between devices  61.1 us (40%)
  Pallas kernels  49.3 us (32%)
  starting transfers between devices  33.3 us (22%)
  other arithmetic  5.07 us (3%)
    ppermute x30, waiting for transfers between devices, shift(): return lax.ppermute(block, AXES, route)  61.1 us
    pallas_call x5, Pallas kernels, feed_forward(): return list(call(*operands, *kept(blocks), *kept(came), *weights, *after))  33.4 us
    ppermute x30, starting transfers between devices, shift(): return lax.ppermute(block, AXES, route)  33.3 us
    pallas_call x2, Pallas kernels, load(): return list(call(*kept(arrays, pltpu.HBM), *after))  7.12 us
    pallas_call x4, Pallas kernels, combine(): return list(call(chosen, *kept(blocks), *kept(back), *kept(extra), *after))  5.28 us
    pallas_call x4, Pallas kernels, send_rows(): return list(call(chosen, *kept(blocks), *after))  3.48 us
  transfers between devices with their start and end apart: 30, of which 13 were waited for; matrix products, arithmetic and copies ran while one was open for 4% of the time, Pallas kernels for 32%

profile of v2, /device:TPU:0, one launch (start us, length us, event | category | flops | bytes accessed | tf_op | source)
XLA Modules:
  0.0 152.3 jit_solution(15456559906935696707)
XLA Ops:
  5.7 2.6 %collective-permute-start = (bf16[136,2048]{1,0:T(8,128)(2,1)S(1)}, bf16[136,2048]{1,0:T(8,128)(2,1)S(1)}, u32[]{:S(2)}, u32[]{:S(2)}) collective-permute-start(bf16[136,2048]{1,0:T(8,128)(2,1)S(1)} %pad_maximum_fusion.refs_3_.refs_0_.refs_1_), channel_id=1, source_target_pairs={{0,2},{1,5},{2,0},{3,7},{4,6},{5,1},{6,4},{7,3},{8,10},{9,13},{10,... | collective-permute-start | bytes 1671176 | tf_op jit(solution)/shard_map/ppermute | solution.py:43
  8.3 1.6 %collective-permute-start.9 = (bf16[136,2048]{1,0:T(8,128)(2,1)S(1)}, bf16[136,2048]{1,0:T(8,128)(2,1)S(1)}, u32[]{:S(2)}, u32[]{:S(2)}) collective-permute-start(bf16[136,2048]{1,0:T(8,128)(2,1)S(1)} %pad_maximum_fusion.refs_3_.refs_0_.refs_1_), channel_id=1, source_target_pairs={{0,8},{1,9},{2,10},{3,11},{4,12},{5,13},{6,14},{7,15},{8,16},{9,17... | collective-permute-start | bytes 1671176 | tf_op jit(solution)/shard_map/ppermute | solution.py:43
  10.6 3.6 %load.2 = (bf16[704,2048]{1,0:T(8,128)(2,1)S(1)}, bf16[704,2048]{1,0:T(8,128)(2,1)S(1)}, bf16[704,2048]{1,0:T(8,128)(2,1)S(1)}) custom-call(bf16[704,2048]{1,0:T(8,128)(2,1)} %bitcast.13, bf16[704,2048]{1,0:T(8,128)(2,1)} %bitcast.15, bf16[704,2048]{1,0:T(8,128)(2,1)} %refs_2_.1, bf16[136,2048]{1,0:T(8,128)(2,1)S(1)} %pad_maximum_fusion.refs_3_.refs_0_.refs_1_), custom_call_target="tpu_custom_call" | custom-call | flops 4294967296 | tf_op jit(solution)/shard_map/load/pallas_call | solution.py:131
  14.2 1.7 %collective-permute-done.refs_1_.refs_2_ = bf16[136,2048]{1,0:T(8,128)(2,1)S(1)} collective-permute-done((bf16[136,2048]{1,0:T(8,128)(2,1)S(1)}, bf16[136,2048]{1,0:T(8,128)(2,1)S(1)}, u32[]{:S(2)}, u32[]{:S(2)}) %collective-permute-start) | collective-permute-done | bytes 557088 | tf_op jit(solution)/shard_map/ppermute | solution.py:43
  16.7 2.1 %collective-permute-start.1 = (bf16[144,2048]{1,0:T(8,128)(2,1)S(1)}, bf16[144,2048]{1,0:T(8,128)(2,1)S(1)}, u32[]{:S(2)}, u32[]{:S(2)}) collective-permute-start(bf16[144,2048]{1,0:T(8,128)(2,1)S(1)} %send_rows.4.refs_3_), channel_id=1, source_target_pairs={{0,4},{1,3},{2,6},{3,1},{4,0},{5,7},{6,2},{7,5},{8,12},{9,11},{10,... | collective-permute-start | bytes 1769480 | tf_op jit(solution)/shard_map/ppermute | solution.py:43
  18.8 6.1 %collective-permute-done.9.refs_0_.refs_1_ = bf16[136,2048]{1,0:T(8,128)(2,1)S(1)} collective-permute-done((bf16[136,2048]{1,0:T(8,128)(2,1)S(1)}, bf16[136,2048]{1,0:T(8,128)(2,1)S(1)}, u32[]{:S(2)}, u32[]{:S(2)}) %collective-permute-start.9) | collective-permute-done | bytes 557088 | tf_op jit(solution)/shard_map/ppermute | solution.py:43
  25.8 3.6 %load.3 = (bf16[704,2048]{1,0:T(8,128)(2,1)S(1)}, bf16[704,2048]{1,0:T(8,128)(2,1)S(1)}, bf16[704,2048]{1,0:T(8,128)(2,1)S(1)}) custom-call(bf16[704,2048]{1,0:T(8,128)(2,1)} %collective-permute-done.2.refs_0_, bf16[704,2048]{1,0:T(8,128)(2,1)} %collective-permute-done.3.refs_1_, bf16[704,2048]{1,0:T(8,128)(2,1)} %collective-permute-done.4.refs_2_, ...), custom_call_target="tpu_custom_call" | custom-call | flops 4294967296 | tf_op jit(solution)/shard_map/load/pallas_call | solution.py:131
  29.3 6.5 %experts.4 = (bf16[144,2048]{1,0:T(8,128)(2,1)S(1)}, bf16[144,2048]{1,0:T(8,128)(2,1)S(1)}) custom-call(s32[3]{0:T(128)S(1)} %get-tuple-element.53.slot_ref.refs_0_, bf16[136,2048]{1,0:T(8,128)(2,1)S(1)} %pad_maximum_fusion.refs_3_.refs_0_.refs_1_, bf16[136,2048]{1,0:T(8,128)(2,1)S(1)} %collective-permute-done.refs_1_.refs_2_, ...), custom_call_target="tpu_custom_call" | custom-call | flops 4982833152 | tf_op jit(solution)/shard_map/experts/pallas_call | solution.py:265
  38.0 2.6 %collective-permute-done.10.refs_0_.refs_1_ = bf16[136,2048]{1,0:T(8,128)(2,1)S(1)} collective-permute-done((bf16[136,2048]{1,0:T(8,128)(2,1)S(1)}, bf16[136,2048]{1,0:T(8,128)(2,1)S(1)}, u32[]{:S(2)}, u32[]{:S(2)}) %collective-permute-start.10) | collective-permute-done | bytes 557088 | tf_op jit(solution)/shard_map/ppermute | solution.py:43
  40.6 1.7 %collective-permute-start.13 = (bf16[136,2048]{1,0:T(8,128)(2,1)S(1)}, bf16[136,2048]{1,0:T(8,128)(2,1)S(1)}, u32[]{:S(2)}, u32[]{:S(2)}) collective-permute-start(bf16[136,2048]{1,0:T(8,128)(2,1)S(1)} %collective-permute-done.10.refs_0_.refs_1_), channel_id=1, source_target_pairs={{0,2},{1,5},{2,0},{3,7},{4,6},{5,1},{6,4},{7,3},{8,10},{9,13},{10,... | collective-permute-start | bytes 1671176 | tf_op jit(solution)/shard_map/ppermute | solution.py:43
  43.0 8.9 %collective-permute-done.15.refs_3_ = bf16[144,2048]{1,0:T(8,128)(2,1)S(1)} collective-permute-done((bf16[144,2048]{1,0:T(8,128)(2,1)S(1)}, bf16[144,2048]{1,0:T(8,128)(2,1)S(1)}, u32[]{:S(2)}, u32[]{:S(2)}) %collective-permute-start.15) | collective-permute-done | bytes 589856 | tf_op jit(solution)/shard_map/ppermute | solution.py:43
  51.9 6.5 %experts.5 = (bf16[144,2048]{1,0:T(8,128)(2,1)S(1)}, bf16[144,2048]{1,0:T(8,128)(2,1)S(1)}) custom-call(s32[3]{0:T(128)S(1)} %get-tuple-element.53.slot_ref.refs_0_, bf16[136,2048]{1,0:T(8,128)(2,1)S(1)} %collective-permute-done.9.refs_0_.refs_1_, bf16[136,2048]{1,0:T(8,128)(2,1)S(1)} %collective-permute-done.14.refs_1_.refs_2_, ...), custom_call_target="tpu_custom_call" | custom-call | flops 4982833152 | tf_op jit(solution)/shard_map/experts/pallas_call | solution.py:265
  59.1 2.3 %collective-permute-start.11 = (bf16[136,2048]{1,0:T(8,128)(2,1)S(1)}, bf16[136,2048]{1,0:T(8,128)(2,1)S(1)}, u32[]{:S(2)}, u32[]{:S(2)}) collective-permute-start(bf16[136,2048]{1,0:T(8,128)(2,1)S(1)} %collective-permute-done.10.refs_0_.refs_1_), channel_id=1, source_target_pairs={{0,8},{1,9},{2,10},{3,11},{4,12},{5,13},{6,14},{7,15},{8,16},{9,17... | collective-permute-start | bytes 1671176 | tf_op jit(solution)/shard_map/ppermute | solution.py:43
  63.9 2.0 %collective-permute-start.8 = (bf16[136,2048]{1,0:T(8,128)(2,1)S(1)}, bf16[136,2048]{1,0:T(8,128)(2,1)S(1)}, u32[]{:S(2)}, u32[]{:S(2)}) collective-permute-start(bf16[136,2048]{1,0:T(8,128)(2,1)S(1)} %broadcast_select_fusion.refs_1_), channel_id=1, source_target_pairs={{0,1},{1,0},{2,3},{3,2},{4,5},{5,4},{6,7},{7,6},{8,9},{9,8},{10,11... | collective-permute-start | bytes 1671176 | tf_op jit(solution)/shard_map/ppermute | solution.py:43
  65.9 5.0 %collective-permute-done.11.refs_0_.refs_1_ = bf16[136,2048]{1,0:T(8,128)(2,1)S(1)} collective-permute-done((bf16[136,2048]{1,0:T(8,128)(2,1)S(1)}, bf16[136,2048]{1,0:T(8,128)(2,1)S(1)}, u32[]{:S(2)}, u32[]{:S(2)}) %collective-permute-start.11) | collective-permute-done | bytes 557088 | tf_op jit(solution)/shard_map/ppermute | solution.py:43
  70.8 2.3 %collective-permute-start.12 = (bf16[136,2048]{1,0:T(8,128)(2,1)S(1)}, bf16[136,2048]{1,0:T(8,128)(2,1)S(1)}, u32[]{:S(2)}, u32[]{:S(2)}) collective-permute-start(bf16[136,2048]{1,0:T(8,128)(2,1)S(1)} %collective-permute-done.11.refs_0_.refs_1_), channel_id=1, source_target_pairs={{0,2},{1,5},{2,0},{3,7},{4,6},{5,1},{6,4},{7,3},{8,10},{9,13},{10,... | collective-permute-start | bytes 1671176 | tf_op jit(solution)/shard_map/ppermute | solution.py:43
  75.2 4.4 %collective-permute-done.16.refs_3_ = bf16[144,2048]{1,0:T(8,128)(2,1)S(1)} collective-permute-done((bf16[144,2048]{1,0:T(8,128)(2,1)S(1)}, bf16[144,2048]{1,0:T(8,128)(2,1)S(1)}, u32[]{:S(2)}, u32[]{:S(2)}) %collective-permute-start.16) | collective-permute-done | bytes 589856 | tf_op jit(solution)/shard_map/ppermute | solution.py:43
  79.6 1.8 %collective-permute-start.25 = (bf16[128,2048]{1,0:T(8,128)(2,1)S(1)}, bf16[128,2048]{1,0:T(8,128)(2,1)S(1)}, u32[]{:S(2)}, u32[]{:S(2)}) collective-permute-start(bf16[128,2048]{1,0:T(8,128)(2,1)S(1)} %get-tuple-element.52), channel_id=1, source_target_pairs={{0,2},{1,5},{2,0},{3,7},{4,6},{5,1},{6,4},{7,3},{8,10},{9,13},{10,... | collective-permute-start | bytes 1572872 | tf_op jit(solution)/shard_map/ppermute | solution.py:43
  81.4 6.5 %experts.6 = (bf16[144,2048]{1,0:T(8,128)(2,1)S(1)}, bf16[144,2048]{1,0:T(8,128)(2,1)S(1)}) custom-call(s32[3]{0:T(128)S(1)} %get-tuple-element.53.slot_ref.refs_0_, bf16[136,2048]{1,0:T(8,128)(2,1)S(1)} %collective-permute-done.10.refs_0_.refs_1_, bf16[136,2048]{1,0:T(8,128)(2,1)S(1)} %collective-permute-done.13.refs_1_.refs_2_, ...), custom_call_target="tpu_custom_call" | custom-call | flops 4982833152 | tf_op jit(solution)/shard_map/experts/pallas_call | solution.py:265
  88.9 2.1 %collective-permute-start.19 = (bf16[144,2048]{1,0:T(8,128)(2,1)S(1)}, bf16[144,2048]{1,0:T(8,128)(2,1)S(1)}, u32[]{:S(2)}, u32[]{:S(2)}) collective-permute-start(bf16[144,2048]{1,0:T(8,128)(2,1)S(1)} %send_rows.7.refs_7_), channel_id=1, source_target_pairs={{0,4},{1,3},{2,6},{3,1},{4,0},{5,7},{6,2},{7,5},{8,12},{9,11},{10,... | collective-permute-start | bytes 1769480 | tf_op jit(solution)/shard_map/ppermute | solution.py:43
  91.0 7.3 %shared.1 = (f32[256,2048]{1,0:T(8,128)S(1)}, bf16[256,2048]{1,0:T(8,128)(2,1)S(1)}) custom-call(bf16[136,2048]{1,0:T(8,128)(2,1)S(1)} %pad_maximum_fusion.refs_3_.refs_0_.refs_1_, bf16[136,2048]{1,0:T(8,128)(2,1)S(1)} %broadcast_select_fusion.refs_1_, bf16[136,2048]{1,0:T(8,128)(2,1)S(1)} %collective-permute-done.7.refs_2_, ...), custom_call_target="tpu_custom_call" | custom-call | flops 4429185024 | tf_op jit(solution)/shard_map/shared/pallas_call | solution.py:265
  98.5 3.5 %collective-permute-start.26 = (bf16[128,2048]{1,0:T(8,128)(2,1)S(1)}, bf16[128,2048]{1,0:T(8,128)(2,1)S(1)}, u32[]{:S(2)}, u32[]{:S(2)}) collective-permute-start(bf16[128,2048]{1,0:T(8,128)(2,1)S(1)} %add_convert_fusion.4), channel_id=1, source_target_pairs={{0,8},{1,9},{2,10},{3,11},{4,12},{5,13},{6,14},{7,15},{8,16},{9,17... | collective-permute-start | bytes 1572872 | tf_op jit(solution)/shard_map/ppermute | solution.py:43
  103.4 1.9 %collective-permute-done.19.refs_3_ = bf16[144,2048]{1,0:T(8,128)(2,1)S(1)} collective-permute-done((bf16[144,2048]{1,0:T(8,128)(2,1)S(1)}, bf16[144,2048]{1,0:T(8,128)(2,1)S(1)}, u32[]{:S(2)}, u32[]{:S(2)}) %collective-permute-start.19) | collective-permute-done | bytes 589856 | tf_op jit(solution)/shard_map/ppermute | solution.py:43
  105.3 6.5 %experts.7 = (bf16[144,2048]{1,0:T(8,128)(2,1)S(1)}, bf16[144,2048]{1,0:T(8,128)(2,1)S(1)}) custom-call(s32[3]{0:T(128)S(1)} %get-tuple-element.53.slot_ref.refs_0_, bf16[136,2048]{1,0:T(8,128)(2,1)S(1)} %collective-permute-done.11.refs_0_.refs_1_, bf16[136,2048]{1,0:T(8,128)(2,1)S(1)} %collective-permute-done.12.refs_1_.refs_2_, ...), custom_call_target="tpu_custom_call" | custom-call | flops 4982833152 | tf_op jit(solution)/shard_map/experts/pallas_call | solution.py:265
  113.8 5.0 %collective-permute-done.26 = bf16[128,2048]{1,0:T(8,128)(2,1)S(1)} collective-permute-done((bf16[128,2048]{1,0:T(8,128)(2,1)S(1)}, bf16[128,2048]{1,0:T(8,128)(2,1)S(1)}, u32[]{:S(2)}, u32[]{:S(2)}) %collective-permute-start.26) | collective-permute-done | bytes 524320 | tf_op jit(solution)/shard_map/ppermute | solution.py:43
  119.0 2.7 %collective-permute-done.22.refs_3_ = bf16[144,2048]{1,0:T(8,128)(2,1)S(1)} collective-permute-done((bf16[144,2048]{1,0:T(8,128)(2,1)S(1)}, bf16[144,2048]{1,0:T(8,128)(2,1)S(1)}, u32[]{:S(2)}, u32[]{:S(2)}) %collective-permute-start.22) | collective-permute-done | bytes 589856 | tf_op jit(solution)/shard_map/ppermute | solution.py:43
  123.8 1.4 collective-permute-start.21
  126.0 8.6 %collective-permute-done.27 = bf16[128,2048]{1,0:T(8,128)(2,1)S(1)} collective-permute-done((bf16[128,2048]{1,0:T(8,128)(2,1)S(1)}, bf16[128,2048]{1,0:T(8,128)(2,1)S(1)}, u32[]{:S(2)}, u32[]{:S(2)}) %collective-permute-start.27) | collective-permute-done | bytes 524320 | tf_op jit(solution)/shard_map/ppermute | solution.py:43
  134.5 1.9 %collective-permute-done.23 = bf16[128,2048]{1,0:T(8,128)(2,1)S(1)} collective-permute-done((bf16[128,2048]{1,0:T(8,128)(2,1)S(1)}, bf16[128,2048]{1,0:T(8,128)(2,1)S(1)}, u32[]{:S(2)}, u32[]{:S(2)}) %collective-permute-start.23) | collective-permute-done | bytes 524320 | tf_op jit(solution)/shard_map/ppermute | solution.py:43
  136.6 2.3 %collective-permute-start.28 = (bf16[128,2048]{1,0:T(8,128)(2,1)S(1)}, bf16[128,2048]{1,0:T(8,128)(2,1)S(1)}, u32[]{:S(2)}, u32[]{:S(2)}) collective-permute-start(bf16[128,2048]{1,0:T(8,128)(2,1)S(1)} %add_convert_fusion.2), channel_id=1, source_target_pairs={{0,8},{1,9},{2,10},{3,11},{4,12},{5,13},{6,14},{7,15},{8,16},{9,17... | collective-permute-start | bytes 1572872 | tf_op jit(solution)/shard_map/ppermute | solution.py:43
  138.9 4.6 %collective-permute-done.21 = bf16[128,2048]{1,0:T(8,128)(2,1)S(1)} collective-permute-done((bf16[128,2048]{1,0:T(8,128)(2,1)S(1)}, bf16[128,2048]{1,0:T(8,128)(2,1)S(1)}, u32[]{:S(2)}, u32[]{:S(2)}) %collective-permute-start.21) | collective-permute-done | bytes 524320 | tf_op jit(solution)/shard_map/ppermute | solution.py:43
  143.5 7.7 %collective-permute-done.28 = bf16[128,2048]{1,0:T(8,128)(2,1)S(1)} collective-permute-done((bf16[128,2048]{1,0:T(8,128)(2,1)S(1)}, bf16[128,2048]{1,0:T(8,128)(2,1)S(1)}, u32[]{:S(2)}, u32[]{:S(2)}) %collective-permute-start.28) | collective-permute-done | bytes 524320 | tf_op jit(solution)/shard_map/ppermute | solution.py:43
  (66 shorter events, 24.3 us)
Async XLA Ops:
  0.0 4.4 %copy-start = (bf16[2048,16]{0,1:T(8,128)(2,1)S(1)}, bf16[2048,16]{0,1:T(8,128)(2,1)}, u32[]{:S(2)}) copy-start(bf16[2048,16]{0,1:T(8,128)(2,1)} %param.17) | copy-start | bytes 196612
  0.0 25.5 %collective-permute-start.2 = (bf16[704,2048]{1,0:T(8,128)(2,1)}, bf16[704,2048]{1,0:T(8,128)(2,1)}, u32[]{:S(2)}, u32[]{:S(2)}) collective-permute-start(bf16[704,2048]{1,0:T(8,128)(2,1)} %bitcast.12), channel_id=1, source_target_pairs={{0,1},{1,0},{2,3},{3,2},{4,5},{5,4},{6,7},{7,6},{8,9},{9,8},{10,11... | collective-permute-start | bytes 8650760 | tf_op jit(solution)/shard_map/ppermute | solution.py:43
  0.5 25.3 %collective-permute-start.3 = (bf16[704,2048]{1,0:T(8,128)(2,1)}, bf16[704,2048]{1,0:T(8,128)(2,1)}, u32[]{:S(2)}, u32[]{:S(2)}) collective-permute-start(bf16[704,2048]{1,0:T(8,128)(2,1)} %bitcast.14), channel_id=1, source_target_pairs={{0,1},{1,0},{2,3},{3,2},{4,5},{5,4},{6,7},{7,6},{8,9},{9,8},{10,11... | collective-permute-start | bytes 8650760 | tf_op jit(solution)/shard_map/ppermute | solution.py:43
  0.6 25.2 %collective-permute-start.4 = (bf16[704,2048]{1,0:T(8,128)(2,1)}, bf16[704,2048]{1,0:T(8,128)(2,1)}, u32[]{:S(2)}, u32[]{:S(2)}) collective-permute-start(bf16[704,2048]{1,0:T(8,128)(2,1)} %refs_2_.1), channel_id=1, source_target_pairs={{0,1},{1,0},{2,3},{3,2},{4,5},{5,4},{6,7},{7,6},{8,9},{9,8},{10,11... | collective-permute-start | bytes 8650760 | tf_op jit(solution)/shard_map/ppermute | solution.py:43
  5.7 10.1 %collective-permute-start = (bf16[136,2048]{1,0:T(8,128)(2,1)S(1)}, bf16[136,2048]{1,0:T(8,128)(2,1)S(1)}, u32[]{:S(2)}, u32[]{:S(2)}) collective-permute-start(bf16[136,2048]{1,0:T(8,128)(2,1)S(1)} %pad_maximum_fusion.refs_3_.refs_0_.refs_1_), channel_id=1, source_target_pairs={{0,2},{1,5},{2,0},{3,7},{4,6},{5,1},{6,4},{7,3},{8,10},{9,13},{10,... | collective-permute-start | bytes 1671176 | tf_op jit(solution)/shard_map/ppermute | solution.py:43
  8.3 16.6 %collective-permute-start.9 = (bf16[136,2048]{1,0:T(8,128)(2,1)S(1)}, bf16[136,2048]{1,0:T(8,128)(2,1)S(1)}, u32[]{:S(2)}, u32[]{:S(2)}) collective-permute-start(bf16[136,2048]{1,0:T(8,128)(2,1)S(1)} %pad_maximum_fusion.refs_3_.refs_0_.refs_1_), channel_id=1, source_target_pairs={{0,8},{1,9},{2,10},{3,11},{4,12},{5,13},{6,14},{7,15},{8,16},{9,17... | collective-permute-start | bytes 1671176 | tf_op jit(solution)/shard_map/ppermute | solution.py:43
  16.7 12.6 %collective-permute-start.1 = (bf16[144,2048]{1,0:T(8,128)(2,1)S(1)}, bf16[144,2048]{1,0:T(8,128)(2,1)S(1)}, u32[]{:S(2)}, u32[]{:S(2)}) collective-permute-start(bf16[144,2048]{1,0:T(8,128)(2,1)S(1)} %send_rows.4.refs_3_), channel_id=1, source_target_pairs={{0,4},{1,3},{2,6},{3,1},{4,0},{5,7},{6,2},{7,5},{8,12},{9,11},{10,... | collective-permute-start | bytes 1769480 | tf_op jit(solution)/shard_map/ppermute | solution.py:43
  24.9 11.0 %collective-permute-start.14 = (bf16[136,2048]{1,0:T(8,128)(2,1)S(1)}, bf16[136,2048]{1,0:T(8,128)(2,1)S(1)}, u32[]{:S(2)}, u32[]{:S(2)}) collective-permute-start(bf16[136,2048]{1,0:T(8,128)(2,1)S(1)} %collective-permute-done.9.refs_0_.refs_1_), channel_id=1, source_target_pairs={{0,2},{1,5},{2,0},{3,7},{4,6},{5,1},{6,4},{7,3},{8,10},{9,13},{10,... | collective-permute-start | bytes 1671176 | tf_op jit(solution)/shard_map/ppermute | solution.py:43
  25.5 15.1 %collective-permute-start.10 = (bf16[136,2048]{1,0:T(8,128)(2,1)S(1)}, bf16[136,2048]{1,0:T(8,128)(2,1)S(1)}, u32[]{:S(2)}, u32[]{:S(2)}) collective-permute-start(bf16[136,2048]{1,0:T(8,128)(2,1)S(1)} %collective-permute-done.9.refs_0_.refs_1_), channel_id=1, source_target_pairs={{0,8},{1,9},{2,10},{3,11},{4,12},{5,13},{6,14},{7,15},{8,16},{9,17... | collective-permute-start | bytes 1671176 | tf_op jit(solution)/shard_map/ppermute | solution.py:43
  36.8 15.2 %collective-permute-start.15 = (bf16[144,2048]{1,0:T(8,128)(2,1)S(1)}, bf16[144,2048]{1,0:T(8,128)(2,1)S(1)}, u32[]{:S(2)}, u32[]{:S(2)}) collective-permute-start(bf16[144,2048]{1,0:T(8,128)(2,1)S(1)} %send_rows.5.refs_10_), channel_id=1, source_target_pairs={{0,4},{1,3},{2,6},{3,1},{4,0},{5,7},{6,2},{7,5},{8,12},{9,11},{10,... | collective-permute-start | bytes 1769480 | tf_op jit(solution)/shard_map/ppermute | solution.py:43
  40.6 22.0 %collective-permute-start.13 = (bf16[136,2048]{1,0:T(8,128)(2,1)S(1)}, bf16[136,2048]{1,0:T(8,128)(2,1)S(1)}, u32[]{:S(2)}, u32[]{:S(2)}) collective-permute-start(bf16[136,2048]{1,0:T(8,128)(2,1)S(1)} %collective-permute-done.10.refs_0_.refs_1_), channel_id=1, source_target_pairs={{0,2},{1,5},{2,0},{3,7},{4,6},{5,1},{6,4},{7,3},{8,10},{9,13},{10,... | collective-permute-start | bytes 1671176 | tf_op jit(solution)/shard_map/ppermute | solution.py:43
  42.3 21.6 %collective-permute-start.6 = (bf16[136,2048]{1,0:T(8,128)(2,1)S(1)}, bf16[136,2048]{1,0:T(8,128)(2,1)S(1)}, u32[]{:S(2)}, u32[]{:S(2)}) collective-permute-start(bf16[136,2048]{1,0:T(8,128)(2,1)S(1)} %pad_maximum_fusion.refs_3_.refs_0_.refs_1_), channel_id=1, source_target_pairs={{1,3},{3,1},{5,7},{7,5},{9,11},{11,9},{13,15},{15,13},{17,19},{19,... | collective-permute-start | bytes 1671176 | tf_op jit(solution)/shard_map/ppermute | solution.py:43
  58.4 14.7 %collective-permute-start.17 = (bf16[144,2048]{1,0:T(8,128)(2,1)S(1)}, bf16[144,2048]{1,0:T(8,128)(2,1)S(1)}, u32[]{:S(2)}, u32[]{:S(2)}) collective-permute-start(bf16[144,2048]{1,0:T(8,128)(2,1)S(1)} %get-tuple-element.38), channel_id=1, source_target_pairs={{0,4},{1,3},{2,6},{3,1},{4,0},{5,7},{6,2},{7,5},{8,12},{9,11},{10,... | collective-permute-start | bytes 1769480 | tf_op jit(solution)/shard_map/ppermute | solution.py:43
  59.1 11.7 %collective-permute-start.11 = (bf16[136,2048]{1,0:T(8,128)(2,1)S(1)}, bf16[136,2048]{1,0:T(8,128)(2,1)S(1)}, u32[]{:S(2)}, u32[]{:S(2)}) collective-permute-start(bf16[136,2048]{1,0:T(8,128)(2,1)S(1)} %collective-permute-done.10.refs_0_.refs_1_), channel_id=1, source_target_pairs={{0,8},{1,9},{2,10},{3,11},{4,12},{5,13},{6,14},{7,15},{8,16},{9,17... | collective-permute-start | bytes 1671176 | tf_op jit(solution)/shard_map/ppermute | solution.py:43
  61.4 27.6 %collective-permute-start.7 = (bf16[136,2048]{1,0:T(8,128)(2,1)S(1)}, bf16[136,2048]{1,0:T(8,128)(2,1)S(1)}, u32[]{:S(2)}, u32[]{:S(2)}) collective-permute-start(bf16[136,2048]{1,0:T(8,128)(2,1)S(1)} %pad_maximum_fusion.refs_3_.refs_0_.refs_1_), channel_id=1, source_target_pairs={{0,1},{1,0},{2,3},{3,2},{4,5},{5,4},{6,7},{7,6},{8,9},{9,8},{10,11... | collective-permute-start | bytes 1671176 | tf_op jit(solution)/shard_map/ppermute | solution.py:43
  63.5 16.1 %collective-permute-start.16 = (bf16[144,2048]{1,0:T(8,128)(2,1)S(1)}, bf16[144,2048]{1,0:T(8,128)(2,1)S(1)}, u32[]{:S(2)}, u32[]{:S(2)}) collective-permute-start(bf16[144,2048]{1,0:T(8,128)(2,1)S(1)} %send_rows.6.refs_4_), channel_id=1, source_target_pairs={{0,4},{1,3},{2,6},{3,1},{4,0},{5,7},{6,2},{7,5},{8,12},{9,11},{10,... | collective-permute-start | bytes 1769480 | tf_op jit(solution)/shard_map/ppermute | solution.py:43
  63.9 27.1 %collective-permute-start.8 = (bf16[136,2048]{1,0:T(8,128)(2,1)S(1)}, bf16[136,2048]{1,0:T(8,128)(2,1)S(1)}, u32[]{:S(2)}, u32[]{:S(2)}) collective-permute-start(bf16[136,2048]{1,0:T(8,128)(2,1)S(1)} %broadcast_select_fusion.refs_1_), channel_id=1, source_target_pairs={{0,1},{1,0},{2,3},{3,2},{4,5},{5,4},{6,7},{7,6},{8,9},{9,8},{10,11... | collective-permute-start | bytes 1671176 | tf_op jit(solution)/shard_map/ppermute | solution.py:43
  70.8 17.1 %collective-permute-start.12 = (bf16[136,2048]{1,0:T(8,128)(2,1)S(1)}, bf16[136,2048]{1,0:T(8,128)(2,1)S(1)}, u32[]{:S(2)}, u32[]{:S(2)}) collective-permute-start(bf16[136,2048]{1,0:T(8,128)(2,1)S(1)} %collective-permute-done.11.refs_0_.refs_1_), channel_id=1, source_target_pairs={{0,2},{1,5},{2,0},{3,7},{4,6},{5,1},{6,4},{7,3},{8,10},{9,13},{10,... | collective-permute-start | bytes 1671176 | tf_op jit(solution)/shard_map/ppermute | solution.py:43
  73.1 39.3 %collective-permute-start.5 = (bf16[144,2048]{1,0:T(8,128)(2,1)S(1)}, bf16[144,2048]{1,0:T(8,128)(2,1)S(1)}, u32[]{:S(2)}, u32[]{:S(2)}) collective-permute-start(bf16[144,2048]{1,0:T(8,128)(2,1)S(1)} %get-tuple-element.36), channel_id=1, source_target_pairs={{0,4},{1,3},{2,6},{3,1},{4,0},{5,7},{6,2},{7,5},{8,12},{9,11},{10,... | collective-permute-start | bytes 1769480 | tf_op jit(solution)/shard_map/ppermute | solution.py:43
  79.6 18.8 %collective-permute-start.25 = (bf16[128,2048]{1,0:T(8,128)(2,1)S(1)}, bf16[128,2048]{1,0:T(8,128)(2,1)S(1)}, u32[]{:S(2)}, u32[]{:S(2)}) collective-permute-start(bf16[128,2048]{1,0:T(8,128)(2,1)S(1)} %get-tuple-element.52), channel_id=1, source_target_pairs={{0,2},{1,5},{2,0},{3,7},{4,6},{5,1},{6,4},{7,3},{8,10},{9,13},{10,... | collective-permute-start | bytes 1572872 | tf_op jit(solution)/shard_map/ppermute | solution.py:43
  88.0 14.0 %collective-permute-start.20 = (bf16[144,2048]{1,0:T(8,128)(2,1)S(1)}, bf16[144,2048]{1,0:T(8,128)(2,1)S(1)}, u32[]{:S(2)}, u32[]{:S(2)}) collective-permute-start(bf16[144,2048]{1,0:T(8,128)(2,1)S(1)} %get-tuple-element.43), channel_id=1, source_target_pairs={{0,4},{1,3},{2,6},{3,1},{4,0},{5,7},{6,2},{7,5},{8,12},{9,11},{10,... | collective-permute-start | bytes 1769480 | tf_op jit(solution)/shard_map/ppermute | solution.py:43
  88.9 16.3 %collective-permute-start.19 = (bf16[144,2048]{1,0:T(8,128)(2,1)S(1)}, bf16[144,2048]{1,0:T(8,128)(2,1)S(1)}, u32[]{:S(2)}, u32[]{:S(2)}) collective-permute-start(bf16[144,2048]{1,0:T(8,128)(2,1)S(1)} %send_rows.7.refs_7_), channel_id=1, source_target_pairs={{0,4},{1,3},{2,6},{3,1},{4,0},{5,7},{6,2},{7,5},{8,12},{9,11},{10,... | collective-permute-start | bytes 1769480 | tf_op jit(solution)/shard_map/ppermute | solution.py:43
  98.3 14.1 %collective-permute-start.18 = (bf16[256,2048]{1,0:T(8,128)(2,1)S(1)}, bf16[256,2048]{1,0:T(8,128)(2,1)S(1)}, u32[]{:S(2)}, u32[]{:S(2)}) collective-permute-start(bf16[256,2048]{1,0:T(8,128)(2,1)S(1)} %get-tuple-element.42), channel_id=1, source_target_pairs={{0,1},{1,0},{2,3},{3,2},{4,5},{5,4},{6,7},{7,6},{8,9},{9,8},{10,11... | collective-permute-start | bytes 3145736 | tf_op jit(solution)/shard_map/ppermute | solution.py:43
  98.5 20.2 %collective-permute-start.26 = (bf16[128,2048]{1,0:T(8,128)(2,1)S(1)}, bf16[128,2048]{1,0:T(8,128)(2,1)S(1)}, u32[]{:S(2)}, u32[]{:S(2)}) collective-permute-start(bf16[128,2048]{1,0:T(8,128)(2,1)S(1)} %add_convert_fusion.4), channel_id=1, source_target_pairs={{0,8},{1,9},{2,10},{3,11},{4,12},{5,13},{6,14},{7,15},{8,16},{9,17... | collective-permute-start | bytes 1572872 | tf_op jit(solution)/shard_map/ppermute | solution.py:43
  103.3 15.4 %collective-permute-start.24 = (bf16[128,2048]{1,0:T(8,128)(2,1)S(1)}, bf16[128,2048]{1,0:T(8,128)(2,1)S(1)}, u32[]{:S(2)}, u32[]{:S(2)}) collective-permute-start(bf16[128,2048]{1,0:T(8,128)(2,1)S(1)} %get-tuple-element.51), channel_id=1, source_target_pairs={{0,2},{1,5},{2,0},{3,7},{4,6},{5,1},{6,4},{7,3},{8,10},{9,13},{10,... | collective-permute-start | bytes 1572872 | tf_op jit(solution)/shard_map/ppermute | solution.py:43
  111.8 9.9 %collective-permute-start.22 = (bf16[144,2048]{1,0:T(8,128)(2,1)S(1)}, bf16[144,2048]{1,0:T(8,128)(2,1)S(1)}, u32[]{:S(2)}, u32[]{:S(2)}) collective-permute-start(bf16[144,2048]{1,0:T(8,128)(2,1)S(1)} %get-tuple-element.48), channel_id=1, source_target_pairs={{0,4},{1,3},{2,6},{3,1},{4,0},{5,7},{6,2},{7,5},{8,12},{9,11},{10,... | collective-permute-start | bytes 1769480 | tf_op jit(solution)/shard_map/ppermute | solution.py:43
  119.0 15.6 %collective-permute-start.27 = (bf16[128,2048]{1,0:T(8,128)(2,1)S(1)}, bf16[128,2048]{1,0:T(8,128)(2,1)S(1)}, u32[]{:S(2)}, u32[]{:S(2)}) collective-permute-start(bf16[128,2048]{1,0:T(8,128)(2,1)S(1)} %add_convert_fusion.3), channel_id=1, source_target_pairs={{0,8},{1,9},{2,10},{3,11},{4,12},{5,13},{6,14},{7,15},{8,16},{9,17... | collective-permute-start | bytes 1572872 | tf_op jit(solution)/shard_map/ppermute | solution.py:43
  123.0 13.4 %collective-permute-start.23 = (bf16[128,2048]{1,0:T(8,128)(2,1)S(1)}, bf16[128,2048]{1,0:T(8,128)(2,1)S(1)}, u32[]{:S(2)}, u32[]{:S(2)}) collective-permute-start(bf16[128,2048]{1,0:T(8,128)(2,1)S(1)} %get-tuple-element.50), channel_id=1, source_target_pairs={{0,2},{1,5},{2,0},{3,7},{4,6},{5,1},{6,4},{7,3},{8,10},{9,13},{10,... | collective-permute-start | bytes 1572872 | tf_op jit(solution)/shard_map/ppermute | solution.py:43
  123.8 19.7 %collective-permute-start.21 = (bf16[128,2048]{1,0:T(8,128)(2,1)S(1)}, bf16[128,2048]{1,0:T(8,128)(2,1)S(1)}, u32[]{:S(2)}, u32[]{:S(2)}) collective-permute-start(bf16[128,2048]{1,0:T(8,128)(2,1)S(1)} %get-tuple-element.47), channel_id=1, source_target_pairs={{0,2},{1,5},{2,0},{3,7},{4,6},{5,1},{6,4},{7,3},{8,10},{9,13},{10,... | collective-permute-start | bytes 1572872 | tf_op jit(solution)/shard_map/ppermute | solution.py:43
  125.3 18.3 %collective-permute-start.29 = (bf16[128,2048]{1,0:T(8,128)(2,1)S(1)}, bf16[128,2048]{1,0:T(8,128)(2,1)S(1)}, u32[]{:S(2)}, u32[]{:S(2)}) collective-permute-start(bf16[128,2048]{1,0:T(8,128)(2,1)S(1)} %add_convert_fusion.1), channel_id=1, source_target_pairs={{1,3},{3,1},{5,7},{7,5},{9,11},{11,9},{13,15},{15,13},{17,19},{19,... | collective-permute-start | bytes 1572872 | tf_op jit(solution)/shard_map/ppermute | solution.py:43
  136.4 15.9 %copy-start.1 = (bf16[2048,16]{0,1:T(8,128)(2,1)S(1)}, bf16[2048,16]{0,1:T(8,128)(2,1)}, u32[]{:S(2)}) copy-start(bf16[2048,16]{0,1:T(8,128)(2,1)} %param.17) | copy-start | bytes 196612
  136.6 14.6 %collective-permute-start.28 = (bf16[128,2048]{1,0:T(8,128)(2,1)S(1)}, bf16[128,2048]{1,0:T(8,128)(2,1)S(1)}, u32[]{:S(2)}, u32[]{:S(2)}) collective-permute-start(bf16[128,2048]{1,0:T(8,128)(2,1)S(1)} %add_convert_fusion.2), channel_id=1, source_target_pairs={{0,8},{1,9},{2,10},{3,11},{4,12},{5,13},{6,14},{7,15},{8,16},{9,17... | collective-permute-start | bytes 1572872 | tf_op jit(solution)/shard_map/ppermute | solution.py:43

commit v3 on v0

--- a/solution.py
+++ b/solution.py
@@ -15,7 +15,7 @@
 STRIP = 8
 UNUSED = -4096.0
 PIECE = 256
-LIMIT = 16 << 20
+LIMIT = 10 << 20
 
 
 def places(dims):
@@ -348,9 +348,6 @@
         own.append(shift(own[-1], dims, "z", 1))
 
     last = own[:1]
-    loaded = load([w for weights in expert_slices for w in weights], last)
-    expert_slices = [loaded[i : i + 3] for i in range(0, len(loaded), 3)]
-    last = loaded[-1:]
     blocks, chosen, came, results, parts = {}, {}, {}, {}, {}
     firsts = [[o[0] for o in order] for order in orders]
     seconds = [[o[1] for o in order] for order in orders]
@@ -373,10 +370,8 @@
         )
         last = results[step][:1]
 
-    def give(step, held=None):
+    def give(step):
         own_rows, *rest = results[step]
-        if held is not None:
-            rest = lax.optimization_barrier((*rest, results[held][0]))[:-1]
         results[step] = [own_rows] + [
             shift(r, dims, seconds[step], -d - 1) for d, r in enumerate(rest)
         ]
@@ -389,33 +384,40 @@
             shift(r, dims, firsts[step], -d - 1) for d, r in enumerate(out[1:])
         ]
 
+    def spread():
+        nonlocal last, shared
+        peers = [shift(b, dims, "c", d) for d in range(1, cores) for b in blocks[0]]
+        shared = feed_forward(
+            blocks[0], peers, [[shared_gate.T, shared_up.T, shared_down]], None, shape, last
+        )
+        last = shared[:1]
+        shared = shared[:1] + [shift(r, dims, "c", -d - 1) for d, r in enumerate(shared[1:])]
+
+    shared = []
     later = list(range(1, steps))
-    send(0)
-    peers = [shift(b, dims, "c", d) for d in range(1, cores) for b in blocks[0]]
-    shared = feed_forward(
-        blocks[0], peers, [[shared_gate.T, shared_up.T, shared_down]], None, shape, last
-    )
-    last = shared[:1]
-    shared = shared[:1] + [shift(r, dims, "c", -d - 1) for d, r in enumerate(shared[1:])]
+    for step in [0] + later[:1]:
+        send(step)
+    loaded = load([w for weights in expert_slices for w in weights], last)
+    expert_slices = [loaded[i : i + 3] for i in range(0, len(loaded), 3)]
+    last = loaded[-1:]
+    spread()
+    for step in later[1:2]:
+        send(step)
+    for step in later[:1] + [0]:
+        run(step)
     for step in later[:1]:
+        give(step)
+    for step in later[2:]:
         send(step)
-    run(0)
-    for n, step in enumerate(later):
-        if n + 1 < len(later):
-            send(later[n + 1])
-        if n > 1:
-            join(later[n - 2])
+    for step in later[:1]:
+        join(step)
+    for step in later[1:]:
         run(step)
         give(step)
-        if n == 0:
-            give(0, step)
-    for step in later[-2:-1]:
+    give(0)
+    for step in later[1:]:
         join(step)
-    if not later:
-        give(0)
     join(0, shared)
-    for step in later[-1:]:
-        join(step)
 
     passed = []
     for step in later + [0]:

time: 171 us -> 159 us (0.930)
  waiting for transfers between devices: 92.3 us -> 80.1 us
    ppermute x28, waiting for transfers between devices: 92.3 us -> 80.1 us  [shift(): return lax.ppermute(block, AXES, route)]
  transfers between devices with their start and end apart: 28 -> 28, of which waited for: 11 -> 11; matrix products, arithmetic and copies ran while one was open for 4% -> 4% of each run, Pallas kernels for 28% -> 31%
where the time goes in v3:
time: 159 us; the launch traced here: 158 us
  waiting for transfers between devices  80.1 us (50%)
  Pallas kernels  48.4 us (30%)
  starting transfers between devices  22.1 us (14%)
  other arithmetic  4.84 us (3%)
    ppermute x28, waiting for transfers between devices, shift(): return lax.ppermute(block, AXES, route)  80.1 us
    pallas_call x5, Pallas kernels, feed_forward(): return list(call(*operands, *kept(blocks), *kept(came), *weights, *after))  33.6 us
    ppermute x28, starting transfers between devices, shift(): return lax.ppermute(block, AXES, route)  22.1 us
    pallas_call x1, Pallas kernels, load(): return list(call(*kept(arrays, pltpu.HBM), *after))  6.05 us
    pallas_call x4, Pallas kernels, combine(): return list(call(chosen, *kept(blocks), *kept(back), *kept(extra), *after))  5.29 us
    pallas_call x4, Pallas kernels, send_rows(): return list(call(chosen, *kept(blocks), *after))  3.49 us
  transfers between devices with their start and end apart: 28, of which 11 were waited for; matrix products, arithmetic and copies ran while one was open for 4% of the time, Pallas kernels for 31%

profile of v3, /device:TPU:0, one launch (start us, length us, event | category | flops | bytes accessed | tf_op | source)
XLA Modules:
  0.0 158.3 jit_solution(2986170171367142645)
XLA Ops:
  3.2 1.2 fusion.9
  5.7 2.7 %collective-permute-start.5 = (bf16[136,2048]{1,0:T(8,128)(2,1)S(1)}, bf16[136,2048]{1,0:T(8,128)(2,1)S(1)}, u32[]{:S(2)}, u32[]{:S(2)}) collective-permute-start(bf16[136,2048]{1,0:T(8,128)(2,1)S(1)} %pad_maximum_fusion.refs_0_.refs_2_.refs_1_), channel_id=1, source_target_pairs={{0,8},{1,9},{2,10},{3,11},{4,12},{5,13},{6,14},{7,15},{8,16},{9,17... | collective-permute-start | bytes 1671176 | tf_op jit(solution)/shard_map/ppermute | solution.py:39
  8.4 1.5 collective-permute-start
  9.9 13.8 %collective-permute-done.5.refs_0_.refs_1_ = bf16[136,2048]{1,0:T(8,128)(2,1)S(1)} collective-permute-done((bf16[136,2048]{1,0:T(8,128)(2,1)S(1)}, bf16[136,2048]{1,0:T(8,128)(2,1)S(1)}, u32[]{:S(2)}, u32[]{:S(2)}) %collective-permute-start.5) | collective-permute-done | bytes 557088 | tf_op jit(solution)/shard_map/ppermute | solution.py:39
  23.6 1.5 collective-permute-start.6
  25.8 7.3 %collective-permute-done.6.refs_1_.refs_2_ = bf16[136,2048]{1,0:T(8,128)(2,1)S(1)} collective-permute-done((bf16[136,2048]{1,0:T(8,128)(2,1)S(1)}, bf16[136,2048]{1,0:T(8,128)(2,1)S(1)}, u32[]{:S(2)}, u32[]{:S(2)}) %collective-permute-start.6) | collective-permute-done | bytes 557088 | tf_op jit(solution)/shard_map/ppermute | solution.py:39
  33.2 7.7 %collective-permute-done.8.refs_0_.refs_1_ = bf16[136,2048]{1,0:T(8,128)(2,1)S(1)} collective-permute-done((bf16[136,2048]{1,0:T(8,128)(2,1)S(1)}, bf16[136,2048]{1,0:T(8,128)(2,1)S(1)}, u32[]{:S(2)}, u32[]{:S(2)}) %collective-permute-start.8) | collective-permute-done | bytes 557088 | tf_op jit(solution)/shard_map/ppermute | solution.py:39
  44.1 1.3 collective-permute-start.9
  45.4 6.0 %load.1 = (bf16[704,2048]{1,0:T(8,128)(2,1)S(1)}, bf16[704,2048]{1,0:T(8,128)(2,1)S(1)}, bf16[704,2048]{1,0:T(8,128)(2,1)S(1)}, bf16[704,2048]{1,0:T(8,128)(2,1)...) custom-call(bf16[704,2048]{1,0:T(8,128)(2,1)} %bitcast.13, bf16[704,2048]{1,0:T(8,128)(2,1)} %bitcast.15, ...), custom_call_target="tpu_custom_call" | custom-call | flops 4294967296 | tf_op jit(solution)/shard_map/load/pallas_call | solution.py:124
  51.5 1.6 %collective-permute-start.1 = (bf16[144,2048]{1,0:T(8,128)(2,1)S(1)}, bf16[144,2048]{1,0:T(8,128)(2,1)S(1)}, u32[]{:S(2)}, u32[]{:S(2)}) collective-permute-start(bf16[144,2048]{1,0:T(8,128)(2,1)S(1)} %send_rows.4.refs_2_), channel_id=1, source_target_pairs={{0,4},{1,5},{2,6},{3,7},{4,0},{5,1},{6,2},{7,3},{8,12},{9,13},{10,... | collective-permute-start | bytes 1769480 | tf_op jit(solution)/shard_map/ppermute | solution.py:39
  53.1 4.6 %collective-permute-done.14.refs_0_.refs_1_ = bf16[136,2048]{1,0:T(8,128)(2,1)S(1)} collective-permute-done((bf16[136,2048]{1,0:T(8,128)(2,1)S(1)}, bf16[136,2048]{1,0:T(8,128)(2,1)S(1)}, u32[]{:S(2)}, u32[]{:S(2)}) %collective-permute-start.14) | collective-permute-done | bytes 557088 | tf_op jit(solution)/shard_map/ppermute | solution.py:39
  57.7 1.5 collective-permute-start.15
  59.2 7.3 %shared.1 = (f32[256,2048]{1,0:T(8,128)S(1)}, bf16[256,2048]{1,0:T(8,128)(2,1)S(1)}) custom-call(bf16[136,2048]{1,0:T(8,128)(2,1)S(1)} %pad_maximum_fusion.refs_0_.refs_2_.refs_1_, bf16[136,2048]{1,0:T(8,128)(2,1)S(1)} %collective-permute-done.refs_1_.refs_2_, bf16[136,2048]{1,0:T(8,128)(2,1)S(1)} %collective-permute-done.10.refs_2_, ...), custom_call_target="tpu_custom_call" | custom-call | flops 4429185024 | tf_op jit(solution)/shard_map/shared/pallas_call | solution.py:258
  67.4 6.5 %experts.4 = (bf16[144,2048]{1,0:T(8,128)(2,1)S(1)}, bf16[144,2048]{1,0:T(8,128)(2,1)S(1)}) custom-call(s32[2]{0:T(128)S(1)} %dynamic-slice_bitcast_fusion.slot_ref.refs_0_, bf16[136,2048]{1,0:T(8,128)(2,1)S(1)} %collective-permute-done.5.refs_0_.refs_1_, bf16[136,2048]{1,0:T(8,128)(2,1)S(1)} %collective-permute-done.6.refs_1_.refs_2_, ...), custom_call_target="tpu_custom_call" | custom-call | flops 4982833152 | tf_op jit(solution)/shard_map/experts/pallas_call | solution.py:258
  74.5 1.5 collective-permute-start.17
  76.0 6.7 %experts.5 = (bf16[144,2048]{1,0:T(8,128)(2,1)S(1)}, bf16[144,2048]{1,0:T(8,128)(2,1)S(1)}) custom-call(s32[2]{0:T(128)S(1)} %dynamic-slice_bitcast_fusion.1.slot_ref.refs_0_, bf16[136,2048]{1,0:T(8,128)(2,1)S(1)} %pad_maximum_fusion.refs_0_.refs_2_.refs_1_, bf16[136,2048]{1,0:T(8,128)(2,1)S(1)} %collective-permute-done.refs_1_.refs_2_, ...), custom_call_target="tpu_custom_call" | custom-call | flops 4982833152 | tf_op jit(solution)/shard_map/experts/pallas_call | solution.py:258
  84.2 1.3 combine.4
  85.5 1.3 collective-permute-start.24
  86.8 7.4 %collective-permute-done.17.refs_3_ = bf16[144,2048]{1,0:T(8,128)(2,1)S(1)} collective-permute-done((bf16[144,2048]{1,0:T(8,128)(2,1)S(1)}, bf16[144,2048]{1,0:T(8,128)(2,1)S(1)}, u32[]{:S(2)}, u32[]{:S(2)}) %collective-permute-start.17) | collective-permute-done | bytes 589856 | tf_op jit(solution)/shard_map/ppermute | solution.py:39
  94.3 6.5 %experts.6 = (bf16[144,2048]{1,0:T(8,128)(2,1)S(1)}, bf16[144,2048]{1,0:T(8,128)(2,1)S(1)}) custom-call(s32[2]{0:T(128)S(1)} %dynamic-slice_bitcast_fusion.slot_ref.refs_0_, bf16[136,2048]{1,0:T(8,128)(2,1)S(1)} %collective-permute-done.8.refs_0_.refs_1_, bf16[136,2048]{1,0:T(8,128)(2,1)S(1)} %collective-permute-done.9.refs_1_.refs_2_, ...), custom_call_target="tpu_custom_call" | custom-call | flops 4982833152 | tf_op jit(solution)/shard_map/experts/pallas_call | solution.py:258
  100.9 1.6 collective-permute-done.16.refs_3_
  102.4 6.5 %experts.7 = (bf16[144,2048]{1,0:T(8,128)(2,1)S(1)}, bf16[144,2048]{1,0:T(8,128)(2,1)S(1)}) custom-call(s32[2]{0:T(128)S(1)} %dynamic-slice_bitcast_fusion.slot_ref.refs_0_, bf16[136,2048]{1,0:T(8,128)(2,1)S(1)} %collective-permute-done.14.refs_0_.refs_1_, bf16[136,2048]{1,0:T(8,128)(2,1)S(1)} %collective-permute-done.15.refs_1_.refs_2_, ...), custom_call_target="tpu_custom_call" | custom-call | flops 4982833152 | tf_op jit(solution)/shard_map/experts/pallas_call | solution.py:258
  110.8 1.3 combine.5
  112.1 2.4 %collective-permute-start.23 = (bf16[128,2048]{1,0:T(8,128)(2,1)S(1)}, bf16[128,2048]{1,0:T(8,128)(2,1)S(1)}, u32[]{:S(2)}, u32[]{:S(2)}) collective-permute-start(bf16[128,2048]{1,0:T(8,128)(2,1)S(1)} %get-tuple-element.51), channel_id=1, source_target_pairs={{0,2},{1,5},{2,0},{3,7},{4,6},{5,1},{6,4},{7,3},{8,10},{9,13},{10,... | collective-permute-start | bytes 1572872 | tf_op jit(solution)/shard_map/ppermute | solution.py:39
  114.5 10.7 %collective-permute-done.19.refs_3_ = bf16[144,2048]{1,0:T(8,128)(2,1)S(1)} collective-permute-done((bf16[144,2048]{1,0:T(8,128)(2,1)S(1)}, bf16[144,2048]{1,0:T(8,128)(2,1)S(1)}, u32[]{:S(2)}, u32[]{:S(2)}) %collective-permute-start.19) | collective-permute-done | bytes 589856 | tf_op jit(solution)/shard_map/ppermute | solution.py:39
  125.2 1.3 combine.6
  126.5 1.3 collective-permute-start.22
  128.2 9.6 %collective-permute-done.12.refs_3_ = bf16[144,2048]{1,0:T(8,128)(2,1)S(1)} collective-permute-done((bf16[144,2048]{1,0:T(8,128)(2,1)S(1)}, bf16[144,2048]{1,0:T(8,128)(2,1)S(1)}, u32[]{:S(2)}, u32[]{:S(2)}) %collective-permute-start.12) | collective-permute-done | bytes 589856 | tf_op jit(solution)/shard_map/ppermute | solution.py:39
  137.9 1.4 combine.7
  139.2 1.3 collective-permute-start.21
  140.9 8.9 %collective-permute-done.21 = bf16[128,2048]{1,0:T(8,128)(2,1)S(1)} collective-permute-done((bf16[128,2048]{1,0:T(8,128)(2,1)S(1)}, bf16[128,2048]{1,0:T(8,128)(2,1)S(1)}, u32[]{:S(2)}, u32[]{:S(2)}) %collective-permute-start.21) | collective-permute-done | bytes 524320 | tf_op jit(solution)/shard_map/ppermute | solution.py:39
  149.8 7.5 %collective-permute-done.27 = bf16[128,2048]{1,0:T(8,128)(2,1)S(1)} collective-permute-done((bf16[128,2048]{1,0:T(8,128)(2,1)S(1)}, bf16[128,2048]{1,0:T(8,128)(2,1)S(1)}, u32[]{:S(2)}, u32[]{:S(2)}) %collective-permute-start.27) | collective-permute-done | bytes 524320 | tf_op jit(solution)/shard_map/ppermute | solution.py:39
  (59 shorter events, 14.7 us)
Async XLA Ops:
  0.0 4.4 %copy-start = (bf16[2048,16]{0,1:T(8,128)(2,1)S(1)}, bf16[2048,16]{0,1:T(8,128)(2,1)}, u32[]{:S(2)}) copy-start(bf16[2048,16]{0,1:T(8,128)(2,1)} %param.17) | copy-start | bytes 196612
  0.0 40.9 %collective-permute-start.2 = (bf16[704,2048]{1,0:T(8,128)(2,1)}, bf16[704,2048]{1,0:T(8,128)(2,1)}, u32[]{:S(2)}, u32[]{:S(2)}) collective-permute-start(bf16[704,2048]{1,0:T(8,128)(2,1)} %bitcast.12), channel_id=1, source_target_pairs={{0,1},{1,0},{2,3},{3,2},{4,5},{5,4},{6,7},{7,6},{8,9},{9,8},{10,11... | collective-permute-start | bytes 8650760 | tf_op jit(solution)/shard_map/ppermute | solution.py:39
  0.5 42.8 %collective-permute-start.3 = (bf16[704,2048]{1,0:T(8,128)(2,1)}, bf16[704,2048]{1,0:T(8,128)(2,1)}, u32[]{:S(2)}, u32[]{:S(2)}) collective-permute-start(bf16[704,2048]{1,0:T(8,128)(2,1)} %bitcast.14), channel_id=1, source_target_pairs={{0,1},{1,0},{2,3},{3,2},{4,5},{5,4},{6,7},{7,6},{8,9},{9,8},{10,11... | collective-permute-start | bytes 8650760 | tf_op jit(solution)/shard_map/ppermute | solution.py:39
  0.6 43.6 %collective-permute-start.4 = (bf16[704,2048]{1,0:T(8,128)(2,1)}, bf16[704,2048]{1,0:T(8,128)(2,1)}, u32[]{:S(2)}, u32[]{:S(2)}) collective-permute-start(bf16[704,2048]{1,0:T(8,128)(2,1)} %refs_2_.1), channel_id=1, source_target_pairs={{0,1},{1,0},{2,3},{3,2},{4,5},{5,4},{6,7},{7,6},{8,9},{9,8},{10,11... | collective-permute-start | bytes 8650760 | tf_op jit(solution)/shard_map/ppermute | solution.py:39
  5.7 17.9 %collective-permute-start.5 = (bf16[136,2048]{1,0:T(8,128)(2,1)S(1)}, bf16[136,2048]{1,0:T(8,128)(2,1)S(1)}, u32[]{:S(2)}, u32[]{:S(2)}) collective-permute-start(bf16[136,2048]{1,0:T(8,128)(2,1)S(1)} %pad_maximum_fusion.refs_0_.refs_2_.refs_1_), channel_id=1, source_target_pairs={{0,8},{1,9},{2,10},{3,11},{4,12},{5,13},{6,14},{7,15},{8,16},{9,17... | collective-permute-start | bytes 1671176 | tf_op jit(solution)/shard_map/ppermute | solution.py:39
  8.4 16.8 %collective-permute-start = (bf16[136,2048]{1,0:T(8,128)(2,1)S(1)}, bf16[136,2048]{1,0:T(8,128)(2,1)S(1)}, u32[]{:S(2)}, u32[]{:S(2)}) collective-permute-start(bf16[136,2048]{1,0:T(8,128)(2,1)S(1)} %pad_maximum_fusion.refs_0_.refs_2_.refs_1_), channel_id=1, source_target_pairs={{0,2},{1,3},{2,0},{3,1},{4,6},{5,7},{6,4},{7,5},{8,10},{9,11},{10,... | collective-permute-start | bytes 1671176 | tf_op jit(solution)/shard_map/ppermute | solution.py:39
  23.6 9.5 %collective-permute-start.6 = (bf16[136,2048]{1,0:T(8,128)(2,1)S(1)}, bf16[136,2048]{1,0:T(8,128)(2,1)S(1)}, u32[]{:S(2)}, u32[]{:S(2)}) collective-permute-start(bf16[136,2048]{1,0:T(8,128)(2,1)S(1)} %collective-permute-done.5.refs_0_.refs_1_), channel_id=1, source_target_pairs={{0,2},{1,5},{2,0},{3,7},{4,6},{5,1},{6,4},{7,3},{8,10},{9,13},{10,... | collective-permute-start | bytes 1671176 | tf_op jit(solution)/shard_map/ppermute | solution.py:39
  25.1 15.7 %collective-permute-start.8 = (bf16[136,2048]{1,0:T(8,128)(2,1)S(1)}, bf16[136,2048]{1,0:T(8,128)(2,1)S(1)}, u32[]{:S(2)}, u32[]{:S(2)}) collective-permute-start(bf16[136,2048]{1,0:T(8,128)(2,1)S(1)} %collective-permute-done.5.refs_0_.refs_1_), channel_id=1, source_target_pairs={{0,8},{1,9},{2,10},{3,11},{4,12},{5,13},{6,14},{7,15},{8,16},{9,17... | collective-permute-start | bytes 1671176 | tf_op jit(solution)/shard_map/ppermute | solution.py:39
  33.2 18.3 %collective-permute-start.10 = (bf16[136,2048]{1,0:T(8,128)(2,1)S(1)}, bf16[136,2048]{1,0:T(8,128)(2,1)S(1)}, u32[]{:S(2)}, u32[]{:S(2)}) collective-permute-start(bf16[136,2048]{1,0:T(8,128)(2,1)S(1)} %pad_maximum_fusion.refs_0_.refs_2_.refs_1_), channel_id=1, source_target_pairs={{0,1},{1,0},{2,3},{3,2},{4,5},{5,4},{6,7},{7,6},{8,9},{9,8},{10,11... | collective-permute-start | bytes 1671176 | tf_op jit(solution)/shard_map/ppermute | solution.py:39
  40.9 18.3 %collective-permute-start.11 = (bf16[136,2048]{1,0:T(8,128)(2,1)S(1)}, bf16[136,2048]{1,0:T(8,128)(2,1)S(1)}, u32[]{:S(2)}, u32[]{:S(2)}) collective-permute-start(bf16[136,2048]{1,0:T(8,128)(2,1)S(1)} %collective-permute-done.refs_1_.refs_2_), channel_id=1, source_target_pairs={{0,1},{1,0},{2,3},{3,2},{4,5},{5,4},{6,7},{7,6},{8,9},{9,8},{10,11... | collective-permute-start | bytes 1671176 | tf_op jit(solution)/shard_map/ppermute | solution.py:39
  40.9 16.8 %collective-permute-start.14 = (bf16[136,2048]{1,0:T(8,128)(2,1)S(1)}, bf16[136,2048]{1,0:T(8,128)(2,1)S(1)}, u32[]{:S(2)}, u32[]{:S(2)}) collective-permute-start(bf16[136,2048]{1,0:T(8,128)(2,1)S(1)} %collective-permute-done.8.refs_0_.refs_1_), channel_id=1, source_target_pairs={{0,8},{1,9},{2,10},{3,11},{4,12},{5,13},{6,14},{7,15},{8,16},{9,17... | collective-permute-start | bytes 1671176 | tf_op jit(solution)/shard_map/ppermute | solution.py:39
  43.3 24.1 %collective-permute-start.7 = (bf16[144,2048]{1,0:T(8,128)(2,1)S(1)}, bf16[144,2048]{1,0:T(8,128)(2,1)S(1)}, u32[]{:S(2)}, u32[]{:S(2)}) collective-permute-start(bf16[144,2048]{1,0:T(8,128)(2,1)S(1)} %send_rows.5.refs_6_), channel_id=1, source_target_pairs={{0,4},{1,3},{2,6},{3,1},{4,0},{5,7},{6,2},{7,5},{8,12},{9,11},{10,... | collective-permute-start | bytes 1769480 | tf_op jit(solution)/shard_map/ppermute | solution.py:39
  44.1 22.4 %collective-permute-start.9 = (bf16[136,2048]{1,0:T(8,128)(2,1)S(1)}, bf16[136,2048]{1,0:T(8,128)(2,1)S(1)}, u32[]{:S(2)}, u32[]{:S(2)}) collective-permute-start(bf16[136,2048]{1,0:T(8,128)(2,1)S(1)} %collective-permute-done.8.refs_0_.refs_1_), channel_id=1, source_target_pairs={{0,2},{1,5},{2,0},{3,7},{4,6},{5,1},{6,4},{7,3},{8,10},{9,13},{10,... | collective-permute-start | bytes 1671176 | tf_op jit(solution)/shard_map/ppermute | solution.py:39
  51.5 24.6 %collective-permute-start.1 = (bf16[144,2048]{1,0:T(8,128)(2,1)S(1)}, bf16[144,2048]{1,0:T(8,128)(2,1)S(1)}, u32[]{:S(2)}, u32[]{:S(2)}) collective-permute-start(bf16[144,2048]{1,0:T(8,128)(2,1)S(1)} %send_rows.4.refs_2_), channel_id=1, source_target_pairs={{0,4},{1,5},{2,6},{3,7},{4,0},{5,1},{6,2},{7,3},{8,12},{9,13},{10,... | collective-permute-start | bytes 1769480 | tf_op jit(solution)/shard_map/ppermute | solution.py:39
  57.7 25.1 %collective-permute-start.15 = (bf16[136,2048]{1,0:T(8,128)(2,1)S(1)}, bf16[136,2048]{1,0:T(8,128)(2,1)S(1)}, u32[]{:S(2)}, u32[]{:S(2)}) collective-permute-start(bf16[136,2048]{1,0:T(8,128)(2,1)S(1)} %collective-permute-done.14.refs_0_.refs_1_), channel_id=1, source_target_pairs={{0,2},{1,5},{2,0},{3,7},{4,6},{5,1},{6,4},{7,3},{8,10},{9,13},{10,... | collective-permute-start | bytes 1671176 | tf_op jit(solution)/shard_map/ppermute | solution.py:39
  73.9 10.3 %collective-permute-start.18 = (bf16[144,2048]{1,0:T(8,128)(2,1)S(1)}, bf16[144,2048]{1,0:T(8,128)(2,1)S(1)}, u32[]{:S(2)}, u32[]{:S(2)}) collective-permute-start(bf16[144,2048]{1,0:T(8,128)(2,1)S(1)} %get-tuple-element.40), channel_id=1, source_target_pairs={{0,4},{1,3},{2,6},{3,1},{4,0},{5,7},{6,2},{7,5},{8,12},{9,11},{10,... | collective-permute-start | bytes 1769480 | tf_op jit(solution)/shard_map/ppermute | solution.py:39
  74.5 19.8 %collective-permute-start.17 = (bf16[144,2048]{1,0:T(8,128)(2,1)S(1)}, bf16[144,2048]{1,0:T(8,128)(2,1)S(1)}, u32[]{:S(2)}, u32[]{:S(2)}) collective-permute-start(bf16[144,2048]{1,0:T(8,128)(2,1)S(1)} %send_rows.6.refs_10_), channel_id=1, source_target_pairs={{0,4},{1,3},{2,6},{3,1},{4,0},{5,7},{6,2},{7,5},{8,12},{9,11},{10,... | collective-permute-start | bytes 1769480 | tf_op jit(solution)/shard_map/ppermute | solution.py:39
  83.6 18.8 %collective-permute-start.16 = (bf16[144,2048]{1,0:T(8,128)(2,1)S(1)}, bf16[144,2048]{1,0:T(8,128)(2,1)S(1)}, u32[]{:S(2)}, u32[]{:S(2)}) collective-permute-start(bf16[144,2048]{1,0:T(8,128)(2,1)S(1)} %send_rows.7.refs_4_), channel_id=1, source_target_pairs={{0,4},{1,3},{2,6},{3,1},{4,0},{5,7},{6,2},{7,5},{8,12},{9,11},{10,... | collective-permute-start | bytes 1769480 | tf_op jit(solution)/shard_map/ppermute | solution.py:39
  85.5 24.2 %collective-permute-start.24 = (bf16[128,2048]{1,0:T(8,128)(2,1)S(1)}, bf16[128,2048]{1,0:T(8,128)(2,1)S(1)}, u32[]{:S(2)}, u32[]{:S(2)}) collective-permute-start(bf16[128,2048]{1,0:T(8,128)(2,1)S(1)} %get-tuple-element.52), channel_id=1, source_target_pairs={{0,2},{1,5},{2,0},{3,7},{4,6},{5,1},{6,4},{7,3},{8,10},{9,13},{10,... | collective-permute-start | bytes 1572872 | tf_op jit(solution)/shard_map/ppermute | solution.py:39
  100.8 9.9 %collective-permute-start.20 = (bf16[144,2048]{1,0:T(8,128)(2,1)S(1)}, bf16[144,2048]{1,0:T(8,128)(2,1)S(1)}, u32[]{:S(2)}, u32[]{:S(2)}) collective-permute-start(bf16[144,2048]{1,0:T(8,128)(2,1)S(1)} %get-tuple-element.45), channel_id=1, source_target_pairs={{0,4},{1,3},{2,6},{3,1},{4,0},{5,7},{6,2},{7,5},{8,12},{9,11},{10,... | collective-permute-start | bytes 1769480 | tf_op jit(solution)/shard_map/ppermute | solution.py:39
  109.0 16.3 %collective-permute-start.19 = (bf16[144,2048]{1,0:T(8,128)(2,1)S(1)}, bf16[144,2048]{1,0:T(8,128)(2,1)S(1)}, u32[]{:S(2)}, u32[]{:S(2)}) collective-permute-start(bf16[144,2048]{1,0:T(8,128)(2,1)S(1)} %get-tuple-element.44), channel_id=1, source_target_pairs={{0,4},{1,3},{2,6},{3,1},{4,0},{5,7},{6,2},{7,5},{8,12},{9,11},{10,... | collective-permute-start | bytes 1769480 | tf_op jit(solution)/shard_map/ppermute | solution.py:39
  109.9 18.0 %collective-permute-start.25 = (bf16[128,2048]{1,0:T(8,128)(2,1)S(1)}, bf16[128,2048]{1,0:T(8,128)(2,1)S(1)}, u32[]{:S(2)}, u32[]{:S(2)}) collective-permute-start(bf16[128,2048]{1,0:T(8,128)(2,1)S(1)} %add_convert_fusion.3), channel_id=1, source_target_pairs={{0,8},{1,9},{2,10},{3,11},{4,12},{5,13},{6,14},{7,15},{8,16},{9,17... | collective-permute-start | bytes 1572872 | tf_op jit(solution)/shard_map/ppermute | solution.py:39
  112.1 15.8 %collective-permute-start.23 = (bf16[128,2048]{1,0:T(8,128)(2,1)S(1)}, bf16[128,2048]{1,0:T(8,128)(2,1)S(1)}, u32[]{:S(2)}, u32[]{:S(2)}) collective-permute-start(bf16[128,2048]{1,0:T(8,128)(2,1)S(1)} %get-tuple-element.51), channel_id=1, source_target_pairs={{0,2},{1,5},{2,0},{3,7},{4,6},{5,1},{6,4},{7,3},{8,10},{9,13},{10,... | collective-permute-start | bytes 1572872 | tf_op jit(solution)/shard_map/ppermute | solution.py:39
  114.5 23.4 %collective-permute-start.13 = (bf16[256,2048]{1,0:T(8,128)(2,1)S(1)}, bf16[256,2048]{1,0:T(8,128)(2,1)S(1)}, u32[]{:S(2)}, u32[]{:S(2)}) collective-permute-start(bf16[256,2048]{1,0:T(8,128)(2,1)S(1)} %get-tuple-element.39), channel_id=1, source_target_pairs={{0,1},{1,0},{2,3},{3,2},{4,5},{5,4},{6,7},{7,6},{8,9},{9,8},{10,11... | collective-permute-start | bytes 3145736 | tf_op jit(solution)/shard_map/ppermute | solution.py:39
  114.5 23.4 %collective-permute-start.12 = (bf16[144,2048]{1,0:T(8,128)(2,1)S(1)}, bf16[144,2048]{1,0:T(8,128)(2,1)S(1)}, u32[]{:S(2)}, u32[]{:S(2)}) collective-permute-start(bf16[144,2048]{1,0:T(8,128)(2,1)S(1)} %get-tuple-element.38), channel_id=1, source_target_pairs={{0,4},{1,5},{2,6},{3,7},{4,0},{5,1},{6,2},{7,3},{8,12},{9,13},{10,... | collective-permute-start | bytes 1769480 | tf_op jit(solution)/shard_map/ppermute | solution.py:39
  126.5 14.0 %collective-permute-start.22 = (bf16[128,2048]{1,0:T(8,128)(2,1)S(1)}, bf16[128,2048]{1,0:T(8,128)(2,1)S(1)}, u32[]{:S(2)}, u32[]{:S(2)}) collective-permute-start(bf16[128,2048]{1,0:T(8,128)(2,1)S(1)} %get-tuple-element.50), channel_id=1, source_target_pairs={{0,2},{1,5},{2,0},{3,7},{4,6},{5,1},{6,4},{7,3},{8,10},{9,13},{10,... | collective-permute-start | bytes 1572872 | tf_op jit(solution)/shard_map/ppermute | solution.py:39
  128.1 12.5 %collective-permute-start.26 = (bf16[128,2048]{1,0:T(8,128)(2,1)S(1)}, bf16[128,2048]{1,0:T(8,128)(2,1)S(1)}, u32[]{:S(2)}, u32[]{:S(2)}) collective-permute-start(bf16[128,2048]{1,0:T(8,128)(2,1)S(1)} %add_convert_fusion.2), channel_id=1, source_target_pairs={{0,8},{1,9},{2,10},{3,11},{4,12},{5,13},{6,14},{7,15},{8,16},{9,17... | collective-permute-start | bytes 1572872 | tf_op jit(solution)/shard_map/ppermute | solution.py:39
  137.9 20.5 %copy-start.1 = (bf16[2048,16]{0,1:T(8,128)(2,1)S(1)}, bf16[2048,16]{0,1:T(8,128)(2,1)}, u32[]{:S(2)}) copy-start(bf16[2048,16]{0,1:T(8,128)(2,1)} %param.17) | copy-start | bytes 196612
  139.2 10.6 %collective-permute-start.21 = (bf16[128,2048]{1,0:T(8,128)(2,1)S(1)}, bf16[128,2048]{1,0:T(8,128)(2,1)S(1)}, u32[]{:S(2)}, u32[]{:S(2)}) collective-permute-start(bf16[128,2048]{1,0:T(8,128)(2,1)S(1)} %get-tuple-element.49), channel_id=1, source_target_pairs={{0,2},{1,3},{2,0},{3,1},{4,6},{5,7},{6,4},{7,5},{8,10},{9,11},{10,... | collective-permute-start | bytes 1572872 | tf_op jit(solution)/shard_map/ppermute | solution.py:39
  140.8 16.6 %collective-permute-start.27 = (bf16[128,2048]{1,0:T(8,128)(2,1)S(1)}, bf16[128,2048]{1,0:T(8,128)(2,1)S(1)}, u32[]{:S(2)}, u32[]{:S(2)}) collective-permute-start(bf16[128,2048]{1,0:T(8,128)(2,1)S(1)} %add_convert_fusion.1), channel_id=1, source_target_pairs={{0,8},{1,9},{2,10},{3,11},{4,12},{5,13},{6,14},{7,15},{8,16},{9,17... | collective-permute-start | bytes 1572872 | tf_op jit(solution)/shard_map/ppermute | solution.py:39

commit v4 on v3

--- a/solution.py
+++ b/solution.py
@@ -403,19 +403,24 @@
     spread()
     for step in later[1:2]:
         send(step)
-    for step in later[:1] + [0]:
+    for step in later[:1]:
         run(step)
-    for step in later[:1]:
         give(step)
     for step in later[2:]:
         send(step)
+    for step in later[1:2]:
+        run(step)
+        give(step)
     for step in later[:1]:
         join(step)
-    for step in later[1:]:
+    for step in later[2:]:
         run(step)
         give(step)
+    for step in later[1:2]:
+        join(step)
+    run(0)
     give(0)
-    for step in later[1:]:
+    for step in later[2:]:
         join(step)
     join(0, shared)
 

time: 159 us -> 171 us (1.075)
  waiting for transfers between devices: 80.1 us -> 91.6 us
    ppermute x28, waiting for transfers between devices: 80.1 us -> 91.6 us  [shift(): return lax.ppermute(block, AXES, route)]
  transfers between devices with their start and end apart: 28 -> 28, of which waited for: 11 -> 10; matrix products, arithmetic and copies ran while one was open for 4% -> 4% of each run, Pallas kernels for 31% -> 28%
where the time goes in v4:
time: 171 us; the launch traced here: 170 us
  waiting for transfers between devices  91.6 us (54%)
  Pallas kernels  48.4 us (28%)
  starting transfers between devices  22.6 us (13%)
  other arithmetic  4.84 us (3%)
    ppermute x28, waiting for transfers between devices, shift(): return lax.ppermute(block, AXES, route)  91.6 us
    pallas_call x5, Pallas kernels, feed_forward(): return list(call(*operands, *kept(blocks), *kept(came), *weights, *after))  33.5 us
    ppermute x28, starting transfers between devices, shift(): return lax.ppermute(block, AXES, route)  22.6 us
    pallas_call x1, Pallas kernels, load(): return list(call(*kept(arrays, pltpu.HBM), *after))  6.05 us
    pallas_call x4, Pallas kernels, combine(): return list(call(chosen, *kept(blocks), *kept(back), *kept(extra), *after))  5.27 us
    pallas_call x4, Pallas kernels, send_rows(): return list(call(chosen, *kept(blocks), *after))  3.48 us
  transfers between devices with their start and end apart: 28, of which 10 were waited for; matrix products, arithmetic and copies ran while one was open for 4% of the time, Pallas kernels for 28%

profile of v4, /device:TPU:0, one launch (start us, length us, event | category | flops | bytes accessed | tf_op | source)
XLA Modules:
  0.0 170.4 jit_solution(18008148240616788215)
XLA Ops:
  1.0 1.2 fusion.7
  3.1 1.2 fusion.9
  4.3 1.2 fusion.22
  5.7 2.7 %collective-permute-start.5 = (bf16[136,2048]{1,0:T(8,128)(2,1)S(1)}, bf16[136,2048]{1,0:T(8,128)(2,1)S(1)}, u32[]{:S(2)}, u32[]{:S(2)}) collective-permute-start(bf16[136,2048]{1,0:T(8,128)(2,1)S(1)} %pad_maximum_fusion.refs_0_.refs_2_.refs_1_), channel_id=1, source_target_pairs={{0,8},{1,9},{2,10},{3,11},{4,12},{5,13},{6,14},{7,15},{8,16},{9,17... | collective-permute-start | bytes 1671176 | tf_op jit(solution)/shard_map/ppermute | solution.py:39
  8.4 1.5 collective-permute-start
  9.9 13.8 %collective-permute-done.5.refs_0_.refs_1_ = bf16[136,2048]{1,0:T(8,128)(2,1)S(1)} collective-permute-done((bf16[136,2048]{1,0:T(8,128)(2,1)S(1)}, bf16[136,2048]{1,0:T(8,128)(2,1)S(1)}, u32[]{:S(2)}, u32[]{:S(2)}) %collective-permute-start.5) | collective-permute-done | bytes 557088 | tf_op jit(solution)/shard_map/ppermute | solution.py:39
  23.6 1.5 collective-permute-start.6
  25.1 14.7 %collective-permute-done.7.refs_0_.refs_1_ = bf16[136,2048]{1,0:T(8,128)(2,1)S(1)} collective-permute-done((bf16[136,2048]{1,0:T(8,128)(2,1)S(1)}, bf16[136,2048]{1,0:T(8,128)(2,1)S(1)}, u32[]{:S(2)}, u32[]{:S(2)}) %collective-permute-start.7) | collective-permute-done | bytes 557088 | tf_op jit(solution)/shard_map/ppermute | solution.py:39
  40.5 14.6 %collective-permute-done.12.refs_0_.refs_1_ = bf16[136,2048]{1,0:T(8,128)(2,1)S(1)} collective-permute-done((bf16[136,2048]{1,0:T(8,128)(2,1)S(1)}, bf16[136,2048]{1,0:T(8,128)(2,1)S(1)}, u32[]{:S(2)}, u32[]{:S(2)}) %collective-permute-start.12) | collective-permute-done | bytes 557088 | tf_op jit(solution)/shard_map/ppermute | solution.py:39
  57.6 1.1 collective-permute-start.14
  58.8 1.5 collective-permute-start.8
  60.8 6.0 %load.1 = (bf16[704,2048]{1,0:T(8,128)(2,1)S(1)}, bf16[704,2048]{1,0:T(8,128)(2,1)S(1)}, bf16[704,2048]{1,0:T(8,128)(2,1)S(1)}, bf16[704,2048]{1,0:T(8,128)(2,1)...) custom-call(bf16[704,2048]{1,0:T(8,128)(2,1)} %bitcast.13, bf16[704,2048]{1,0:T(8,128)(2,1)} %bitcast.15, ...), custom_call_target="tpu_custom_call" | custom-call | flops 4294967296 | tf_op jit(solution)/shard_map/load/pallas_call | solution.py:124
  66.9 7.3 %shared.1 = (f32[256,2048]{1,0:T(8,128)S(1)}, bf16[256,2048]{1,0:T(8,128)(2,1)S(1)}) custom-call(bf16[136,2048]{1,0:T(8,128)(2,1)S(1)} %pad_maximum_fusion.refs_0_.refs_2_.refs_1_, bf16[136,2048]{1,0:T(8,128)(2,1)S(1)} %collective-permute-done.refs_1_.refs_2_, bf16[136,2048]{1,0:T(8,128)(2,1)S(1)} %collective-permute-done.9.refs_2_, ...), custom_call_target="tpu_custom_call" | custom-call | flops 4429185024 | tf_op jit(solution)/shard_map/shared/pallas_call | solution.py:258
  76.1 6.5 %experts.4 = (bf16[144,2048]{1,0:T(8,128)(2,1)S(1)}, bf16[144,2048]{1,0:T(8,128)(2,1)S(1)}) custom-call(s32[2]{0:T(128)S(1)} %dynamic-slice_bitcast_fusion.slot_ref.refs_0_, bf16[136,2048]{1,0:T(8,128)(2,1)S(1)} %collective-permute-done.5.refs_0_.refs_1_, bf16[136,2048]{1,0:T(8,128)(2,1)S(1)} %collective-permute-done.6.refs_1_.refs_2_, ...), custom_call_target="tpu_custom_call" | custom-call | flops 4982833152 | tf_op jit(solution)/shard_map/experts/pallas_call | solution.py:258
  82.6 1.1 collective-permute-start.17
  85.8 6.7 %experts.5 = (bf16[144,2048]{1,0:T(8,128)(2,1)S(1)}, bf16[144,2048]{1,0:T(8,128)(2,1)S(1)}) custom-call(s32[2]{0:T(128)S(1)} %dynamic-slice_bitcast_fusion.slot_ref.refs_0_, bf16[136,2048]{1,0:T(8,128)(2,1)S(1)} %collective-permute-done.7.refs_0_.refs_1_, bf16[136,2048]{1,0:T(8,128)(2,1)S(1)} %collective-permute-done.8.refs_1_.refs_2_, ...), custom_call_target="tpu_custom_call" | custom-call | flops 4982833152 | tf_op jit(solution)/shard_map/experts/pallas_call | solution.py:258
  92.6 1.3 combine.4
  95.0 1.5 collective-permute-start.1
  97.1 4.6 %collective-permute-done.16.refs_3_ = bf16[144,2048]{1,0:T(8,128)(2,1)S(1)} collective-permute-done((bf16[144,2048]{1,0:T(8,128)(2,1)S(1)}, bf16[144,2048]{1,0:T(8,128)(2,1)S(1)}, u32[]{:S(2)}, u32[]{:S(2)}) %collective-permute-start.16) | collective-permute-done | bytes 589856 | tf_op jit(solution)/shard_map/ppermute | solution.py:39
  101.6 6.5 %experts.6 = (bf16[144,2048]{1,0:T(8,128)(2,1)S(1)}, bf16[144,2048]{1,0:T(8,128)(2,1)S(1)}) custom-call(s32[2]{0:T(128)S(1)} %dynamic-slice_bitcast_fusion.slot_ref.refs_0_, bf16[136,2048]{1,0:T(8,128)(2,1)S(1)} %collective-permute-done.12.refs_0_.refs_1_, bf16[136,2048]{1,0:T(8,128)(2,1)S(1)} %collective-permute-done.13.refs_1_.refs_2_, ...), custom_call_target="tpu_custom_call" | custom-call | flops 4982833152 | tf_op jit(solution)/shard_map/experts/pallas_call | solution.py:258
  108.2 1.1 collective-permute-start.20
  109.7 17.2 %collective-permute-done.15.refs_3_ = bf16[144,2048]{1,0:T(8,128)(2,1)S(1)} collective-permute-done((bf16[144,2048]{1,0:T(8,128)(2,1)S(1)}, bf16[144,2048]{1,0:T(8,128)(2,1)S(1)}, u32[]{:S(2)}, u32[]{:S(2)}) %collective-permute-start.15) | collective-permute-done | bytes 589856 | tf_op jit(solution)/shard_map/ppermute | solution.py:39
  126.9 1.3 combine.5
  128.2 1.1 collective-permute-start.23
  129.4 6.5 %experts.7 = (bf16[144,2048]{1,0:T(8,128)(2,1)S(1)}, bf16[144,2048]{1,0:T(8,128)(2,1)S(1)}) custom-call(s32[2]{0:T(128)S(1)} %dynamic-slice_bitcast_fusion.1.slot_ref.refs_0_, bf16[136,2048]{1,0:T(8,128)(2,1)S(1)} %pad_maximum_fusion.refs_0_.refs_2_.refs_1_, bf16[136,2048]{1,0:T(8,128)(2,1)S(1)} %collective-permute-done.refs_1_.refs_2_, ...), custom_call_target="tpu_custom_call" | custom-call | flops 4982833152 | tf_op jit(solution)/shard_map/experts/pallas_call | solution.py:258
  135.9 1.6 collective-permute-start.18
  137.5 2.1 %collective-permute-done.20.refs_3_ = bf16[144,2048]{1,0:T(8,128)(2,1)S(1)} collective-permute-done((bf16[144,2048]{1,0:T(8,128)(2,1)S(1)}, bf16[144,2048]{1,0:T(8,128)(2,1)S(1)}, u32[]{:S(2)}, u32[]{:S(2)}) %collective-permute-start.20) | collective-permute-done | bytes 589856 | tf_op jit(solution)/shard_map/ppermute | solution.py:39
  139.6 1.3 combine.6
  142.3 9.9 %collective-permute-done.18.refs_3_ = bf16[144,2048]{1,0:T(8,128)(2,1)S(1)} collective-permute-done((bf16[144,2048]{1,0:T(8,128)(2,1)S(1)}, bf16[144,2048]{1,0:T(8,128)(2,1)S(1)}, u32[]{:S(2)}, u32[]{:S(2)}) %collective-permute-start.18) | collective-permute-done | bytes 589856 | tf_op jit(solution)/shard_map/ppermute | solution.py:39
  152.2 1.3 combine.7
  155.0 7.8 %collective-permute-done.21 = bf16[128,2048]{1,0:T(8,128)(2,1)S(1)} collective-permute-done((bf16[128,2048]{1,0:T(8,128)(2,1)S(1)}, bf16[128,2048]{1,0:T(8,128)(2,1)S(1)}, u32[]{:S(2)}, u32[]{:S(2)}) %collective-permute-start.21) | collective-permute-done | bytes 524320 | tf_op jit(solution)/shard_map/ppermute | solution.py:39
  162.8 6.6 %collective-permute-done.27 = bf16[128,2048]{1,0:T(8,128)(2,1)S(1)} collective-permute-done((bf16[128,2048]{1,0:T(8,128)(2,1)S(1)}, bf16[128,2048]{1,0:T(8,128)(2,1)S(1)}, u32[]{:S(2)}, u32[]{:S(2)}) %collective-permute-start.27) | collective-permute-done | bytes 524320 | tf_op jit(solution)/shard_map/ppermute | solution.py:39
  (59 shorter events, 15.5 us)
Async XLA Ops:
  0.0 4.3 %copy-start = (bf16[2048,16]{0,1:T(8,128)(2,1)S(1)}, bf16[2048,16]{0,1:T(8,128)(2,1)}, u32[]{:S(2)}) copy-start(bf16[2048,16]{0,1:T(8,128)(2,1)} %param.17) | copy-start | bytes 196612
  0.0 57.6 %collective-permute-start.2 = (bf16[704,2048]{1,0:T(8,128)(2,1)}, bf16[704,2048]{1,0:T(8,128)(2,1)}, u32[]{:S(2)}, u32[]{:S(2)}) collective-permute-start(bf16[704,2048]{1,0:T(8,128)(2,1)} %bitcast.12), channel_id=1, source_target_pairs={{0,1},{1,0},{2,3},{3,2},{4,5},{5,4},{6,7},{7,6},{8,9},{9,8},{10,11... | collective-permute-start | bytes 8650760 | tf_op jit(solution)/shard_map/ppermute | solution.py:39
  0.5 58.3 %collective-permute-start.3 = (bf16[704,2048]{1,0:T(8,128)(2,1)}, bf16[704,2048]{1,0:T(8,128)(2,1)}, u32[]{:S(2)}, u32[]{:S(2)}) collective-permute-start(bf16[704,2048]{1,0:T(8,128)(2,1)} %bitcast.14), channel_id=1, source_target_pairs={{0,1},{1,0},{2,3},{3,2},{4,5},{5,4},{6,7},{7,6},{8,9},{9,8},{10,11... | collective-permute-start | bytes 8650760 | tf_op jit(solution)/shard_map/ppermute | solution.py:39
  0.6 59.7 %collective-permute-start.4 = (bf16[704,2048]{1,0:T(8,128)(2,1)}, bf16[704,2048]{1,0:T(8,128)(2,1)}, u32[]{:S(2)}, u32[]{:S(2)}) collective-permute-start(bf16[704,2048]{1,0:T(8,128)(2,1)} %refs_2_.1), channel_id=1, source_target_pairs={{0,1},{1,0},{2,3},{3,2},{4,5},{5,4},{6,7},{7,6},{8,9},{9,8},{10,11... | collective-permute-start | bytes 8650760 | tf_op jit(solution)/shard_map/ppermute | solution.py:39
  5.7 17.9 %collective-permute-start.5 = (bf16[136,2048]{1,0:T(8,128)(2,1)S(1)}, bf16[136,2048]{1,0:T(8,128)(2,1)S(1)}, u32[]{:S(2)}, u32[]{:S(2)}) collective-permute-start(bf16[136,2048]{1,0:T(8,128)(2,1)S(1)} %pad_maximum_fusion.refs_0_.refs_2_.refs_1_), channel_id=1, source_target_pairs={{0,8},{1,9},{2,10},{3,11},{4,12},{5,13},{6,14},{7,15},{8,16},{9,17... | collective-permute-start | bytes 1671176 | tf_op jit(solution)/shard_map/ppermute | solution.py:39
  8.4 15.3 %collective-permute-start = (bf16[136,2048]{1,0:T(8,128)(2,1)S(1)}, bf16[136,2048]{1,0:T(8,128)(2,1)S(1)}, u32[]{:S(2)}, u32[]{:S(2)}) collective-permute-start(bf16[136,2048]{1,0:T(8,128)(2,1)S(1)} %pad_maximum_fusion.refs_0_.refs_2_.refs_1_), channel_id=1, source_target_pairs={{0,2},{1,3},{2,0},{3,1},{4,6},{5,7},{6,4},{7,5},{8,10},{9,11},{10,... | collective-permute-start | bytes 1671176 | tf_op jit(solution)/shard_map/ppermute | solution.py:39
  23.6 16.2 %collective-permute-start.7 = (bf16[136,2048]{1,0:T(8,128)(2,1)S(1)}, bf16[136,2048]{1,0:T(8,128)(2,1)S(1)}, u32[]{:S(2)}, u32[]{:S(2)}) collective-permute-start(bf16[136,2048]{1,0:T(8,128)(2,1)S(1)} %collective-permute-done.5.refs_0_.refs_1_), channel_id=1, source_target_pairs={{0,8},{1,9},{2,10},{3,11},{4,12},{5,13},{6,14},{7,15},{8,16},{9,17... | collective-permute-start | bytes 1671176 | tf_op jit(solution)/shard_map/ppermute | solution.py:39
  23.6 16.9 %collective-permute-start.6 = (bf16[136,2048]{1,0:T(8,128)(2,1)S(1)}, bf16[136,2048]{1,0:T(8,128)(2,1)S(1)}, u32[]{:S(2)}, u32[]{:S(2)}) collective-permute-start(bf16[136,2048]{1,0:T(8,128)(2,1)S(1)} %collective-permute-done.5.refs_0_.refs_1_), channel_id=1, source_target_pairs={{0,2},{1,5},{2,0},{3,7},{4,6},{5,1},{6,4},{7,3},{8,10},{9,13},{10,... | collective-permute-start | bytes 1671176 | tf_op jit(solution)/shard_map/ppermute | solution.py:39
  39.8 15.3 %collective-permute-start.12 = (bf16[136,2048]{1,0:T(8,128)(2,1)S(1)}, bf16[136,2048]{1,0:T(8,128)(2,1)S(1)}, u32[]{:S(2)}, u32[]{:S(2)}) collective-permute-start(bf16[136,2048]{1,0:T(8,128)(2,1)S(1)} %collective-permute-done.7.refs_0_.refs_1_), channel_id=1, source_target_pairs={{0,8},{1,9},{2,10},{3,11},{4,12},{5,13},{6,14},{7,15},{8,16},{9,17... | collective-permute-start | bytes 1671176 | tf_op jit(solution)/shard_map/ppermute | solution.py:39
  40.5 26.3 %collective-permute-start.9 = (bf16[136,2048]{1,0:T(8,128)(2,1)S(1)}, bf16[136,2048]{1,0:T(8,128)(2,1)S(1)}, u32[]{:S(2)}, u32[]{:S(2)}) collective-permute-start(bf16[136,2048]{1,0:T(8,128)(2,1)S(1)} %pad_maximum_fusion.refs_0_.refs_2_.refs_1_), channel_id=1, source_target_pairs={{0,1},{1,0},{2,3},{3,2},{4,5},{5,4},{6,7},{7,6},{8,9},{9,8},{10,11... | collective-permute-start | bytes 1671176 | tf_op jit(solution)/shard_map/ppermute | solution.py:39
  55.2 11.7 %collective-permute-start.10 = (bf16[136,2048]{1,0:T(8,128)(2,1)S(1)}, bf16[136,2048]{1,0:T(8,128)(2,1)S(1)}, u32[]{:S(2)}, u32[]{:S(2)}) collective-permute-start(bf16[136,2048]{1,0:T(8,128)(2,1)S(1)} %collective-permute-done.refs_1_.refs_2_), channel_id=1, source_target_pairs={{0,1},{1,0},{2,3},{3,2},{4,5},{5,4},{6,7},{7,6},{8,9},{9,8},{10,11... | collective-permute-start | bytes 1671176 | tf_op jit(solution)/shard_map/ppermute | solution.py:39
  57.6 18.5 %collective-permute-start.14 = (bf16[144,2048]{1,0:T(8,128)(2,1)S(1)}, bf16[144,2048]{1,0:T(8,128)(2,1)S(1)}, u32[]{:S(2)}, u32[]{:S(2)}) collective-permute-start(bf16[144,2048]{1,0:T(8,128)(2,1)S(1)} %send_rows.5.refs_6_), channel_id=1, source_target_pairs={{0,4},{1,3},{2,6},{3,1},{4,0},{5,7},{6,2},{7,5},{8,12},{9,11},{10,... | collective-permute-start | bytes 1769480 | tf_op jit(solution)/shard_map/ppermute | solution.py:39
  58.8 15.4 %collective-permute-start.8 = (bf16[136,2048]{1,0:T(8,128)(2,1)S(1)}, bf16[136,2048]{1,0:T(8,128)(2,1)S(1)}, u32[]{:S(2)}, u32[]{:S(2)}) collective-permute-start(bf16[136,2048]{1,0:T(8,128)(2,1)S(1)} %collective-permute-done.7.refs_0_.refs_1_), channel_id=1, source_target_pairs={{0,2},{1,5},{2,0},{3,7},{4,6},{5,1},{6,4},{7,3},{8,10},{9,13},{10,... | collective-permute-start | bytes 1671176 | tf_op jit(solution)/shard_map/ppermute | solution.py:39
  60.3 23.5 %collective-permute-start.13 = (bf16[136,2048]{1,0:T(8,128)(2,1)S(1)}, bf16[136,2048]{1,0:T(8,128)(2,1)S(1)}, u32[]{:S(2)}, u32[]{:S(2)}) collective-permute-start(bf16[136,2048]{1,0:T(8,128)(2,1)S(1)} %collective-permute-done.12.refs_0_.refs_1_), channel_id=1, source_target_pairs={{0,2},{1,5},{2,0},{3,7},{4,6},{5,1},{6,4},{7,3},{8,10},{9,13},{10,... | collective-permute-start | bytes 1671176 | tf_op jit(solution)/shard_map/ppermute | solution.py:39
  75.1 10.7 %collective-permute-start.11 = (bf16[144,2048]{1,0:T(8,128)(2,1)S(1)}, bf16[144,2048]{1,0:T(8,128)(2,1)S(1)}, u32[]{:S(2)}, u32[]{:S(2)}) collective-permute-start(bf16[144,2048]{1,0:T(8,128)(2,1)S(1)} %send_rows.6.refs_10_), channel_id=1, source_target_pairs={{0,4},{1,3},{2,6},{3,1},{4,0},{5,7},{6,2},{7,5},{8,12},{9,11},{10,... | collective-permute-start | bytes 1769480 | tf_op jit(solution)/shard_map/ppermute | solution.py:39
  82.6 9.9 %collective-permute-start.17 = (bf16[144,2048]{1,0:T(8,128)(2,1)S(1)}, bf16[144,2048]{1,0:T(8,128)(2,1)S(1)}, u32[]{:S(2)}, u32[]{:S(2)}) collective-permute-start(bf16[144,2048]{1,0:T(8,128)(2,1)S(1)} %get-tuple-element.39), channel_id=1, source_target_pairs={{0,4},{1,3},{2,6},{3,1},{4,0},{5,7},{6,2},{7,5},{8,12},{9,11},{10,... | collective-permute-start | bytes 1769480 | tf_op jit(solution)/shard_map/ppermute | solution.py:39
  84.7 17.0 %collective-permute-start.16 = (bf16[144,2048]{1,0:T(8,128)(2,1)S(1)}, bf16[144,2048]{1,0:T(8,128)(2,1)S(1)}, u32[]{:S(2)}, u32[]{:S(2)}) collective-permute-start(bf16[144,2048]{1,0:T(8,128)(2,1)S(1)} %send_rows.7.refs_10_), channel_id=1, source_target_pairs={{0,4},{1,3},{2,6},{3,1},{4,0},{5,7},{6,2},{7,5},{8,12},{9,11},{10,... | collective-permute-start | bytes 1769480 | tf_op jit(solution)/shard_map/ppermute | solution.py:39
  93.9 15.4 %collective-permute-start.24 = (bf16[128,2048]{1,0:T(8,128)(2,1)S(1)}, bf16[128,2048]{1,0:T(8,128)(2,1)S(1)}, u32[]{:S(2)}, u32[]{:S(2)}) collective-permute-start(bf16[128,2048]{1,0:T(8,128)(2,1)S(1)} %get-tuple-element.52), channel_id=1, source_target_pairs={{0,2},{1,5},{2,0},{3,7},{4,6},{5,1},{6,4},{7,3},{8,10},{9,13},{10,... | collective-permute-start | bytes 1572872 | tf_op jit(solution)/shard_map/ppermute | solution.py:39
  95.0 34.3 %collective-permute-start.1 = (bf16[144,2048]{1,0:T(8,128)(2,1)S(1)}, bf16[144,2048]{1,0:T(8,128)(2,1)S(1)}, u32[]{:S(2)}, u32[]{:S(2)}) collective-permute-start(bf16[144,2048]{1,0:T(8,128)(2,1)S(1)} %send_rows.4.refs_2_), channel_id=1, source_target_pairs={{0,4},{1,5},{2,6},{3,7},{4,0},{5,1},{6,2},{7,3},{8,12},{9,13},{10,... | collective-permute-start | bytes 1769480 | tf_op jit(solution)/shard_map/ppermute | solution.py:39
  96.5 45.7 %collective-permute-start.19 = (bf16[256,2048]{1,0:T(8,128)(2,1)S(1)}, bf16[256,2048]{1,0:T(8,128)(2,1)S(1)}, u32[]{:S(2)}, u32[]{:S(2)}) collective-permute-start(bf16[256,2048]{1,0:T(8,128)(2,1)S(1)} %get-tuple-element.45), channel_id=1, source_target_pairs={{0,1},{1,0},{2,3},{3,2},{4,5},{5,4},{6,7},{7,6},{8,9},{9,8},{10,11... | collective-permute-start | bytes 3145736 | tf_op jit(solution)/shard_map/ppermute | solution.py:39
  96.6 30.4 %collective-permute-start.15 = (bf16[144,2048]{1,0:T(8,128)(2,1)S(1)}, bf16[144,2048]{1,0:T(8,128)(2,1)S(1)}, u32[]{:S(2)}, u32[]{:S(2)}) collective-permute-start(bf16[144,2048]{1,0:T(8,128)(2,1)S(1)} %get-tuple-element.38), channel_id=1, source_target_pairs={{0,4},{1,3},{2,6},{3,1},{4,0},{5,7},{6,2},{7,5},{8,12},{9,11},{10,... | collective-permute-start | bytes 1769480 | tf_op jit(solution)/shard_map/ppermute | solution.py:39
  108.2 31.4 %collective-permute-start.20 = (bf16[144,2048]{1,0:T(8,128)(2,1)S(1)}, bf16[144,2048]{1,0:T(8,128)(2,1)S(1)}, u32[]{:S(2)}, u32[]{:S(2)}) collective-permute-start(bf16[144,2048]{1,0:T(8,128)(2,1)S(1)} %get-tuple-element.46), channel_id=1, source_target_pairs={{0,4},{1,3},{2,6},{3,1},{4,0},{5,7},{6,2},{7,5},{8,12},{9,11},{10,... | collective-permute-start | bytes 1769480 | tf_op jit(solution)/shard_map/ppermute | solution.py:39
  109.5 32.6 %collective-permute-start.25 = (bf16[128,2048]{1,0:T(8,128)(2,1)S(1)}, bf16[128,2048]{1,0:T(8,128)(2,1)S(1)}, u32[]{:S(2)}, u32[]{:S(2)}) collective-permute-start(bf16[128,2048]{1,0:T(8,128)(2,1)S(1)} %add_convert_fusion.3), channel_id=1, source_target_pairs={{0,8},{1,9},{2,10},{3,11},{4,12},{5,13},{6,14},{7,15},{8,16},{9,17... | collective-permute-start | bytes 1572872 | tf_op jit(solution)/shard_map/ppermute | solution.py:39
  128.2 13.8 %collective-permute-start.23 = (bf16[128,2048]{1,0:T(8,128)(2,1)S(1)}, bf16[128,2048]{1,0:T(8,128)(2,1)S(1)}, u32[]{:S(2)}, u32[]{:S(2)}) collective-permute-start(bf16[128,2048]{1,0:T(8,128)(2,1)S(1)} %get-tuple-element.51), channel_id=1, source_target_pairs={{0,2},{1,5},{2,0},{3,7},{4,6},{5,1},{6,4},{7,3},{8,10},{9,13},{10,... | collective-permute-start | bytes 1572872 | tf_op jit(solution)/shard_map/ppermute | solution.py:39
  135.9 16.3 %collective-permute-start.18 = (bf16[144,2048]{1,0:T(8,128)(2,1)S(1)}, bf16[144,2048]{1,0:T(8,128)(2,1)S(1)}, u32[]{:S(2)}, u32[]{:S(2)}) collective-permute-start(bf16[144,2048]{1,0:T(8,128)(2,1)S(1)} %get-tuple-element.44), channel_id=1, source_target_pairs={{0,4},{1,5},{2,6},{3,7},{4,0},{5,1},{6,2},{7,3},{8,12},{9,13},{10,... | collective-permute-start | bytes 1769480 | tf_op jit(solution)/shard_map/ppermute | solution.py:39
  140.9 13.8 %collective-permute-start.22 = (bf16[128,2048]{1,0:T(8,128)(2,1)S(1)}, bf16[128,2048]{1,0:T(8,128)(2,1)S(1)}, u32[]{:S(2)}, u32[]{:S(2)}) collective-permute-start(bf16[128,2048]{1,0:T(8,128)(2,1)S(1)} %get-tuple-element.50), channel_id=1, source_target_pairs={{0,2},{1,5},{2,0},{3,7},{4,6},{5,1},{6,4},{7,3},{8,10},{9,13},{10,... | collective-permute-start | bytes 1572872 | tf_op jit(solution)/shard_map/ppermute | solution.py:39
  142.2 12.5 %collective-permute-start.26 = (bf16[128,2048]{1,0:T(8,128)(2,1)S(1)}, bf16[128,2048]{1,0:T(8,128)(2,1)S(1)}, u32[]{:S(2)}, u32[]{:S(2)}) collective-permute-start(bf16[128,2048]{1,0:T(8,128)(2,1)S(1)} %add_convert_fusion.2), channel_id=1, source_target_pairs={{0,8},{1,9},{2,10},{3,11},{4,12},{5,13},{6,14},{7,15},{8,16},{9,17... | collective-permute-start | bytes 1572872 | tf_op jit(solution)/shard_map/ppermute | solution.py:39
  152.2 18.2 %copy-start.1 = (bf16[2048,16]{0,1:T(8,128)(2,1)S(1)}, bf16[2048,16]{0,1:T(8,128)(2,1)}, u32[]{:S(2)}) copy-start(bf16[2048,16]{0,1:T(8,128)(2,1)} %param.17) | copy-start | bytes 196612
  153.6 9.2 %collective-permute-start.21 = (bf16[128,2048]{1,0:T(8,128)(2,1)S(1)}, bf16[128,2048]{1,0:T(8,128)(2,1)S(1)}, u32[]{:S(2)}, u32[]{:S(2)}) collective-permute-start(bf16[128,2048]{1,0:T(8,128)(2,1)S(1)} %get-tuple-element.49), channel_id=1, source_target_pairs={{0,2},{1,3},{2,0},{3,1},{4,6},{5,7},{6,4},{7,5},{8,10},{9,11},{10,... | collective-permute-start | bytes 1572872 | tf_op jit(solution)/shard_map/ppermute | solution.py:39
  154.9 14.5 %collective-permute-start.27 = (bf16[128,2048]{1,0:T(8,128)(2,1)S(1)}, bf16[128,2048]{1,0:T(8,128)(2,1)S(1)}, u32[]{:S(2)}, u32[]{:S(2)}) collective-permute-start(bf16[128,2048]{1,0:T(8,128)(2,1)S(1)} %add_convert_fusion.1), channel_id=1, source_target_pairs={{0,8},{1,9},{2,10},{3,11},{4,12},{5,13},{6,14},{7,15},{8,16},{9,17... | collective-permute-start | bytes 1572872 | tf_op jit(solution)/shard_map/ppermute | solution.py:39
